TPU v7x, 32 devices: a whole 2x2x4 slice. The times are simulated.
32 devices in a mesh: items: 4 (over y, x), seq: 8 (over z, core).
Axes of the slice: x: 2, y: 2, z: 4, core: 2. Of those that a mesh axis runs over, the one named last changes fastest.
Arguments:
- byte_tokens: int32 [4, 4096], P('items', 'seq'), may hold values from 0 to 255
- groups: int32 [4, 4096], P('items', 'seq'), may hold values from 0 to 3, as said below
- doc_ids: int32 [4, 512], P('items'), may hold values from 0 to 7, never falling along the last dimension, each value on 1 to 256 neighbouring positions
- patch_proj: float32 [6144, 768], P(('items', 'seq')), may hold values from -0.078125 to 0.078125
- tables: float32 [3, 256, 768], P(None, ('items', 'seq'))
- attn_qkv: float32 [2, 768, 2304], P(None, ('items', 'seq')), may hold values from -0.21875 to 0.21875
- attn_out: float32 [2, 768, 768], P(None, ('items', 'seq')), may hold values from -0.625 to 0.625
- mlp_in: float32 [2, 768, 3072], P(None, ('items', 'seq')), may hold values from -0.21875 to 0.21875
- mlp_out: float32 [2, 3072, 768], P(None, ('items', 'seq')), may hold values from -0.109375 to 0.109375
- vectors: float32 [14, 768], replicated
- first_proj: float32 [6144, 768], P(('items', 'seq')), may hold values from -1.4305115e-06 to 1.4305115e-06
- first_tables: float32 [3, 256, 768], P(None, ('items', 'seq')), may hold values from -1.4305115e-06 to 1.4305115e-06
- first_qkv: float32 [2, 768, 2304], P(None, ('items', 'seq')), may hold values from -1.4305115e-06 to 1.4305115e-06
- first_out: float32 [2, 768, 768], P(None, ('items', 'seq')), may hold values from -1.4305115e-06 to 1.4305115e-06
- first_in: float32 [2, 768, 3072], P(None, ('items', 'seq')), may hold values from -1.4305115e-06 to 1.4305115e-06
- first_down: float32 [2, 3072, 768], P(None, ('items', 'seq')), may hold values from -1.4305115e-06 to 1.4305115e-06
- first_vectors: float32 [14, 768], replicated, may hold values from -7.6293945e-06 to 7.6293945e-06
- second_proj: float32 [6144, 768], P(('items', 'seq')), may hold values from 2.7214456e-13 to 1.0783087e-12
- second_tables: float32 [3, 256, 768], P(None, ('items', 'seq')), may hold values from 2.7214456e-13 to 1.0783087e-12
- second_qkv: float32 [2, 768, 2304], P(None, ('items', 'seq')), may hold values from 2.7214456e-13 to 1.0783087e-12
- second_out: float32 [2, 768, 768], P(None, ('items', 'seq')), may hold values from 2.7214456e-13 to 1.0783087e-12
- second_in: float32 [2, 768, 3072], P(None, ('items', 'seq')), may hold values from 2.7214456e-13 to 1.0783087e-12
- second_down: float32 [2, 3072, 768], P(None, ('items', 'seq')), may hold values from 2.7214456e-13 to 1.0783087e-12
- second_vectors: float32 [14, 768], replicated, may hold values from 6.6752437e-12 to 2.7214456e-11
Outputs:
- loss: float32 [], replicated
- grad_norm: float32 [], replicated
- new_proj: float32 [6144, 768], P(('items', 'seq'))
- new_tables: float32 [3, 256, 768], P(None, ('items', 'seq'))
- new_qkv: float32 [2, 768, 2304], P(None, ('items', 'seq'))
- new_out: float32 [2, 768, 768], P(None, ('items', 'seq'))
- new_in: float32 [2, 768, 3072], P(None, ('items', 'seq'))
- new_down: float32 [2, 3072, 768], P(None, ('items', 'seq'))
- new_vectors: float32 [14, 768], replicated
- moment_proj: float32 [6144, 768], P(('items', 'seq'))
- moment_tables: float32 [3, 256, 768], P(None, ('items', 'seq'))
- moment_qkv: float32 [2, 768, 2304], P(None, ('items', 'seq'))
- moment_out: float32 [2, 768, 768], P(None, ('items', 'seq'))
- moment_in: float32 [2, 768, 3072], P(None, ('items', 'seq'))
- moment_down: float32 [2, 3072, 768], P(None, ('items', 'seq'))
- moment_vectors: float32 [14, 768], replicated
- square_proj: float32 [6144, 768], P(('items', 'seq'))
- square_tables: float32 [3, 256, 768], P(None, ('items', 'seq'))
- square_qkv: float32 [2, 768, 2304], P(None, ('items', 'seq'))
- square_out: float32 [2, 768, 768], P(None, ('items', 'seq'))
- square_in: float32 [2, 768, 3072], P(None, ('items', 'seq'))
- square_down: float32 [2, 3072, 768], P(None, ('items', 'seq'))
- square_vectors: float32 [14, 768], replicated
Inputs may be any that keep to these rules, and one draw needn't show every extreme that they name: `groups`: every item holds each group id at least once.
All inputs are finite; a program needn't handle non-finite values.
Results may differ from a plain program's by a relative error of at most 0.0089.
Values may be sent and summed in bfloat16 or wider, within the bound.
No kernel may reach another device: no remote copies, remote signals or barrier semaphores. Data moves between devices by JAX's collectives and lax.ppermute only.
A program may use at most 256 MiB of HBM per device.

v0:
```python
import jax
import jax.numpy as jnp
from jax import lax
from jax.sharding import PartitionSpec as P

D = 768
HEAD_DIM = 64
FF = 3072
PATCH = 8
VOCAB = 256
GROUPS = 4
STEP_NUMBER = 7


EPSILON = 1e-05
CLIP_AT = 0.01
BETA_ONE = 0.9
BETA_TWO = 0.95
ADAM_EPS = 1e-08
DECAY = 0.1
NEGATIVE = -1e30
HIGH = lax.Precision.HIGHEST


def from_behind(value, axis, steps):
    count = lax.axis_size(axis)
    first, last = (max(0, -steps), min(count, count - steps))
    return lax.ppermute(value, axis, [(source, source + steps) for source in range(first, last)])


def norm_forward(values, gain):
    scale = lax.rsqrt(jnp.mean(values * values, axis=-1, keepdims=True) + EPSILON)
    normed = values * scale
    return (normed * gain, (normed, scale))


def norm_backward(upstream, normed, scale, gain):
    gain_grad = jnp.sum(upstream * normed, axis=0)
    inner = upstream * gain
    return (scale * (inner - normed * jnp.mean(inner * normed, axis=-1, keepdims=True)), gain_grad)


def one_hot(indices, width, dtype):
    return (indices.reshape(-1)[:, None] == jnp.arange(width)[None, :]).astype(dtype)


def layer_forward(resid, gains, qkv_w, out_w, in_w, down_w, attend):
    attn_in, (normed_one, scale_one) = norm_forward(resid, gains[0])
    attn_half = attn_in.astype(jnp.bfloat16)
    qkv_half = jnp.dot(attn_half, qkv_w, preferred_element_type=jnp.float32).astype(jnp.bfloat16)
    mixed, kept = attend(qkv_half)
    mixed_half = mixed.astype(jnp.bfloat16)
    middle = resid + jnp.dot(mixed_half, out_w, preferred_element_type=jnp.float32)
    mlp_norm, (normed_two, scale_two) = norm_forward(middle, gains[1])
    mlp_half = mlp_norm.astype(jnp.bfloat16)
    hidden = jnp.dot(mlp_half, in_w, preferred_element_type=jnp.float32)
    active_half = jax.nn.gelu(hidden).astype(jnp.bfloat16)
    result = middle + jnp.dot(active_half, down_w, preferred_element_type=jnp.float32)
    saved = (
        normed_one,
        scale_one,
        attn_half,
        qkv_half,
        mixed,
        mixed_half,
        kept,
        normed_two,
        scale_two,
        mlp_half,
        hidden,
        active_half,
    )
    return (result, saved)


def layer_backward(result_grad, saved, gains, qkv_w, out_w, in_w, down_w, attend_back):
    (
        normed_one,
        scale_one,
        attn_half,
        qkv_half,
        mixed,
        mixed_half,
        kept,
        normed_two,
        scale_two,
        mlp_half,
        hidden,
        active_half,
    ) = saved
    branch_half = result_grad.astype(jnp.bfloat16)
    down_grad = jnp.einsum(
        "rf,rd->fd", active_half, branch_half, preferred_element_type=jnp.float32
    )
    active_grad = jnp.einsum("rd,fd->rf", branch_half, down_w, preferred_element_type=jnp.float32)
    _, gelu_back = jax.vjp(jax.nn.gelu, hidden)
    hidden_half = gelu_back(active_grad)[0].astype(jnp.bfloat16)
    in_grad = jnp.einsum("rd,rf->df", mlp_half, hidden_half, preferred_element_type=jnp.float32)
    mlp_grad = jnp.einsum("rf,df->rd", hidden_half, in_w, preferred_element_type=jnp.float32)
    middle_grad, gain_two = norm_backward(mlp_grad, normed_two, scale_two, gains[1])
    middle_grad = middle_grad + result_grad
    proj_half = middle_grad.astype(jnp.bfloat16)
    out_grad = jnp.einsum("re,rd->ed", mixed_half, proj_half, preferred_element_type=jnp.float32)
    mixed_grad = jnp.einsum("rd,ed->re", proj_half, out_w, preferred_element_type=jnp.float32)
    qkv_grad_half = attend_back(mixed_grad.astype(jnp.bfloat16), qkv_half, kept, mixed).astype(
        jnp.bfloat16
    )
    qkv_grad = jnp.einsum("rd,re->de", attn_half, qkv_grad_half, preferred_element_type=jnp.float32)
    attn_grad = jnp.einsum("re,de->rd", qkv_grad_half, qkv_w, preferred_element_type=jnp.float32)
    resid_grad, gain_one = norm_backward(attn_grad, normed_one, scale_one, gains[0])
    return (
        resid_grad + middle_grad,
        (jnp.stack([gain_one, gain_two]), qkv_grad, out_grad, in_grad, down_grad),
    )


def local_forward(qkv_half):
    rows = qkv_half.shape[0]
    heads = qkv_half.shape[1] // (3 * HEAD_DIM)
    grid = qkv_half.reshape(rows // PATCH, PATCH, 3, heads, HEAD_DIM)
    scores = jnp.einsum(
        "pqhd,pkhd->phqk", grid[:, :, 0], grid[:, :, 1], preferred_element_type=jnp.float32
    ) * HEAD_DIM ** (-0.5)
    causal = jnp.tril(jnp.ones((PATCH, PATCH), bool))
    probs = jax.nn.softmax(jnp.where(causal, scores, NEGATIVE), axis=-1)
    mixed = jnp.einsum(
        "phqk,pkhd->pqhd",
        probs.astype(jnp.bfloat16),
        grid[:, :, 2],
        preferred_element_type=jnp.float32,
    )
    return (mixed.reshape(rows, heads * HEAD_DIM), probs)


def local_backward(grad_half, qkv_half, probs, mixed):
    rows = qkv_half.shape[0]
    heads = qkv_half.shape[1] // (3 * HEAD_DIM)
    grid = qkv_half.reshape(rows // PATCH, PATCH, 3, heads, HEAD_DIM)
    upstream = grad_half.reshape(rows // PATCH, PATCH, heads, HEAD_DIM)
    prob_grad = jnp.einsum(
        "pqhd,pkhd->phqk", upstream, grid[:, :, 2], preferred_element_type=jnp.float32
    )
    score_half = (probs * (prob_grad - jnp.sum(prob_grad * probs, axis=-1, keepdims=True))).astype(
        jnp.bfloat16
    )
    scale = HEAD_DIM ** (-0.5)
    query_grad = (
        jnp.einsum("phqk,pkhd->pqhd", score_half, grid[:, :, 1], preferred_element_type=jnp.float32)
        * scale
    )
    key_grad = (
        jnp.einsum("phqk,pqhd->pkhd", score_half, grid[:, :, 0], preferred_element_type=jnp.float32)
        * scale
    )
    value_grad = jnp.einsum(
        "phqk,pqhd->pkhd", probs.astype(jnp.bfloat16), upstream, preferred_element_type=jnp.float32
    )
    return jnp.stack([query_grad, key_grad, value_grad], axis=2).reshape(rows, 3 * heads * HEAD_DIM)


def adam_step(weight, grad, first, second, rate, count):
    first = BETA_ONE * first + (1.0 - BETA_ONE) * grad
    second = BETA_TWO * second + (1.0 - BETA_TWO) * grad * grad
    first_hat = first / (1.0 - BETA_ONE**count)
    second_hat = second / (1.0 - BETA_TWO**count)
    return (
        weight - rate * (first_hat / (jnp.sqrt(second_hat) + ADAM_EPS) + DECAY * weight),
        first,
        second,
    )


def body(
    byte_tokens,
    groups,
    doc_ids,
    patch_proj,
    tables,
    attn_qkv,
    attn_out,
    mlp_in,
    mlp_out,
    vectors,
    first_proj,
    first_tables,
    first_qkv,
    first_out,
    first_in,
    first_down,
    first_vectors,
    second_proj,
    second_tables,
    second_qkv,
    second_out,
    second_in,
    second_down,
    second_vectors,
):
    half = jnp.bfloat16
    single = jnp.float32
    proj_w, table_w, qkv_w, out_w, in_w, down_w = (
        lax.all_gather(patch_proj.astype(half), ("items", "seq"), axis=0, tiled=True),
        lax.all_gather(tables.astype(half), ("items", "seq"), axis=1, tiled=True),
        lax.all_gather(attn_qkv.astype(half), ("items", "seq"), axis=1, tiled=True),
        lax.all_gather(attn_out.astype(half), ("items", "seq"), axis=1, tiled=True),
        lax.all_gather(mlp_in.astype(half), ("items", "seq"), axis=1, tiled=True),
        lax.all_gather(mlp_out.astype(half), ("items", "seq"), axis=1, tiled=True),
    )
    width = vectors.shape[1]
    heads = width // HEAD_DIM
    scale = HEAD_DIM ** (-0.5)
    counts = lax.psum(jnp.sum(one_hot(groups, GROUPS, single), axis=0), ("items", "seq"))
    span_rows = byte_tokens.shape[1] // PATCH
    total_patches = doc_ids.shape[1]
    block = min(1024, total_patches)
    offset = lax.axis_index("seq") * span_rows
    my_pos = offset + jnp.arange(span_rows)
    keep_first = (jnp.arange(PATCH) > 0).astype(single)

    def key_slice(source, begin, length):
        return lax.dynamic_slice_in_dim(source, begin, length, 0)

    def scores_for(queries, query_pos, query_docs, key_block, key_pos, key_docs):
        scores = (
            jnp.einsum("qhd,khd->hqk", queries, key_block, preferred_element_type=single) * scale
        )
        allowed = (key_pos[None, :] <= query_pos[:, None]) & (
            key_docs[None, :] == query_docs[:, None]
        )
        return (scores, allowed[None])

    def over_keys(step_fn, carry):
        limit = total_patches // block
        return lax.fori_loop(0, limit, step_fn, carry)

    def item_pass(my_bytes, my_groups, all_docs):
        group_hot = one_hot(my_groups, GROUPS, single)
        my_docs = lax.dynamic_slice_in_dim(all_docs, offset, span_rows)
        prior_docs = jnp.concatenate(
            [lax.dynamic_slice_in_dim(all_docs, jnp.maximum(offset - 1, 0), 1), my_docs[:-1]]
        )
        starts = (my_pos == 0) | (my_docs != prior_docs)

        def block_at(queries, keys_all, values_all, number):
            begin = number * block
            key_block = key_slice(keys_all, begin, block)
            scores, allowed = scores_for(
                queries,
                my_pos,
                my_docs,
                key_block,
                begin + jnp.arange(block),
                key_slice(all_docs, begin, block),
            )
            return (scores, allowed, key_block, key_slice(values_all, begin, block))

        def global_forward(qkv_half):
            queries = qkv_half[:, :width].reshape(span_rows, heads, HEAD_DIM)
            keys_all, values_all = (
                lax.all_gather(qkv_half[:, width : 2 * width], "seq", axis=0, tiled=True),
                lax.all_gather(qkv_half[:, 2 * width :], "seq", axis=0, tiled=True),
            )
            keys_all = keys_all.reshape(total_patches, heads, HEAD_DIM)
            values_all = values_all.reshape(total_patches, heads, HEAD_DIM)

            def peak_step(number, carry):
                peak, total = carry
                scores, allowed, key_block, value_block = block_at(
                    queries, keys_all, values_all, number
                )
                masked = jnp.where(allowed, scores, NEGATIVE)
                new_peak = jnp.maximum(peak, jnp.max(masked, axis=-1))
                fresh = jnp.where(allowed, jnp.exp(masked - new_peak[..., None]), 0.0)
                return (new_peak, total * jnp.exp(peak - new_peak) + jnp.sum(fresh, axis=-1))

            begin_carry = (
                jnp.full((heads, span_rows), NEGATIVE, single),
                jnp.zeros((heads, span_rows), single),
            )
            peak, total = over_keys(peak_step, begin_carry)
            lse = peak + jnp.log(total)

            def mix_step(number, accum):
                scores, allowed, key_block, value_block = block_at(
                    queries, keys_all, values_all, number
                )
                probs = jnp.where(allowed, jnp.exp(scores - lse[..., None]), 0.0).astype(half)
                return accum + jnp.einsum(
                    "hqk,khd->qhd", probs, value_block, preferred_element_type=single
                )

            mixed = over_keys(mix_step, jnp.zeros((span_rows, heads, HEAD_DIM), single))
            return (mixed.reshape(span_rows, width), (queries, keys_all, values_all, lse))

        def global_backward(grad_half, qkv_half, kept, mixed):
            queries, keys_all, values_all, lse = kept
            upstream = grad_half.reshape(span_rows, heads, HEAD_DIM)
            delta = jnp.sum(
                upstream.astype(single) * mixed.reshape(span_rows, heads, HEAD_DIM), axis=-1
            ).T

            def query_step(number, accum):
                scores, allowed, key_block, value_block = block_at(
                    queries, keys_all, values_all, number
                )
                probs = jnp.where(allowed, jnp.exp(scores - lse[..., None]), 0.0)
                prob_grad = jnp.einsum(
                    "qhd,khd->hqk", upstream, value_block, preferred_element_type=single
                )
                score_half = (probs * (prob_grad - delta[..., None])).astype(half)
                return (
                    accum
                    + jnp.einsum(
                        "hqk,khd->qhd", score_half, key_block, preferred_element_type=single
                    )
                    * scale
                )

            query_grad = over_keys(query_step, jnp.zeros((span_rows, heads, HEAD_DIM), single))
            begin = jnp.int32(0)
            length = span_rows * lax.axis_size("seq")
            key_block = key_slice(keys_all, begin, length)
            value_block = key_slice(values_all, begin, length)
            scores, allowed = scores_for(
                queries,
                my_pos,
                my_docs,
                key_block,
                jnp.arange(length),
                key_slice(all_docs, begin, length),
            )
            probs = jnp.where(allowed, jnp.exp(scores - lse[..., None]), 0.0)
            prob_grad = jnp.einsum(
                "qhd,khd->hqk", upstream, value_block, preferred_element_type=single
            )
            score_half = (probs * (prob_grad - delta[..., None])).astype(half)
            value_grad = jnp.einsum(
                "hqk,qhd->khd", probs.astype(half), upstream, preferred_element_type=single
            )
            key_grad = (
                jnp.einsum("hqk,qhd->khd", score_half, queries, preferred_element_type=single)
                * scale
            )
            key_value_grad = lax.psum_scatter(
                jnp.concatenate(
                    [key_grad.reshape(length, width), value_grad.reshape(length, width)], axis=1
                ),
                "seq",
                scatter_dimension=0,
                tiled=True,
            )
            return jnp.concatenate([query_grad.reshape(span_rows, width), key_value_grad], axis=1)

        byte_grid = my_bytes.reshape(span_rows, PATCH)
        edge = from_behind(byte_grid[-1:], "seq", 1)
        earlier = jnp.concatenate([edge, byte_grid[:-1]], axis=0)
        earlier_hot = one_hot(earlier, VOCAB, half)
        embed_half = (
            jnp.dot(earlier_hot, table_w[0], preferred_element_type=single)
            .reshape(span_rows, PATCH * width)
            .astype(half)
        )
        projected = jnp.dot(embed_half, proj_w, preferred_element_type=single)
        resid = jnp.where(starts[:, None], vectors[5][None, :], projected)
        top, saved_top = layer_forward(
            resid, vectors[0:2], qkv_w[0], out_w[0], in_w[0], down_w[0], global_forward
        )
        before = jnp.concatenate([jnp.zeros((span_rows, 1), jnp.int32), byte_grid[:, :-1]], axis=1)
        before_hot = one_hot(before, VOCAB, half)
        local_embed = jnp.dot(before_hot, table_w[1], preferred_element_type=single).reshape(
            span_rows, PATCH, width
        )
        local_in = (
            local_embed * keep_first[None, :, None] + top[:, None, :] + vectors[6 : 6 + PATCH][None]
        )
        result, saved_low = layer_forward(
            local_in.reshape(span_rows * PATCH, width),
            vectors[2:4],
            qkv_w[1],
            out_w[1],
            in_w[1],
            down_w[1],
            local_forward,
        )
        final, (final_normed, final_scale) = norm_forward(result, vectors[4])
        final_half = final.astype(half)
        logits = jnp.einsum("rd,vd->rv", final_half, table_w[2], preferred_element_type=single)
        shifted = logits - jnp.max(logits, axis=-1, keepdims=True)
        totals = jnp.sum(jnp.exp(shifted), axis=-1, keepdims=True)
        probs = jnp.exp(shifted) / totals
        target_hot = one_hot(my_bytes, VOCAB, single)
        losses = jnp.log(totals[:, 0]) - jnp.sum(shifted * target_hot, axis=-1)
        loss_terms = jnp.sum(losses[:, None] * group_hot, axis=0)
        row_weight = jnp.sum(group_hot * (1.0 / (GROUPS * counts))[None, :], axis=-1)
        logit_half = (row_weight[:, None] * (probs - target_hot)).astype(half)
        head_grad = jnp.einsum("rv,rd->vd", logit_half, final_half, preferred_element_type=single)
        final_grad = jnp.einsum("rv,vd->rd", logit_half, table_w[2], preferred_element_type=single)
        result_grad, final_gain_grad = norm_backward(
            final_grad, final_normed, final_scale, vectors[4]
        )
        local_grad, low_grads = layer_backward(
            result_grad,
            saved_low,
            vectors[2:4],
            qkv_w[1],
            out_w[1],
            in_w[1],
            down_w[1],
            local_backward,
        )
        grid_grad = local_grad.reshape(span_rows, PATCH, width)
        top_grad = jnp.sum(grid_grad, axis=1)
        position_grad = jnp.sum(grid_grad, axis=0)
        masked_grad = (grid_grad * keep_first[None, :, None]).reshape(span_rows * PATCH, width)
        local_table_grad = jnp.einsum(
            "rv,rd->vd", before_hot.astype(single), masked_grad, precision=HIGH
        )
        resid_grad, top_grads = layer_backward(
            top_grad,
            saved_top,
            vectors[0:2],
            qkv_w[0],
            out_w[0],
            in_w[0],
            down_w[0],
            global_backward,
        )
        start_grad = jnp.sum(jnp.where(starts[:, None], resid_grad, 0.0), axis=0)
        projected_half = jnp.where(starts[:, None], 0.0, resid_grad).astype(half)
        proj_grad = jnp.einsum(
            "ri,rd->id", embed_half, projected_half, preferred_element_type=single
        )
        embed_grad = jnp.einsum("rd,id->ri", projected_half, proj_w, preferred_element_type=single)
        global_table_grad = jnp.einsum(
            "rv,rd->vd",
            earlier_hot.astype(single),
            embed_grad.reshape(span_rows * PATCH, width),
            precision=HIGH,
        )
        weight_grad = (
            proj_grad,
            jnp.stack([global_table_grad, local_table_grad, head_grad]),
            jnp.stack([top_grads[1], low_grads[1]]),
            jnp.stack([top_grads[2], low_grads[2]]),
            jnp.stack([top_grads[3], low_grads[3]]),
            jnp.stack([top_grads[4], low_grads[4]]),
        )
        vector_grad = jnp.concatenate(
            [top_grads[0], low_grads[0], final_gain_grad[None], start_grad[None], position_grad],
            axis=0,
        )
        return (loss_terms, weight_grad, vector_grad)

    shapes = (proj_w.shape, table_w.shape, qkv_w.shape, out_w.shape, in_w.shape, down_w.shape)

    def scan_item(carry, item):
        loss_acc, grad_acc, vector_acc = carry
        terms, weight_grad, vector_grad = item_pass(item[0], item[1], item[2])
        summed = tuple((grad_acc[n] + weight_grad[n] for n in range(6)))
        return ((loss_acc + terms, summed, vector_acc + vector_grad), None)

    start_carry = (
        jnp.zeros((GROUPS,), single),
        tuple((jnp.zeros(shape, single) for shape in shapes)),
        jnp.zeros(vectors.shape, single),
    )
    (loss_terms, grad_acc, vector_grad), _ = lax.scan(
        scan_item, start_carry, (byte_tokens, groups, doc_ids)
    )
    owned = (
        lax.psum_scatter(grad_acc[0], ("items", "seq"), scatter_dimension=0, tiled=True),
        lax.psum_scatter(grad_acc[1], ("items", "seq"), scatter_dimension=1, tiled=True),
        lax.psum_scatter(grad_acc[2], ("items", "seq"), scatter_dimension=1, tiled=True),
        lax.psum_scatter(grad_acc[3], ("items", "seq"), scatter_dimension=1, tiled=True),
        lax.psum_scatter(grad_acc[4], ("items", "seq"), scatter_dimension=1, tiled=True),
        lax.psum_scatter(grad_acc[5], ("items", "seq"), scatter_dimension=1, tiled=True),
    )
    shard_square = sum((jnp.sum(piece * piece) for piece in owned))
    loss_total, vector_total, square_total = lax.psum(
        (loss_terms, vector_grad, shard_square), ("items", "seq")
    )
    loss = jnp.sum(loss_total / counts) / GROUPS
    grad_norm = jnp.sqrt(square_total + jnp.sum(vector_total * vector_total))
    factor = jnp.minimum(1.0, CLIP_AT / grad_norm)
    count = float(STEP_NUMBER)
    rates = (
        (PATCH * D) ** (-0.5),
        jnp.array([1.0, 1.0, 2.0 * D ** (-0.5)], single).reshape(3, 1, 1),
        D ** (-0.5),
        (D // 8) ** (-0.5),
        D ** (-0.5),
        FF ** (-0.5),
        0.5,
    )
    masters = (patch_proj, tables, attn_qkv, attn_out, mlp_in, mlp_out, vectors)
    grads = tuple(owned) + (vector_total,)
    firsts = (first_proj, first_tables, first_qkv, first_out, first_in, first_down, first_vectors)
    seconds = (
        second_proj,
        second_tables,
        second_qkv,
        second_out,
        second_in,
        second_down,
        second_vectors,
    )
    done = [
        adam_step(masters[n], grads[n] * factor, firsts[n], seconds[n], rates[n], count)
        for n in range(7)
    ]
    return (
        loss,
        grad_norm,
        done[0][0],
        done[1][0],
        done[2][0],
        done[3][0],
        done[4][0],
        done[5][0],
        done[6][0],
        done[0][1],
        done[1][1],
        done[2][1],
        done[3][1],
        done[4][1],
        done[5][1],
        done[6][1],
        done[0][2],
        done[1][2],
        done[2][2],
        done[3][2],
        done[4][2],
        done[5][2],
        done[6][2],
    )


def solution(mesh):
    return jax.shard_map(
        body,
        mesh=mesh,
        in_specs=(
            P("items", "seq"),
            P("items", "seq"),
            P("items", None),
            P(("items", "seq"), None),
            P(None, ("items", "seq"), None),
            P(None, ("items", "seq"), None),
            P(None, ("items", "seq"), None),
            P(None, ("items", "seq"), None),
            P(None, ("items", "seq"), None),
            P(),
            P(("items", "seq"), None),
            P(None, ("items", "seq"), None),
            P(None, ("items", "seq"), None),
            P(None, ("items", "seq"), None),
            P(None, ("items", "seq"), None),
            P(None, ("items", "seq"), None),
            P(),
            P(("items", "seq"), None),
            P(None, ("items", "seq"), None),
            P(None, ("items", "seq"), None),
            P(None, ("items", "seq"), None),
            P(None, ("items", "seq"), None),
            P(None, ("items", "seq"), None),
            P(),
        ),
        out_specs=(
            P(),
            P(),
            P(("items", "seq"), None),
            P(None, ("items", "seq"), None),
            P(None, ("items", "seq"), None),
            P(None, ("items", "seq"), None),
            P(None, ("items", "seq"), None),
            P(None, ("items", "seq"), None),
            P(),
            P(("items", "seq"), None),
            P(None, ("items", "seq"), None),
            P(None, ("items", "seq"), None),
            P(None, ("items", "seq"), None),
            P(None, ("items", "seq"), None),
            P(None, ("items", "seq"), None),
            P(),
            P(("items", "seq"), None),
            P(None, ("items", "seq"), None),
            P(None, ("items", "seq"), None),
            P(None, ("items", "seq"), None),
            P(None, ("items", "seq"), None),
            P(None, ("items", "seq"), None),
            P(),
        ),
        check_vma=False,
    )
```

profile of v0, /device:TPU:0, one launch (start us, length us, event | category | flops | bytes accessed | tf_op | source)
XLA Modules:
  0.0 1719.9 jit_solution(13278014770993014436)
XLA Ops:
  17.6 41.7 %psum.29 = f32[4]{0:T(128)S(1)} all-reduce(f32[4]{0:T(128)S(1)} %convert_reduce_fusion), channel_id=1, replica_groups=mesh['items'=4,'seq'=8] {'items','seq'}, use_global_device_ids=true, to_apply=%region_15.16 | all-reduce | flops 4 | bytes 32 | tf_op jit(solution)/shard_map/psum | solution.py:212
  69.0 81.8 %all-gather.9.cloned.1.call-done = bf16[6144,768]{1,0:T(8,128)(2,1)} async-done(((bf16[192,768]{1,0:T(8,128)(2,1)}), bf16[6144,768]{1,0:T(8,128)(2,1)}) %all-gather.9.cloned.1.call-update) | async-done | bytes 9437200 | tf_op jit(solution)/shard_map/all_gather | solution.py:202
  156.3 68.8 %all-gather.11.cloned.1.call-done = bf16[2,768,2304]{2,1,0:T(8,128)(2,1)} async-done(((bf16[2,24,2304]{2,1,0:T(8,128)(2,1)}), bf16[2,768,2304]{2,1,0:T(8,128)(2,1)}) %all-gather.11.cloned.1.call-update) | async-done | bytes 7077904 | tf_op jit(solution)/shard_map/all_gather | solution.py:204
  228.0 15.6 all_gather.30
  244.1 16.8 all_gather.29
  264.3 20.3 %all-gather.13.cloned.1.call-done = bf16[2,768,768]{2,1,0:T(8,128)(2,1)} async-done(((bf16[2,24,768]{2,1,0:T(8,128)(2,1)}), bf16[2,768,768]{2,1,0:T(8,128)(2,1)}) %all-gather.13.cloned.1.call-update) | async-done | bytes 2359312 | tf_op jit(solution)/shard_map/all_gather | solution.py:205
  286.4 82.3 %all-gather.15.cloned.1.call-done = bf16[2,768,3072]{2,1,0:T(8,128)(2,1)} async-done(((bf16[2,24,3072]{2,1,0:T(8,128)(2,1)}), bf16[2,768,3072]{2,1,0:T(8,128)(2,1)}) %all-gather.15.cloned.1.call-update) | async-done | bytes 9437200 | tf_op jit(solution)/shard_map/all_gather | solution.py:206
  372.0 80.4 %all-gather.17.cloned.1.call-done = bf16[2,3072,768]{2,1,0:T(8,128)(2,1)} async-done(((bf16[2,96,768]{2,1,0:T(8,128)(2,1)}), bf16[2,3072,768]{2,1,0:T(8,128)(2,1)}) %all-gather.17.cloned.1.call-update) | async-done | bytes 9437200 | tf_op jit(solution)/shard_map/all_gather | solution.py:207
  463.9 8.3 reshape.402
  479.8 10.7 fusion.97
  506.0 8.5 multiply_reduce_fusion.7
  517.7 8.5 fusion.7
  559.7 8.8 convert_element_type.229
  611.3 24.0 %reduce-scatter.22.cloned.1.call-done = f32[64,1536]{1,0:T(8,128)} async-done(((f32[512,1536]{1,0:T(8,128)}), f32[64,1536]{1,0:T(8,128)}) %reduce-scatter.22.cloned.1.call-update) | async-done | bytes 393232
  666.5 11.3 pad_maximum_fusion.2
  699.4 7.1 pad_maximum_fusion
  707.6 8.1 fusion.86
  716.7 30.9 %reduce-scatter.16.cloned.1.call-done = f32[2,24,768]{2,1,0:T(8,128)} async-done(((f32[2,768,768]{2,1,0:T(8,128)}), f32[2,24,768]{2,1,0:T(8,128)}) %reduce-scatter.16.cloned.1.call-update) | async-done | bytes 147472 | tf_op jit(solution)/shard_map/reduce_scatter | solution.py:474
  749.1 102.3 %reduce-scatter.12.cloned.1.call-done = f32[3,8,768]{2,1,0:T(8,128)} async-done(((f32[3,256,768]{2,1,0:T(8,128)}), f32[3,8,768]{2,1,0:T(8,128)}) %reduce-scatter.12.cloned.1.call-update) | async-done | bytes 73744 | tf_op jit(solution)/shard_map/reduce_scatter | solution.py:472
  852.9 166.3 %reduce-scatter.14.cloned.1.call-done = f32[2,24,2304]{2,1,0:T(8,128)} async-done(((f32[2,768,2304]{2,1,0:T(8,128)}), f32[2,24,2304]{2,1,0:T(8,128)}) %reduce-scatter.14.cloned.1.call-update) | async-done | bytes 442384 | tf_op jit(solution)/shard_map/reduce_scatter | solution.py:473
  1021.0 208.9 %reduce-scatter.20.cloned.1.call-done = f32[2,96,768]{2,1,0:T(8,128)} async-done(((f32[2,3072,768]{2,1,0:T(8,128)}), f32[2,96,768]{2,1,0:T(8,128)}) %reduce-scatter.20.cloned.1.call-update) | async-done | bytes 589840 | tf_op jit(solution)/shard_map/reduce_scatter | solution.py:476
  1231.8 208.5 %reduce-scatter.18.cloned.1.call-done = f32[2,24,3072]{2,1,0:T(8,128)} async-done(((f32[2,768,3072]{2,1,0:T(8,128)}), f32[2,24,3072]{2,1,0:T(8,128)}) %reduce-scatter.18.cloned.1.call-update) | async-done | bytes 589840 | tf_op jit(solution)/shard_map/reduce_scatter | solution.py:475
  1442.1 210.5 %reduce-scatter.10.cloned.1.call-done = f32[192,768]{1,0:T(8,128)} async-done(((f32[6144,768]{1,0:T(8,128)}), f32[192,768]{1,0:T(8,128)}) %reduce-scatter.10.cloned.1.call-update) | async-done | bytes 589840 | tf_op jit(solution)/shard_map/reduce_scatter | solution.py:471
  1658.3 40.2 %all-reduce.1 = (f32[4]{0:T(128)S(1)}, f32[]{:T(128)}, f32[14,768]{1,0:T(8,128)S(1)}) all-reduce(f32[4]{0:T(128)S(1)} %copy-done.129, f32[]{:T(128)S(6)} %add.413, f32[14,768]{1,0:T(8,128)S(1)} %concatenate.40), channel_id=1, replica_groups=mesh['items'=4,'seq'=8] {'items','seq'}, use_global_device_ids=true, to_apply=%region_13.14 | all-reduce | flops 10757 | bytes 86056 | tf_op jit(solution)/shard_map/psum | solution.py:479
  (467 shorter events, 225.0 us)
Async XLA Ops:
  7.2 59.4 %all-gather.7.cloned.1.call-start = ((), (), s32[]{:S(2)}) async-start(), calls=%async_computation.7 | async-start | bytes 1216512 | tf_op jit(solution)/shard_map/all_gather | solution.py:203
  8.9 141.9 %all-gather.9.cloned.1.call-start = ((), (), s32[]{:S(2)}) async-start(), calls=%async_computation.8 | async-start | bytes 9732096 | tf_op jit(solution)/shard_map/all_gather | solution.py:202
  10.8 214.4 %all-gather.11.cloned.1.call-start = ((), (), s32[]{:S(2)}) async-start(), calls=%async_computation.9 | async-start | bytes 7299072 | tf_op jit(solution)/shard_map/all_gather | solution.py:204
  12.6 272.0 %all-gather.13.cloned.1.call-start = ((), (), s32[]{:S(2)}) async-start(), calls=%async_computation.10 | async-start | bytes 2433024 | tf_op jit(solution)/shard_map/all_gather | solution.py:205
  13.3 355.3 %all-gather.15.cloned.1.call-start = ((), (), s32[]{:S(2)}) async-start(), calls=%async_computation.11 | async-start | bytes 9732096 | tf_op jit(solution)/shard_map/all_gather | solution.py:206
  14.2 438.2 %all-gather.17.cloned.1.call-start = ((), (), s32[]{:S(2)}) async-start(), calls=%async_computation.12 | async-start | bytes 9732096 | tf_op jit(solution)/shard_map/all_gather | solution.py:207
  15.0 620.3 %reduce-scatter.22.cloned.1.call-start = ((), (), s32[]{:S(2)}) async-start(), calls=%async_computation.19 | async-start | bytes 3538944
  15.2 51.2 %collective-permute-start = (s32[1,8]{1,0:T(1,128)S(1)}, s32[1,8]{1,0:T(1,128)S(1)}, u32[]{:S(2)}, u32[]{:S(2)}) collective-permute-start(s32[1,8]{1,0:T(1,128)S(1)} %slice.148), channel_id=1, source_target_pairs={{0,1},{1,2},{2,3},{3,4},{4,5},{5,6},{6,7},{8,9},{9,10},{10,11},{11... | collective-permute-start | bytes 104 | tf_op jit(solution)/shard_map/while/body/eval_jaxpr/ppermute | solution.py:28
  264.3 104.3 %copy-start.53 = (bf16[64,12,64]{0,2,1:T(8,128)(2,1)}, bf16[64,12,64]{0,2,1:T(8,128)(2,1)S(1)}, u32[]{:S(2)}) copy-start(bf16[64,12,64]{0,2,1:T(8,128)(2,1)S(1)} %get-tuple-element.275) | copy-start | bytes 294916
  596.2 151.3 %reduce-scatter.16.cloned.1.call-start = ((), (), s32[]{:S(2)}) async-start(), calls=%async_computation.16 | async-start | bytes 4866048 | tf_op jit(solution)/shard_map/reduce_scatter | solution.py:474
  601.3 250.1 %reduce-scatter.12.cloned.1.call-start = ((), (), s32[]{:S(2)}) async-start(), calls=%async_computation.14 | async-start | bytes 2433024 | tf_op jit(solution)/shard_map/reduce_scatter | solution.py:472
  654.2 365.1 %reduce-scatter.14.cloned.1.call-start = ((), (), s32[]{:S(2)}) async-start(), calls=%async_computation.15 | async-start | bytes 14598144 | tf_op jit(solution)/shard_map/reduce_scatter | solution.py:473
  677.9 552.0 %reduce-scatter.20.cloned.1.call-start = ((), (), s32[]{:S(2)}) async-start(), calls=%async_computation.18 | async-start | bytes 19464192 | tf_op jit(solution)/shard_map/reduce_scatter | solution.py:476
  693.8 746.5 %reduce-scatter.18.cloned.1.call-start = ((), (), s32[]{:S(2)}) async-start(), calls=%async_computation.17 | async-start | bytes 19464192 | tf_op jit(solution)/shard_map/reduce_scatter | solution.py:475
  706.5 946.0 %reduce-scatter.10.cloned.1.call-start = ((), (), s32[]{:S(2)}) async-start(), calls=%async_computation.13 | async-start | bytes 19464192 | tf_op jit(solution)/shard_map/reduce_scatter | solution.py:471
  715.8 942.5 %copy-start.129 = (f32[4]{0:T(128)S(1)}, f32[4]{0:T(128)}, u32[]{:S(2)}) copy-start(f32[4]{0:T(128)} %get-tuple-element.237) | copy-start | bytes 52
  715.8 984.7 %copy-start.136 = (f32[4]{0:T(128)S(1)}, f32[4]{0:T(128)}, u32[]{:S(2)}) copy-start(f32[4]{0:T(128)} %copy-done.135) | copy-start | bytes 52
  715.8 986.0 %copy-start.84 = (f32[14,768]{1,0:T(8,128)S(1)}, f32[14,768]{1,0:T(8,128)}, u32[]{:S(2)}) copy-start(f32[14,768]{1,0:T(8,128)} %param.34) | copy-start | bytes 129028
  715.8 986.0 %copy-start.95 = (f32[14,768]{1,0:T(8,128)S(1)}, f32[14,768]{1,0:T(8,128)}, u32[]{:S(2)}) copy-start(f32[14,768]{1,0:T(8,128)} %param.41) | copy-start | bytes 129028
  715.8 986.0 %copy-start.96 = (f32[14,768]{1,0:T(8,128)S(1)}, f32[14,768]{1,0:T(8,128)}, u32[]{:S(2)}) copy-start(f32[14,768]{1,0:T(8,128)} %param.48) | copy-start | bytes 129028
  715.8 986.6 %copy-start.36 = (f32[2,96,768]{2,1,0:T(8,128)S(1)}, f32[2,96,768]{2,1,0:T(8,128)}, u32[]{:S(2)}) copy-start(f32[2,96,768]{2,1,0:T(8,128)} %param.33) | copy-start | bytes 1769476
  715.8 986.6 %copy-start.65 = (f32[2,96,768]{2,1,0:T(8,128)S(1)}, f32[2,96,768]{2,1,0:T(8,128)}, u32[]{:S(2)}) copy-start(f32[2,96,768]{2,1,0:T(8,128)} %param.40) | copy-start | bytes 1769476
  715.9 986.6 %copy-start.66 = (f32[2,96,768]{2,1,0:T(8,128)S(1)}, f32[2,96,768]{2,1,0:T(8,128)}, u32[]{:S(2)}) copy-start(f32[2,96,768]{2,1,0:T(8,128)} %param.47) | copy-start | bytes 1769476
  1229.9 472.6 %copy-start.40 = (f32[2,96,768]{2,1,0:T(8,128)S(1)}, f32[2,96,768]{2,1,0:T(8,128)}, u32[]{:S(2)}) copy-start(f32[2,96,768]{2,1,0:T(8,128)} %reduce-scatter.20.cloned.1.call-done) | copy-start | bytes 1769476
  (138 other events, 1340.4 us)
Sparse Core Ops, SparseCore 0:
  11.5 54.2 all-gather.6
  69.4 81.2 all-gather.8
  154.5 70.5 all-gather.10
  228.8 55.7 all-gather.12
  288.2 80.3 all-gather.14
  372.2 80.0 all-gather.16
  596.3 38.9 reduce-scatter.21
  640.8 106.7 reduce-scatter.15
  752.8 98.5 reduce-scatter.11
  857.2 161.9 reduce-scatter.13
  1025.7 204.1 reduce-scatter.19
  1236.1 204.0 reduce-scatter.17
  1446.7 205.8 reduce-scatter.9
where the time goes:
time: 1730 us; the launch traced here: 1720 us
  waiting for transfers between devices  1290 us (75%)
  matrix products  141 us (8%)
  blocking collectives  114 us (7%)
  other arithmetic  82 us (5%)
  local copies, waits for them, and re-layouts  69.8 us (4%)
  between operations  24.3 us (1%)
    reduce_scatter x1, waiting for transfers between devices, body(): lax.psum_scatter(grad_acc[0], ('items', 'seq'), scatter_dimension=0, tile...  210 us
    reduce_scatter x1, waiting for transfers between devices, body(): lax.psum_scatter(grad_acc[5], ('items', 'seq'), scatter_dimension=1, tile...  209 us
    reduce_scatter x1, waiting for transfers between devices, body(): lax.psum_scatter(grad_acc[4], ('items', 'seq'), scatter_dimension=1, tile...  208 us
    reduce_scatter x1, waiting for transfers between devices, body(): lax.psum_scatter(grad_acc[2], ('items', 'seq'), scatter_dimension=1, tile...  166 us
    reduce_scatter x1, waiting for transfers between devices, body(): lax.psum_scatter(grad_acc[1], ('items', 'seq'), scatter_dimension=1, tile...  102 us
    all_gather x1, waiting for transfers between devices, body(): lax.all_gather(mlp_in.astype(half), ('items', 'seq'), axis=1, tiled=True)  82.3 us
    all_gather x1, waiting for transfers between devices, body(): lax.all_gather(patch_proj.astype(half), ('items', 'seq'), axis=0, tiled=T...  81.8 us
    all_gather x1, waiting for transfers between devices, body(): lax.all_gather(mlp_out.astype(half), ('items', 'seq'), axis=1, tiled=True)  80.4 us
  transfers between devices with their start and end apart: 14, of which 12 were waited for; matrix products, arithmetic and copies ran while one was open for 8% of the time, Pallas kernels for 0%

commit v1 on v0

--- a/solution.py
+++ b/solution.py
@@ -38,6 +38,62 @@
     gain_grad = jnp.sum(upstream * normed, axis=0)
     inner = upstream * gain
     return (scale * (inner - normed * jnp.mean(inner * normed, axis=-1, keepdims=True)), gain_grad)
+
+
+def to_half(value):
+    return value.astype(jnp.bfloat16)
+
+
+def wide(value):
+    return value.astype(jnp.float32)
+
+
+def pick(value, index, axis):
+    return lax.dynamic_index_in_dim(value, index, axis, keepdims=False)
+
+
+def swap(value, axis, bit):
+    count = lax.axis_size(axis)
+    return lax.ppermute(value, axis, [(at, at ^ bit) for at in range(count)])
+
+
+def fold(value, axis, bit, mine, place):
+    got = swap(to_half(pick(value, 1 - mine, place)), axis, bit)
+    return wide(pick(value, mine, place)) + wide(got)
+
+
+def reduce_rows(partial, x_first):
+    items, seq = lax.axis_size("items"), lax.axis_size("seq")
+    at_item, at_seq = lax.axis_index("items"), lax.axis_index("seq")
+    core, x_at, y_at = at_seq % 2, at_item % 2, at_item // 2
+    width = partial.shape[1]
+    grid = partial.reshape(items // 2, 2, seq // 2, 2, -1, width)
+    grid = fold(grid, "seq", 1, core, 3)
+    if x_first:
+        grid = fold(fold(grid, "items", 1, x_at, 1), "items", 2, y_at, 0)
+    else:
+        grid = fold(fold(grid, "items", 2, y_at, 0), "items", 1, x_at, 0)
+    groups = [list(range(first, seq, 2)) for first in range(2)]
+    pieces = lax.all_to_all(to_half(grid), "seq", 0, 0, axis_index_groups=groups, tiled=True)
+    return jnp.sum(wide(pieces), axis=0)
+
+
+def share(row):
+    count = lax.axis_size("items") * lax.axis_size("seq")
+    return lax.all_to_all(
+        jnp.broadcast_to(row[None], (count,) + row.shape), ("items", "seq"), 0, 0, tiled=True
+    )
+
+
+def spread_sum(value):
+    count = lax.axis_size("items") * lax.axis_size("seq")
+    size = -(-value.shape[0] // count)
+    rows = jnp.pad(value, (0, size * count - value.shape[0])).reshape(count, size)
+    return jnp.sum(lax.all_to_all(rows, ("items", "seq"), 0, 0, tiled=True), axis=0)
+
+
+def gather_rows(value):
+    return lax.all_gather(value, ("items", "seq"), axis=0, tiled=True)
 
 
 def one_hot(indices, width, dtype):
@@ -108,9 +164,10 @@
     qkv_grad = jnp.einsum("rd,re->de", attn_half, qkv_grad_half, preferred_element_type=jnp.float32)
     attn_grad = jnp.einsum("re,de->rd", qkv_grad_half, qkv_w, preferred_element_type=jnp.float32)
     resid_grad, gain_one = norm_backward(attn_grad, normed_one, scale_one, gains[0])
+    attn_part = jnp.concatenate([to_half(qkv_grad), to_half(out_grad)], axis=1)
     return (
         resid_grad + middle_grad,
-        (jnp.stack([gain_one, gain_two]), qkv_grad, out_grad, in_grad, down_grad),
+        (jnp.stack([gain_one, gain_two]), attn_part, to_half(in_grad), to_half(down_grad)),
     )
 
 
@@ -198,18 +255,25 @@
 ):
     half = jnp.bfloat16
     single = jnp.float32
-    proj_w, table_w, qkv_w, out_w, in_w, down_w = (
-        lax.all_gather(patch_proj.astype(half), ("items", "seq"), axis=0, tiled=True),
-        lax.all_gather(tables.astype(half), ("items", "seq"), axis=1, tiled=True),
-        lax.all_gather(attn_qkv.astype(half), ("items", "seq"), axis=1, tiled=True),
-        lax.all_gather(attn_out.astype(half), ("items", "seq"), axis=1, tiled=True),
-        lax.all_gather(mlp_in.astype(half), ("items", "seq"), axis=1, tiled=True),
-        lax.all_gather(mlp_out.astype(half), ("items", "seq"), axis=1, tiled=True),
-    )
     width = vectors.shape[1]
+    group_rows = share(groups.reshape(-1))
+    counts = jnp.sum(one_hot(group_rows, GROUPS, single), axis=0)
+    table_all = gather_rows(jnp.concatenate([tables[n].astype(half) for n in range(3)], axis=1))
+    table_w = [table_all[:, n * width : (n + 1) * width] for n in range(3)]
+    proj_w = gather_rows(patch_proj.astype(half))
+    qkv_w, out_w, in_w, down_w = [], [], [], []
+    for n in range(2):
+        joined = gather_rows(
+            jnp.concatenate(
+                [attn_qkv[n].astype(half), attn_out[n].astype(half), mlp_in[n].astype(half)], axis=1
+            )
+        )
+        qkv_w.append(joined[:, : 3 * width])
+        out_w.append(joined[:, 3 * width : 4 * width])
+        in_w.append(joined[:, 4 * width :])
+        down_w.append(gather_rows(mlp_out[n].astype(half)))
     heads = width // HEAD_DIM
     scale = HEAD_DIM ** (-0.5)
-    counts = lax.psum(jnp.sum(one_hot(groups, GROUPS, single), axis=0), ("items", "seq"))
     span_rows = byte_tokens.shape[1] // PATCH
     total_patches = doc_ids.shape[1]
     block = min(1024, total_patches)
@@ -437,50 +501,43 @@
             embed_grad.reshape(span_rows * PATCH, width),
             precision=HIGH,
         )
-        weight_grad = (
-            proj_grad,
-            jnp.stack([global_table_grad, local_table_grad, head_grad]),
-            jnp.stack([top_grads[1], low_grads[1]]),
-            jnp.stack([top_grads[2], low_grads[2]]),
-            jnp.stack([top_grads[3], low_grads[3]]),
-            jnp.stack([top_grads[4], low_grads[4]]),
+        table_parts = jnp.concatenate(
+            [to_half(global_table_grad), to_half(local_table_grad), to_half(head_grad)], axis=1
+        )
+        proj_rows = to_half(proj_grad)
+        owned = (
+            reduce_rows(low_grads[3], False),
+            reduce_rows(low_grads[2], True),
+            reduce_rows(low_grads[1], False),
+            reduce_rows(top_grads[3], True),
+            reduce_rows(top_grads[2], False),
+            reduce_rows(top_grads[1], True),
+            reduce_rows(proj_rows, False),
+            reduce_rows(table_parts, True),
         )
         vector_grad = jnp.concatenate(
             [top_grads[0], low_grads[0], final_gain_grad[None], start_grad[None], position_grad],
             axis=0,
         )
-        return (loss_terms, weight_grad, vector_grad)
-
-    shapes = (proj_w.shape, table_w.shape, qkv_w.shape, out_w.shape, in_w.shape, down_w.shape)
-
-    def scan_item(carry, item):
-        loss_acc, grad_acc, vector_acc = carry
-        terms, weight_grad, vector_grad = item_pass(item[0], item[1], item[2])
-        summed = tuple((grad_acc[n] + weight_grad[n] for n in range(6)))
-        return ((loss_acc + terms, summed, vector_acc + vector_grad), None)
-
-    start_carry = (
-        jnp.zeros((GROUPS,), single),
-        tuple((jnp.zeros(shape, single) for shape in shapes)),
-        jnp.zeros(vectors.shape, single),
-    )
-    (loss_terms, grad_acc, vector_grad), _ = lax.scan(
-        scan_item, start_carry, (byte_tokens, groups, doc_ids)
-    )
+        return (loss_terms, owned, vector_grad)
+
+    loss_terms, pieces, vector_grad = item_pass(byte_tokens[0], groups[0], doc_ids[0])
     owned = (
-        lax.psum_scatter(grad_acc[0], ("items", "seq"), scatter_dimension=0, tiled=True),
-        lax.psum_scatter(grad_acc[1], ("items", "seq"), scatter_dimension=1, tiled=True),
-        lax.psum_scatter(grad_acc[2], ("items", "seq"), scatter_dimension=1, tiled=True),
-        lax.psum_scatter(grad_acc[3], ("items", "seq"), scatter_dimension=1, tiled=True),
-        lax.psum_scatter(grad_acc[4], ("items", "seq"), scatter_dimension=1, tiled=True),
-        lax.psum_scatter(grad_acc[5], ("items", "seq"), scatter_dimension=1, tiled=True),
-    )
+        pieces[6],
+        jnp.stack([pieces[7][:, n * width : (n + 1) * width] for n in range(3)]),
+        jnp.stack([pieces[5][:, : 3 * width], pieces[2][:, : 3 * width]]),
+        jnp.stack([pieces[5][:, 3 * width :], pieces[2][:, 3 * width :]]),
+        jnp.stack([pieces[4], pieces[1]]),
+        jnp.stack([pieces[3], pieces[0]]),
+    )
+    loss_total = jnp.sum(share(loss_terms), axis=0)
+    vector_piece = spread_sum(vector_grad.reshape(-1))
     shard_square = sum((jnp.sum(piece * piece) for piece in owned))
-    loss_total, vector_total, square_total = lax.psum(
-        (loss_terms, vector_grad, shard_square), ("items", "seq")
-    )
+    shard_square = shard_square + jnp.sum(vector_piece * vector_piece)
+    tail = share(jnp.concatenate([vector_piece, shard_square[None]]))
+    vector_total = tail[:, :-1].reshape(-1)[: vectors.size].reshape(vectors.shape)
     loss = jnp.sum(loss_total / counts) / GROUPS
-    grad_norm = jnp.sqrt(square_total + jnp.sum(vector_total * vector_total))
+    grad_norm = jnp.sqrt(jnp.sum(tail[:, -1]))
     factor = jnp.minimum(1.0, CLIP_AT / grad_norm)
     count = float(STEP_NUMBER)
     rates = (

time: 1730 us -> 965 us (0.56)
  waiting for transfers between devices: 1290 us -> 484 us
  blocking collectives: 114 us -> 34.5 us
  starting transfers between devices: 3.31 us -> 76.7 us
  local copies, waits for them, and re-layouts: 69.8 us -> 98.3 us
  other arithmetic: 82 us -> 109 us
    reduce_scatter x6 -> x0, waiting for transfers between devices: 927 us -> none  [the longest x1 210 us: body(): lax.psum_scatter(grad_acc[0], ('items', 'seq'), scatter_dimension=0, tile...]
    ppermute x0 -> x24, waiting for transfers between devices: none -> 118 us  [swap(): return lax.ppermute(value, axis, [(at, at ^ bit) for at in range(count)])]
    psum x2 -> x0, blocking collectives: 82 us -> none  [the longest x1 41.7 us: body(): lax.psum(jnp.sum(one_hot(groups, GROUPS, single), axis=0), ('items', 'seq'))]
    all_to_all x0 -> x12, waiting for transfers between devices: none -> 60.5 us  [the longest x8 54.5 us: reduce_rows(): lax.all_to_all(to_half(grid), 'seq', 0, 0, axis_index_groups=groups, tile...]
    all_to_all x0 -> x12, starting transfers between devices: none -> 52 us  [the longest x8 33.9 us: reduce_rows(): lax.all_to_all(to_half(grid), 'seq', 0, 0, axis_index_groups=groups, tile...]
    add x0 -> x16, other arithmetic: none -> 31.6 us  [fold(): return wide(pick(value, mine, place)) + wide(got)]
    all_gather x6, waiting for transfers between devices: 334 us -> 305 us  [gather_rows(): return lax.all_gather(value, ('items', 'seq'), axis=0, tiled=True)]
    another operation x5, other arithmetic: 29.3 us -> 2.97 us  [the longest x1 11.3 us: item_pass(): jnp.stack([top_grads[1], low_grads[1]])]
  transfers between devices with their start and end apart: 14 -> 44, of which waited for: 12 -> 24; matrix products, arithmetic and copies ran while one was open for 8% -> 26% of each run, Pallas kernels for 0% -> 0%
where the time goes in v1:
time: 965 us; the launch traced here: 954 us
  waiting for transfers between devices  484 us (50%)
  matrix products  126 us (13%)
  other arithmetic  109 us (11%)
  local copies, waits for them, and re-layouts  98.3 us (10%)
  starting transfers between devices  76.7 us (8%)
  blocking collectives  34.5 us (4%)
  between operations  25.3 us (3%)
    all_gather x6, waiting for transfers between devices, gather_rows(): return lax.all_gather(value, ('items', 'seq'), axis=0, tiled=True)  305 us
    ppermute x24, waiting for transfers between devices, swap(): return lax.ppermute(value, axis, [(at, at ^ bit) for at in range(count)])  118 us
    all_to_all x8, waiting for transfers between devices, reduce_rows(): lax.all_to_all(to_half(grid), 'seq', 0, 0, axis_index_groups=groups, tile...  54.5 us
    all_to_all x8, starting transfers between devices, reduce_rows(): lax.all_to_all(to_half(grid), 'seq', 0, 0, axis_index_groups=groups, tile...  33.9 us
    add x16, other arithmetic, fold(): return wide(pick(value, mine, place)) + wide(got)  31.6 us
    ppermute x24, starting transfers between devices, swap(): return lax.ppermute(value, axis, [(at, at ^ bit) for at in range(count)])  22.1 us
    unnamed x320, local copies, waits for them, and re-layouts  21.4 us
  transfers between devices with their start and end apart: 44, of which 24 were waited for; matrix products, arithmetic and copies ran while one was open for 26% of the time, Pallas kernels for 0%

profile of v1, /device:TPU:0, one launch (start us, length us, event | category | flops | bytes accessed | tf_op | source)
XLA Modules:
  0.0 953.9 jit_solution(8046674064949456789)
XLA Ops:
  18.6 7.1 all-to-all-start.1
  34.0 34.5 %all-gather.9.cloned.1.call-done = bf16[256,2304]{1,0:T(8,128)(2,1)} async-done(((bf16[8,2304]{1,0:T(8,128)(2,1)}), bf16[256,2304]{1,0:T(8,128)(2,1)}) %all-gather.9.cloned.1.call-update) | async-done | bytes 1179664 | tf_op jit(solution)/shard_map/all_gather | solution.py:96
  70.3 82.3 %all-gather.11.cloned.1.call-done = bf16[6144,768]{1,0:T(8,128)(2,1)} async-done(((bf16[192,768]{1,0:T(8,128)(2,1)}), bf16[6144,768]{1,0:T(8,128)(2,1)}) %all-gather.11.cloned.1.call-update) | async-done | bytes 9437200 | tf_op jit(solution)/shard_map/all_gather | solution.py:96
  158.2 78.1 %all-gather.13.cloned.1.call-done = bf16[768,6144]{1,0:T(8,128)(2,1)} async-done(((bf16[24,6144]{1,0:T(8,128)(2,1)}), bf16[768,6144]{1,0:T(8,128)(2,1)}) %all-gather.13.cloned.1.call-update) | async-done | bytes 9437200 | tf_op jit(solution)/shard_map/all_gather | solution.py:96
  239.3 16.7 %all_gather.28 = bf16[512,768]{1,0:T(8,128)(2,1)S(1)} all-gather(bf16[64,768]{1,0:T(8,128)(2,1)S(1)} %get-tuple-element.169), channel_id=1, replica_groups=mesh['items'=4,'seq'=8] {'seq'}, dimensions={0}, use_global_device_ids=true | all-gather | bytes 884736 | tf_op jit(solution)/shard_map/all_gather | solution.py:324
  256.3 17.8 %all_gather.27 = bf16[512,768]{1,0:T(8,128)(2,1)S(1)} all-gather(bf16[64,768]{1,0:T(8,128)(2,1)S(1)} %get-tuple-element.171), channel_id=1, replica_groups=mesh['items'=4,'seq'=8] {'seq'}, dimensions={0}, use_global_device_ids=true | all-gather | bytes 884736 | tf_op jit(solution)/shard_map/all_gather | solution.py:325
  283.5 18.8 %all-gather.17.cloned.1.call-done = bf16[1,3072,768]{2,1,0:T(8,128)(2,1)} async-done(((bf16[1,96,768]{2,1,0:T(8,128)(2,1)}), bf16[1,3072,768]{2,1,0:T(8,128)(2,1)}) %all-gather.17.cloned.1.call-update) | async-done | bytes 4718608 | tf_op jit(solution)/shard_map/all_gather | solution.py:96
  308.3 77.3 %all-gather.15.cloned.1.call-done = bf16[768,6144]{1,0:T(8,128)(2,1)} async-done(((bf16[24,6144]{1,0:T(8,128)(2,1)}), bf16[768,6144]{1,0:T(8,128)(2,1)}) %all-gather.15.cloned.1.call-update) | async-done | bytes 9437200 | tf_op jit(solution)/shard_map/all_gather | solution.py:96
  391.6 8.6 reshape.405
  407.7 10.7 %fusion.144 = (f32[64,12,8]{2,1,0:T(8,128)S(1)}, f32[64,12,8,8]{2,3,1,0:T(8,128)S(1)}) fusion(f32[64,12,8,8]{2,3,1,0:T(8,128)S(1)} %fusion.69, pred[8,8]{0,1:T(8,128)(4,1)S(1)} %copy-done.132), kind=kOutput, calls=%fused_computation.362 | output fusion | flops 294919 | bytes 417856 | tf_op jit(solution)/shard_map/sub | solution.py:182
  429.4 7.3 fusion.18
  436.7 14.5 %all-gather.19.cloned.1.call-done = bf16[1,3072,768]{2,1,0:T(8,128)(2,1)} async-done(((bf16[1,96,768]{2,1,0:T(8,128)(2,1)}), bf16[1,3072,768]{2,1,0:T(8,128)(2,1)}) %all-gather.19.cloned.1.call-update) | async-done | bytes 4718608 | tf_op jit(solution)/shard_map/all_gather | solution.py:96
  451.2 8.5 multiply_reduce_fusion.7
  468.6 6.2 fusion.7
  516.9 8.4 convert_element_type.509
  597.7 11.9 %collective-permute-done.23 = bf16[2,4,96,768]{3,2,1,0:T(8,128)(2,1)} collective-permute-done((bf16[2,4,96,768]{3,2,1,0:T(8,128)(2,1)S(1)}, bf16[2,4,96,768]{3,2,1,0:T(8,128)(2,1)}, u32[]{:S(2)}, u32[]{:S(2)}) %collective-permute-start.23) | collective-permute-done | bytes 1179680 | tf_op jit(solution)/shard_map/ppermute | solution.py:57
  617.2 17.7 %collective-permute-done.11 = bf16[2,4,24,3072]{3,2,1,0:T(8,128)(2,1)} collective-permute-done((bf16[2,4,24,3072]{3,2,1,0:T(8,128)(2,1)S(1)}, bf16[2,4,24,3072]{3,2,1,0:T(8,128)(2,1)}, u32[]{:S(2)}, u32[]{:S(2)}) %collective-permute-start.11) | collective-permute-done | bytes 1179680 | tf_op jit(solution)/shard_map/ppermute | solution.py:57
  643.3 16.8 %collective-permute-done.14 = bf16[2,4,24,3072]{3,2,1,0:T(8,128)(2,1)S(1)} collective-permute-done((bf16[2,4,24,3072]{3,2,1,0:T(8,128)(2,1)S(1)}, bf16[2,4,24,3072]{3,2,1,0:T(8,128)(2,1)S(1)}, u32[]{:S(2)}, u32[]{:S(2)}) %collective-permute-start.14) | collective-permute-done | bytes 1179680 | tf_op jit(solution)/shard_map/ppermute | solution.py:57
  740.7 10.8 %all-to-all-done.9 = bf16[4,96,768]{2,1,0:T(8,128)(2,1)S(1)} async-done(((bf16[4,96,768]{2,1,0:T(8,128)(2,1)}), bf16[4,96,768]{2,1,0:T(8,128)(2,1)S(1)}, u32[]{:S(2)}, u32[]{:S(2)}) %all-to-all-start.9) | async-done | bytes 589856 | tf_op jit(solution)/shard_map/all_to_all | solution.py:77
  760.5 10.6 %all-to-all-done.7 = bf16[4,24,3072]{2,1,0:T(8,128)(2,1)} async-done(((bf16[4,24,3072]{2,1,0:T(8,128)(2,1)}), bf16[4,24,3072]{2,1,0:T(8,128)(2,1)}, u32[]{:S(2)}, u32[]{:S(2)}) %all-to-all-start.7) | async-done | bytes 589856 | tf_op jit(solution)/shard_map/all_to_all | solution.py:77
  793.7 21.9 %collective-permute-done.8 = bf16[2,4,24,3072]{3,2,1,0:T(8,128)(2,1)} collective-permute-done((bf16[2,4,24,3072]{3,2,1,0:T(8,128)(2,1)S(1)}, bf16[2,4,24,3072]{3,2,1,0:T(8,128)(2,1)}, u32[]{:S(2)}, u32[]{:S(2)}) %collective-permute-start.8) | collective-permute-done | bytes 1179680 | tf_op jit(solution)/shard_map/ppermute | solution.py:57
  819.7 29.1 %collective-permute-done.6 = bf16[4,8,2304]{2,1,0:T(8,128)(2,1)S(1)} collective-permute-done((bf16[4,8,2304]{2,1,0:T(8,128)(2,1)S(1)}, bf16[4,8,2304]{2,1,0:T(8,128)(2,1)S(1)}, u32[]{:S(2)}, u32[]{:S(2)}) %collective-permute-start.6) | collective-permute-done | bytes 147488 | tf_op jit(solution)/shard_map/ppermute | solution.py:57
  870.5 9.0 collective-permute-done.3
  893.6 18.9 %all-to-all-done.3 = bf16[4,192,768]{2,1,0:T(8,128)(2,1)S(1)} async-done(((bf16[4,192,768]{2,1,0:T(8,128)(2,1)}), bf16[4,192,768]{2,1,0:T(8,128)(2,1)S(1)}, u32[]{:S(2)}, u32[]{:S(2)}) %all-to-all-start.3) | async-done | bytes 1179680 | tf_op jit(solution)/shard_map/all_to_all | solution.py:77
  (624 shorter events, 385.0 us)
Async XLA Ops:
  7.2 61.3 %all-gather.9.cloned.1.call-start = ((), (), s32[]{:S(2)}) async-start(), calls=%async_computation.13 | async-start | bytes 1216512 | tf_op jit(solution)/shard_map/all_gather | solution.py:96
  8.9 143.7 %all-gather.11.cloned.1.call-start = ((), (), s32[]{:S(2)}) async-start(), calls=%async_computation.14 | async-start | bytes 9732096 | tf_op jit(solution)/shard_map/all_gather | solution.py:96
  10.8 225.5 %all-gather.13.cloned.1.call-start = ((), (), s32[]{:S(2)}) async-start(), calls=%async_computation.15 | async-start | bytes 9732096 | tf_op jit(solution)/shard_map/all_gather | solution.py:96
  13.7 288.5 %all-gather.17.cloned.1.call-start = ((), (), s32[]{:S(2)}) async-start(), calls=%async_computation.17 | async-start | bytes 4866048 | tf_op jit(solution)/shard_map/all_gather | solution.py:96
  14.6 371.0 %all-gather.15.cloned.1.call-start = ((), (), s32[]{:S(2)}) async-start(), calls=%async_computation.16 | async-start | bytes 9732096 | tf_op jit(solution)/shard_map/all_gather | solution.py:96
  25.7 425.5 %all-gather.19.cloned.1.call-start = ((), (), s32[]{:S(2)}) async-start(), calls=%async_computation.18 | async-start | bytes 4866048 | tf_op jit(solution)/shard_map/all_gather | solution.py:96
  504.7 71.3 %all-to-all-start = ((f32[32,1,4]{2,1,0:T(1,128)}), f32[32,1,4]{2,1,0:T(1,128)}, u32[]{:S(2)}, u32[]{:S(2)}) async-start(f32[32,1,4]{2,1,0:T(1,128)} %broadcast_in_dim.207), calls=%async_computation | async-start | bytes 32768 | tf_op jit(solution)/shard_map/all_to_all | solution.py:83
  507.9 179.1 %reduce-scatter.4.cloned.1.call-start = ((), (), s32[]{:S(2)}) async-start(), calls=%async_computation.19 | async-start | bytes 3538944
  585.1 29.0 %collective-permute-start.17 = (bf16[2,4,24,3072]{3,2,1,0:T(8,128)(2,1)S(1)}, bf16[2,4,24,3072]{3,2,1,0:T(8,128)(2,1)}, u32[]{:S(2)}, u32[]{:S(2)}) collective-permute-start(bf16[2,4,24,3072]{3,2,1,0:T(8,128)(2,1)S(1)} %fusion.55), channel_id=1, source_target_pairs={{0,8},{8,0},{16,24},{24,16},{1,9},{9,1},{17,25},{25,17},{2,10},{10... | collective-permute-start | bytes 3538952 | tf_op jit(solution)/shard_map/ppermute | solution.py:57
  589.4 45.6 %collective-permute-start.11 = (bf16[2,4,24,3072]{3,2,1,0:T(8,128)(2,1)S(1)}, bf16[2,4,24,3072]{3,2,1,0:T(8,128)(2,1)}, u32[]{:S(2)}, u32[]{:S(2)}) collective-permute-start(bf16[2,4,24,3072]{3,2,1,0:T(8,128)(2,1)S(1)} %fusion.53), channel_id=1, source_target_pairs={{0,16},{8,24},{16,0},{24,8},{1,17},{9,25},{17,1},{25,9},{2,18},{10... | collective-permute-start | bytes 3538952 | tf_op jit(solution)/shard_map/ppermute | solution.py:57
  593.1 46.3 %collective-permute-start.20 = (bf16[2,4,96,768]{3,2,1,0:T(8,128)(2,1)S(1)}, bf16[2,4,96,768]{3,2,1,0:T(8,128)(2,1)}, u32[]{:S(2)}, u32[]{:S(2)}) collective-permute-start(bf16[2,4,96,768]{3,2,1,0:T(8,128)(2,1)S(1)} %fusion.56), channel_id=1, source_target_pairs={{0,8},{8,0},{16,24},{24,16},{1,9},{9,1},{17,25},{25,17},{2,10},{10... | collective-permute-start | bytes 3538952 | tf_op jit(solution)/shard_map/ppermute | solution.py:57
  596.8 63.3 %collective-permute-start.14 = (bf16[2,4,24,3072]{3,2,1,0:T(8,128)(2,1)S(1)}, bf16[2,4,24,3072]{3,2,1,0:T(8,128)(2,1)S(1)}, u32[]{:S(2)}, u32[]{:S(2)}) collective-permute-start(bf16[2,4,24,3072]{3,2,1,0:T(8,128)(2,1)S(1)} %fusion.54), channel_id=1, source_target_pairs={{0,16},{8,24},{16,0},{24,8},{1,17},{9,25},{17,1},{25,9},{2,18},{10... | collective-permute-start | bytes 3538952 | tf_op jit(solution)/shard_map/ppermute | solution.py:57
  611.2 52.4 %collective-permute-start.24 = (bf16[4,96,768]{2,1,0:T(8,128)(2,1)S(1)}, bf16[4,96,768]{2,1,0:T(8,128)(2,1)S(1)}, u32[]{:S(2)}, u32[]{:S(2)}) collective-permute-start(bf16[4,96,768]{2,1,0:T(8,128)(2,1)S(1)} %fusion.96), channel_id=1, source_target_pairs={{0,8},{8,0},{16,24},{24,16},{1,9},{9,1},{17,25},{25,17},{2,10},{10... | collective-permute-start | bytes 1769480 | tf_op jit(solution)/shard_map/ppermute | solution.py:57
  616.5 56.4 %collective-permute-start.18 = (bf16[4,24,3072]{2,1,0:T(8,128)(2,1)}, bf16[4,24,3072]{2,1,0:T(8,128)(2,1)}, u32[]{:S(2)}, u32[]{:S(2)}) collective-permute-start(bf16[4,24,3072]{2,1,0:T(8,128)(2,1)} %fusion.94), channel_id=1, source_target_pairs={{0,16},{8,24},{16,0},{24,8},{1,17},{9,25},{17,1},{25,9},{2,18},{10... | collective-permute-start | bytes 1769480 | tf_op jit(solution)/shard_map/ppermute | solution.py:57
  637.7 37.2 %collective-permute-start.12 = (bf16[4,24,3072]{2,1,0:T(8,128)(2,1)}, bf16[4,24,3072]{2,1,0:T(8,128)(2,1)}, u32[]{:S(2)}, u32[]{:S(2)}) collective-permute-start(bf16[4,24,3072]{2,1,0:T(8,128)(2,1)} %fusion.92), channel_id=1, source_target_pairs={{0,8},{8,0},{16,24},{24,16},{1,9},{9,1},{17,25},{25,17},{2,10},{10... | collective-permute-start | bytes 1769480 | tf_op jit(solution)/shard_map/ppermute | solution.py:57
  641.9 43.1 %collective-permute-start.21 = (bf16[4,96,768]{2,1,0:T(8,128)(2,1)}, bf16[4,96,768]{2,1,0:T(8,128)(2,1)}, u32[]{:S(2)}, u32[]{:S(2)}) collective-permute-start(bf16[4,96,768]{2,1,0:T(8,128)(2,1)} %fusion.95), channel_id=1, source_target_pairs={{0,16},{8,24},{16,0},{24,8},{1,17},{9,25},{17,1},{25,9},{2,18},{10... | collective-permute-start | bytes 1769480 | tf_op jit(solution)/shard_map/ppermute | solution.py:57
  722.2 63.9 %collective-permute-start.1 = (bf16[2,2,4,192,768]{4,3,2,1,0:T(8,128)(2,1)}, bf16[2,2,4,192,768]{4,3,2,1,0:T(8,128)(2,1)}, u32[]{:S(2)}, u32[]{:S(2)}) collective-permute-start(bf16[2,2,4,192,768]{4,3,2,1,0:T(8,128)(2,1)} %dynamic-slice_bitcast_fusion), channel_id=1, source_target_pairs={{0,1},{1,0},{2,3},{3,2},{4,5},{5,4},{6,7},{7,6},{8,9},{9,8},{10,11... | collective-permute-start | bytes 14155784 | tf_op jit(solution)/shard_map/ppermute | solution.py:57
  739.5 43.1 %collective-permute-start.7 = (bf16[2,2,4,24,3072]{4,3,2,1,0:T(8,128)(2,1)}, bf16[2,2,4,24,3072]{4,3,2,1,0:T(8,128)(2,1)}, u32[]{:S(2)}, u32[]{:S(2)}) collective-permute-start(bf16[2,2,4,24,3072]{4,3,2,1,0:T(8,128)(2,1)} %dynamic-slice_bitcast_fusion.6), channel_id=1, source_target_pairs={{0,1},{1,0},{2,3},{3,2},{4,5},{5,4},{6,7},{7,6},{8,9},{9,8},{10,11... | collective-permute-start | bytes 7077896 | tf_op jit(solution)/shard_map/ppermute | solution.py:57
  775.3 80.0 %all-to-all-start.2 = ((f32[32,1,336]{2,1,0:T(1,128)}), f32[32,1,336]{2,1,0:T(1,128)}, u32[]{:S(2)}, u32[]{:S(2)}) async-start(f32[32,1,336]{2,1,0:T(1,128)} %all_to_all.46), calls=%async_computation.2 | async-start | bytes 98304 | tf_op jit(solution)/shard_map/all_to_all | solution.py:92
  786.0 29.7 %collective-permute-start.8 = (bf16[2,4,24,3072]{3,2,1,0:T(8,128)(2,1)S(1)}, bf16[2,4,24,3072]{3,2,1,0:T(8,128)(2,1)}, u32[]{:S(2)}, u32[]{:S(2)}) collective-permute-start(bf16[2,4,24,3072]{3,2,1,0:T(8,128)(2,1)S(1)} %fusion.52), channel_id=1, source_target_pairs={{0,8},{8,0},{16,24},{24,16},{1,9},{9,1},{17,25},{25,17},{2,10},{10... | collective-permute-start | bytes 3538952 | tf_op jit(solution)/shard_map/ppermute | solution.py:57
  791.5 58.0 %collective-permute-start.2 = (bf16[2,4,192,768]{3,2,1,0:T(8,128)(2,1)S(1)}, bf16[2,4,192,768]{3,2,1,0:T(8,128)(2,1)S(1)}, u32[]{:S(2)}, u32[]{:S(2)}) collective-permute-start(bf16[2,4,192,768]{3,2,1,0:T(8,128)(2,1)S(1)} %fusion.33), channel_id=1, source_target_pairs={{0,16},{8,24},{16,0},{24,8},{1,17},{9,25},{17,1},{25,9},{2,18},{10... | collective-permute-start | bytes 7077896 | tf_op jit(solution)/shard_map/ppermute | solution.py:57
  793.5 55.3 %collective-permute-start.6 = (bf16[4,8,2304]{2,1,0:T(8,128)(2,1)S(1)}, bf16[4,8,2304]{2,1,0:T(8,128)(2,1)S(1)}, u32[]{:S(2)}, u32[]{:S(2)}) collective-permute-start(bf16[4,8,2304]{2,1,0:T(8,128)(2,1)S(1)} %fusion.115), channel_id=1, source_target_pairs={{0,16},{8,24},{16,0},{24,8},{1,17},{9,25},{17,1},{25,9},{2,18},{10... | collective-permute-start | bytes 442376 | tf_op jit(solution)/shard_map/ppermute | solution.py:57
  818.1 42.3 %collective-permute-start.9 = (bf16[4,24,3072]{2,1,0:T(8,128)(2,1)}, bf16[4,24,3072]{2,1,0:T(8,128)(2,1)}, u32[]{:S(2)}, u32[]{:S(2)}) collective-permute-start(bf16[4,24,3072]{2,1,0:T(8,128)(2,1)} %fusion.91), channel_id=1, source_target_pairs={{0,16},{8,24},{16,0},{24,8},{1,17},{9,25},{17,1},{25,9},{2,18},{10... | collective-permute-start | bytes 1769480 | tf_op jit(solution)/shard_map/ppermute | solution.py:57
  882.9 29.7 %all-to-all-start.3 = ((bf16[4,192,768]{2,1,0:T(8,128)(2,1)}), bf16[4,192,768]{2,1,0:T(8,128)(2,1)S(1)}, u32[]{:S(2)}, u32[]{:S(2)}) async-start(bf16[4,192,768]{2,1,0:T(8,128)(2,1)} %fusion.34), calls=%async_computation.3 | async-start | bytes 2359296 | tf_op jit(solution)/shard_map/all_to_all | solution.py:77
  (178 other events, 2066.4 us)
Sparse Core Ops, SparseCore 0:
  11.6 56.8 all-gather.8
  72.1 80.4 all-gather.10
  156.2 80.0 all-gather.12
  239.7 62.4 all-gather.16
  305.7 79.8 all-gather.14
  389.0 62.1 all-gather.18
  549.3 41.5 reduce-scatter.3

commit v2 on v1

v2 whole, which is shorter than its diff:
```python
import jax
import jax.numpy as jnp
from jax import lax
from jax.experimental import pallas as pl
from jax.experimental.pallas import tpu as pltpu
from jax.sharding import PartitionSpec as P

D = 768
HEAD_DIM = 64
FF = 3072
PATCH = 8
VOCAB = 256
GROUPS = 4
STEP_NUMBER = 7


EPSILON = 1e-05
CLIP_AT = 0.01
BETA_ONE = 0.9
BETA_TWO = 0.95
ADAM_EPS = 1e-08
DECAY = 0.1
NEGATIVE = -1e30


def norm_forward(values, gain):
    scale = lax.rsqrt(jnp.mean(values * values, axis=-1, keepdims=True) + EPSILON)
    normed = values * scale
    return (normed * gain, (normed, scale))


def norm_backward(upstream, normed, scale, gain):
    gain_grad = jnp.sum(upstream * normed, axis=0)
    inner = upstream * gain
    return (scale * (inner - normed * jnp.mean(inner * normed, axis=-1, keepdims=True)), gain_grad)


def to_half(value):
    return value.astype(jnp.bfloat16)


def wide(value):
    return value.astype(jnp.float32)


def pick(value, index, axis):
    return lax.dynamic_index_in_dim(value, index, axis, keepdims=False)


def swap(value, axis, bit):
    count = lax.axis_size(axis)
    return lax.ppermute(value, axis, [(at, at ^ bit) for at in range(count)])


def same_core():
    seq = lax.axis_size("seq")
    return [list(range(first, seq, 2)) for first in range(2)]


def deal_depth(value):
    return lax.all_to_all(
        to_half(value), "seq", 0, 0, axis_index_groups=same_core(), tiled=True
    )


def along_depth(value):
    return jnp.sum(wide(deal_depth(value)), axis=0)


def gather_seq(value):
    seq = lax.axis_size("seq")
    mine = lax.all_to_all(
        jnp.broadcast_to(value[None], (seq // 2,) + value.shape),
        "seq",
        0,
        0,
        axis_index_groups=same_core(),
        tiled=True,
    )
    other = swap(mine, "seq", 1)
    second = lax.axis_index("seq") % 2 == 1
    pair = jnp.stack([jnp.where(second, other, mine), jnp.where(second, mine, other)], axis=1)
    return pair.reshape(seq * value.shape[0], value.shape[1])


def group_steps(partials, width, deal=True):
    items, seq = lax.axis_size("items"), lax.axis_size("seq")
    at_item, at_seq = lax.axis_index("items"), lax.axis_index("seq")
    core, x_at, y_at = at_seq % 2, at_item % 2, at_item // 2
    depth = seq // 2
    grids = [
        part.reshape(items // 2, 2, depth, 2, part.shape[0] // (items * seq), part.shape[1])
        for part in partials
    ]

    def side(index):
        return jnp.concatenate(
            [
                pick(grid, index, 3)[..., begin : begin + width]
                for grid in grids
                for begin in range(0, grid.shape[-1], width)
            ],
            axis=3,
        )

    kept = side(core)
    (sent,) = yield (side(1 - core),)
    (got,) = yield (swap(sent, "seq", 1),)
    rows = kept.shape[3]
    cut = rows // 16 * 8
    halves = ((0, cut), (cut, rows))

    def cells(value, y_from, y_count, x_from, x_count, half):
        begin, end = halves[half]
        return lax.dynamic_slice(
            value,
            (y_from, x_from, 0, begin, 0),
            (y_count, x_count, depth, end - begin, width),
        )

    def pair_sum(*where):
        return wide(cells(kept, *where)) + wide(cells(got, *where))

    to_x, to_y = yield (
        to_half(pair_sum(0, 2, 1 - x_at, 1, 0)),
        to_half(pair_sum(1 - y_at, 1, 0, 2, 1)),
    )
    first_in, second_in = yield swap(to_x, "items", 1), swap(to_y, "items", 2)
    to_y, to_x = yield (
        to_half(
            pair_sum(1 - y_at, 1, x_at, 1, 0)
            + wide(lax.dynamic_slice_in_dim(first_in, 1 - y_at, 1, 0))
        ),
        to_half(
            pair_sum(y_at, 1, 1 - x_at, 1, 1)
            + wide(lax.dynamic_slice_in_dim(second_in, 1 - x_at, 1, 1))
        ),
    )
    first_end, second_end = yield swap(to_y, "items", 2), swap(to_x, "items", 1)
    first = (
        pair_sum(y_at, 1, x_at, 1, 0)
        + wide(lax.dynamic_slice_in_dim(first_in, y_at, 1, 0))
        + wide(first_end)
    )
    second = (
        pair_sum(y_at, 1, x_at, 1, 1)
        + wide(lax.dynamic_slice_in_dim(second_in, x_at, 1, 1))
        + wide(second_end)
    )
    (blocks,) = yield (
        jnp.concatenate([to_half(first[0, 0]), to_half(second[0, 0])], axis=1),
    )
    if deal:
        (blocks,) = yield (deal_depth(blocks),)
    rows = jnp.sum(wide(blocks), axis=0)
    out, at = [], 0
    for grid in grids:
        deep, pieces = grid.shape[4], []
        for _ in range(0, grid.shape[-1], width):
            pieces.append(rows[at : at + deep])
            at += deep
        out.append(jnp.concatenate(pieces, axis=1))
    return out


def in_order(mine, other, bit, axis):
    return jnp.stack(
        [jnp.where(bit == 1, other, mine), jnp.where(bit == 1, mine, other)], axis=axis
    )


def gather_steps(mine):
    items, seq = lax.axis_size("items"), lax.axis_size("seq")
    at_item, at_seq = lax.axis_index("items"), lax.axis_index("seq")
    core, x_at, y_at = at_seq % 2, at_item % 2, at_item // 2
    rows, width = mine.shape[1:]
    cut = width // 2
    first, second = yield (mine[..., :cut], mine[..., cut:])
    to_x, to_y = yield (swap(first, "items", 1), swap(second, "items", 2))
    first, second = yield (in_order(first, to_x, x_at, 0), in_order(second, to_y, y_at, 0))
    to_y, to_x = yield (swap(first, "items", 2), swap(second, "items", 1))
    (mine,) = yield (
        jnp.concatenate(
            [in_order(first, to_y, y_at, 0), in_order(second, to_x, x_at, 1)], axis=-1
        ),
    )
    (other,) = yield (swap(mine, "seq", 1),)
    return in_order(mine, other, core, 3).reshape(items * seq * rows, width)


class Stepped:
    def __init__(self, steps):
        self.steps = steps
        self.held = next(self.steps)
        self.sending = True
        self.result = None

    def feed(self, arrays):
        try:
            self.held = self.steps.send(tuple(arrays))
        except StopIteration as end:
            self.held, self.result = (), end.value
        self.sending = not self.sending


def tie(values, groups):
    flat = list(values)
    for group in groups:
        flat.extend(group.held)
    flat = list(lax.optimization_barrier(tuple(flat)))
    values, flat = flat[: len(values)], flat[len(values) :]
    for group in groups:
        size = len(group.held)
        group.feed(flat[:size])
        flat = flat[size:]
    return values


def advance(values, *groups):
    waiting = [group for group in groups if group.result is None and not group.sending]
    if waiting:
        values = tie(values, waiting)
    sending = [group for group in groups if group.result is None]
    return tie(values, sending) if sending else values


def reduce_group(partials, width):
    group = Stepped(group_steps(partials, width))
    while group.result is None:
        advance([], group)
    return group.result


def share(row):
    count = lax.axis_size("items") * lax.axis_size("seq")
    return lax.all_to_all(
        jnp.broadcast_to(row[None], (count,) + row.shape), ("items", "seq"), 0, 0, tiled=True
    )


def spread(value):
    count = lax.axis_size("items") * lax.axis_size("seq")
    size = -(-value.shape[0] // count)
    return jnp.pad(value, (0, size * count - value.shape[0])).reshape(count, size)


def gather_rows(value):
    return lax.all_gather(value, ("items", "seq"), axis=0, tiled=True)


def one_hot(indices, width, dtype):
    return (indices.reshape(-1)[:, None] == jnp.arange(width)[None, :]).astype(dtype)


def hot_sum(hot, value):
    high = to_half(value)
    rest = to_half(value - wide(high))
    add = lambda term: jnp.einsum("rv,rd->vd", hot, term, preferred_element_type=jnp.float32)
    return add(high) + add(rest)


def layer_forward(resid, gains, qkv_w, out_w, in_w, down_w, attend):
    attn_in, (normed_one, scale_one) = norm_forward(resid, gains[0])
    attn_half = attn_in.astype(jnp.bfloat16)
    qkv_half = jnp.dot(attn_half, qkv_w, preferred_element_type=jnp.float32).astype(jnp.bfloat16)
    mixed, kept = attend(qkv_half)
    mixed_half = mixed.astype(jnp.bfloat16)
    middle = resid + jnp.dot(mixed_half, out_w, preferred_element_type=jnp.float32)
    mlp_norm, (normed_two, scale_two) = norm_forward(middle, gains[1])
    mlp_half = mlp_norm.astype(jnp.bfloat16)
    hidden = jnp.dot(mlp_half, in_w, preferred_element_type=jnp.float32)
    active_half = jax.nn.gelu(hidden).astype(jnp.bfloat16)
    result = middle + jnp.dot(active_half, down_w, preferred_element_type=jnp.float32)
    saved = (
        normed_one,
        scale_one,
        attn_half,
        qkv_half,
        mixed,
        mixed_half,
        kept,
        normed_two,
        scale_two,
        mlp_half,
        hidden,
        active_half,
    )
    return (result, saved)


def layer_backward(result_grad, saved, gains, qkv_w, out_w, in_w, down_w, attend_back, after):
    (
        normed_one,
        scale_one,
        attn_half,
        qkv_half,
        mixed,
        mixed_half,
        kept,
        normed_two,
        scale_two,
        mlp_half,
        hidden,
        active_half,
    ) = saved
    branch_half = result_grad.astype(jnp.bfloat16)
    active_grad = jnp.einsum("rd,fd->rf", branch_half, down_w, preferred_element_type=jnp.float32)
    _, gelu_back = jax.vjp(jax.nn.gelu, hidden)
    hidden_half = gelu_back(active_grad)[0].astype(jnp.bfloat16)
    hidden_half = after("mlp", hidden_half, (mlp_half, hidden_half), (active_half, branch_half))
    mlp_grad = jnp.einsum("rf,df->rd", hidden_half, in_w, preferred_element_type=jnp.float32)
    middle_grad, gain_two = norm_backward(mlp_grad, normed_two, scale_two, gains[1])
    middle_grad = middle_grad + result_grad
    proj_half = middle_grad.astype(jnp.bfloat16)
    mixed_grad = jnp.einsum("rd,ed->re", proj_half, out_w, preferred_element_type=jnp.float32)
    mixed_grad_half = after("attention", mixed_grad.astype(jnp.bfloat16))
    qkv_grad_half = attend_back(mixed_grad_half, qkv_half, kept, mixed).astype(jnp.bfloat16)
    qkv_grad_half = after("projections", qkv_grad_half, attn_half, mixed_half, proj_half)
    attn_grad = jnp.einsum("re,de->rd", qkv_grad_half, qkv_w, preferred_element_type=jnp.float32)
    resid_grad, gain_one = norm_backward(attn_grad, normed_one, scale_one, gains[0])
    resid_grad = after("end", resid_grad + middle_grad)
    return resid_grad, jnp.stack([gain_one, gain_two])


def outer(pair):
    return jnp.einsum("ri,rj->ij", *pair, preferred_element_type=jnp.float32)


def deal_columns(parts):
    count = lax.axis_size("items") * lax.axis_size("seq")
    rows = parts[0].shape[0]
    blocks = jnp.concatenate([part.reshape(rows, count, -1) for part in parts], axis=2)
    dealt = lax.all_to_all(
        blocks.transpose(1, 0, 2), ("items", "seq"), 0, 0, tiled=True
    ).reshape(count * rows, -1)
    out, at = [], 0
    for part in parts:
        size = part.shape[1] // count
        out.append(dealt[:, at : at + size])
        at += size
    return out


def deal_rows(parts):
    count = lax.axis_size("items") * lax.axis_size("seq")
    blocks = jnp.concatenate([to_half(part) for part in parts], axis=1)
    dealt = lax.all_to_all(
        blocks.reshape(count, -1, blocks.shape[1]), ("items", "seq"), 0, 0, tiled=True
    )
    out, at = [], 0
    for part in parts:
        size = part.shape[1]
        piece = dealt[:, :, at : at + size].transpose(1, 0, 2)
        out.append(wide(piece.reshape(piece.shape[0], -1)))
        at += size
    return out


ROWS = 128
LANES = 128


def contract(left, right, left_dim, right_dim):
    return lax.dot_general(
        left, right, (((left_dim,), (right_dim,)), ((), ())), preferred_element_type=jnp.float32
    )


def local_masks():
    row = lax.broadcasted_iota(jnp.int32, (ROWS, ROWS), 0)
    column = lax.broadcasted_iota(jnp.int32, (ROWS, ROWS), 1)
    allowed = (row // PATCH == column // PATCH) & (column <= row)
    lane = lax.broadcasted_iota(jnp.int32, (ROWS, LANES), 1)
    lanes = [
        jnp.where(lane // HEAD_DIM == head, 1.0, 0.0).astype(jnp.bfloat16)
        for head in range(LANES // HEAD_DIM)
    ]
    return allowed, lanes


def local_probs(query, key, allowed):
    scores = contract(query, key, 1, 1) * HEAD_DIM ** (-0.5)
    scores = jnp.where(allowed, scores, NEGATIVE)
    raised = jnp.exp(scores - jnp.max(scores, axis=-1, keepdims=True))
    return raised / jnp.sum(raised, axis=-1, keepdims=True)


def local_forward_kernel(qkv_ref, mixed_ref):
    width = mixed_ref.shape[1]
    allowed, lanes = local_masks()
    for begin in range(0, width, LANES):
        query, key, value = (
            qkv_ref[:, part * width + begin : part * width + begin + LANES] for part in range(3)
        )
        mixed = jnp.zeros((ROWS, LANES), jnp.float32)
        for mask in lanes:
            probs = local_probs(query * mask, key, allowed).astype(jnp.bfloat16)
            mixed = mixed + contract(probs, value * mask, 1, 0)
        mixed_ref[:, begin : begin + LANES] = mixed.astype(jnp.bfloat16)


def local_backward_kernel(qkv_ref, grad_ref, out_ref):
    width = grad_ref.shape[1]
    allowed, lanes = local_masks()
    scale = HEAD_DIM ** (-0.5)
    for begin in range(0, width, LANES):
        query, key, value = (
            qkv_ref[:, part * width + begin : part * width + begin + LANES] for part in range(3)
        )
        upstream = grad_ref[:, begin : begin + LANES]
        sums = [jnp.zeros((ROWS, LANES), jnp.float32) for _ in range(3)]
        for mask in lanes:
            head_query, head_upstream = query * mask, upstream * mask
            probs = local_probs(head_query, key, allowed)
            prob_grad = contract(head_upstream, value, 1, 1)
            inner = jnp.sum(prob_grad * probs, axis=-1, keepdims=True)
            score_half = (probs * (prob_grad - inner)).astype(jnp.bfloat16)
            sums[0] = sums[0] + contract(score_half, key * mask, 1, 0)
            sums[1] = sums[1] + contract(score_half, head_query, 0, 0)
            sums[2] = sums[2] + contract(probs.astype(jnp.bfloat16), head_upstream, 0, 0)
        for part, factor in enumerate((scale, scale, 1.0)):
            at = part * width + begin
            out_ref[:, at : at + LANES] = (sums[part] * factor).astype(jnp.bfloat16)


def by_rows(kernel, out_width, *operands):
    rows = operands[0].shape[0]
    moved = sum(value.size for value in operands) * 2 + rows * out_width * 2
    return pl.pallas_call(
        kernel,
        grid=(rows // ROWS,),
        in_specs=[pl.BlockSpec((ROWS, value.shape[1]), lambda at: (at, 0)) for value in operands],
        out_specs=pl.BlockSpec((ROWS, out_width), lambda at: (at, 0)),
        out_shape=jax.ShapeDtypeStruct((rows, out_width), jnp.bfloat16),
        cost_estimate=pl.CostEstimate(
            flops=rows * ROWS * out_width * 8, bytes_accessed=moved, transcendentals=rows * ROWS
        ),
    )(*operands)


def local_forward(qkv_half):
    return by_rows(local_forward_kernel, qkv_half.shape[1] // 3, qkv_half), None


def local_backward(grad_half, qkv_half, kept, mixed):
    return by_rows(local_backward_kernel, qkv_half.shape[1], qkv_half, grad_half)


def patch_probs(query, key, bias):
    scores = contract(query, key, 1, 1) * HEAD_DIM ** (-0.5) + bias
    raised = jnp.exp(scores - jnp.max(scores, axis=-1, keepdims=True))
    return raised / jnp.sum(raised, axis=-1, keepdims=True)


def head_lanes():
    lane = lax.broadcasted_iota(jnp.int32, (1, LANES), 1)
    return [
        jnp.where(lane // HEAD_DIM == head, 1.0, 0.0).astype(jnp.bfloat16)
        for head in range(LANES // HEAD_DIM)
    ]


def patch_forward_kernel(query_ref, key_ref, value_ref, bias_ref, mixed_ref):
    mixed = jnp.zeros(mixed_ref.shape, jnp.float32)
    for mask in head_lanes():
        probs = patch_probs(query_ref[...] * mask, key_ref[...], bias_ref[...])
        mixed = mixed + contract(probs.astype(jnp.bfloat16), value_ref[...] * mask, 1, 0)
    mixed_ref[...] = mixed.astype(jnp.bfloat16)


def patch_backward_kernel(query_ref, key_ref, value_ref, bias_ref, grad_ref, query_out, both_out):
    seq, _, span, _ = both_out.shape
    query_grad = jnp.zeros(query_out.shape, jnp.float32)
    key_grad = jnp.zeros(key_ref.shape, jnp.float32)
    value_grad = jnp.zeros(key_ref.shape, jnp.float32)
    for mask in head_lanes():
        query, upstream, key = query_ref[...] * mask, grad_ref[...] * mask, key_ref[...]
        probs = patch_probs(query, key, bias_ref[...])
        prob_grad = contract(upstream, value_ref[...], 1, 1)
        inner = jnp.sum(prob_grad * probs, axis=-1, keepdims=True)
        score_half = (probs * (prob_grad - inner)).astype(jnp.bfloat16)
        query_grad = query_grad + contract(score_half, key * mask, 1, 0)
        key_grad = key_grad + contract(score_half, query, 0, 0)
        value_grad = value_grad + contract(probs.astype(jnp.bfloat16), upstream, 0, 0)
    scale = HEAD_DIM ** (-0.5)
    query_out[...] = (query_grad * scale).astype(jnp.bfloat16)
    both_out[:, 0] = (key_grad * scale).astype(jnp.bfloat16).reshape(seq, span, LANES)
    both_out[:, 1] = value_grad.astype(jnp.bfloat16).reshape(seq, span, LANES)


def by_heads(kernel, out_shape, out_specs, qkv_half, both_all, bias, *others):
    rows, total, pairs = qkv_half.shape[0], both_all.shape[0], both_all.shape[1] // 2 // LANES
    columns = lambda count, shift: pl.BlockSpec((count, LANES), lambda at: (0, at + shift))
    return pl.pallas_call(
        kernel,
        grid=(pairs,),
        in_specs=[
            columns(rows, 0),
            columns(total, 0),
            columns(total, pairs),
            pl.BlockSpec((rows, total), lambda at: (0, 0)),
        ]
        + [columns(rows, 0) for _ in others],
        out_specs=out_specs,
        out_shape=out_shape,
    )(qkv_half, both_all, both_all, bias, *others)


def adam_step(weight, grad, first, second, rate, count):
    first = BETA_ONE * first + (1.0 - BETA_ONE) * grad
    second = BETA_TWO * second + (1.0 - BETA_TWO) * grad * grad
    first_hat = first / (1.0 - BETA_ONE**count)
    second_hat = second / (1.0 - BETA_TWO**count)
    return (
        weight - rate * (first_hat / (jnp.sqrt(second_hat) + ADAM_EPS) + DECAY * weight),
        first,
        second,
    )


def body(
    byte_tokens,
    groups,
    doc_ids,
    patch_proj,
    tables,
    attn_qkv,
    attn_out,
    mlp_in,
    mlp_out,
    vectors,
    first_proj,
    first_tables,
    first_qkv,
    first_out,
    first_in,
    first_down,
    first_vectors,
    second_proj,
    second_tables,
    second_qkv,
    second_out,
    second_in,
    second_down,
    second_vectors,
):
    half = jnp.bfloat16
    single = jnp.float32
    width = vectors.shape[1]
    depth = attn_qkv.shape[1]
    count = lax.axis_size("items") * lax.axis_size("seq")
    rank = lax.axis_index("items") * lax.axis_size("seq") + lax.axis_index("seq")
    told = share(jnp.concatenate([byte_tokens.reshape(-1), groups.reshape(-1)]))
    told = told.reshape(count, 2, -1)
    counts = jnp.sum(one_hot(told[:, 1], GROUPS, single), axis=0)

    def flat(value):
        return jnp.concatenate(
            [value[at : at + depth] for at in range(0, value.shape[0], depth)], axis=1
        ).astype(half)

    def tall(value):
        pieces = [value[:, at : at + width] for at in range(0, value.shape[1], width)]
        pieces = [piece.reshape(count, 1, depth, width) for piece in pieces]
        return jnp.concatenate(pieces, axis=1)

    def layer_parts(n):
        return [
            attn_qkv[n].astype(half),
            attn_out[n].astype(half),
            mlp_in[n].astype(half),
            flat(mlp_out[n]),
        ]

    ends = [3 * width, 4 * width, 4 * width + mlp_in.shape[2]]
    ends.append(ends[2] + mlp_out.shape[1] // depth * width)

    def layer_weights(joined):
        return (
            joined[:, : ends[0]],
            joined[:, ends[0] : ends[1]],
            joined[:, ends[1] : ends[2]],
            tall(joined[:, ends[2] : ends[3]]).reshape(-1, width),
        )

    patch_all = gather_rows(jnp.concatenate(layer_parts(0), axis=1))
    byte_all = gather_rows(
        jnp.concatenate(layer_parts(1) + [flat(tables.reshape(-1, width))], axis=1)
    )
    weights = [layer_weights(patch_all), layer_weights(byte_all)]
    qkv_w, out_w, in_w, down_w = ([weights[n][at] for n in range(2)] for at in range(4))
    table_rows = byte_all[:, ends[3] :].reshape(count, tables.shape[0], -1, width)
    table_w = [table_rows[:, n].reshape(-1, width) for n in range(3)]

    mine = patch_proj.shape[0]
    splits = width // mine
    slot, column = rank // splits, rank % splits
    narrow = tables[0].astype(half).reshape(-1, splits, mine).transpose(1, 0, 2)
    narrow = lax.all_to_all(
        jnp.tile(narrow, (count // splits, 1, 1)), ("items", "seq"), 0, 0, tiled=True
    ).reshape(-1, mine)
    all_grid = told[:, 0].reshape(byte_tokens.shape[0] * lax.axis_size("items"), -1, PATCH)
    ahead = jnp.concatenate([jnp.zeros_like(all_grid[:, :1]), all_grid[:, :-1]], axis=1)
    slot_hot = one_hot(pick(ahead, slot, 2), VOCAB, half)
    embed_part = to_half(jnp.dot(slot_hot, narrow, preferred_element_type=single))
    proj_half = patch_proj.astype(half)
    projected_part = jnp.dot(embed_part, proj_half, preferred_element_type=single)
    projected = reduce_group([to_half(projected_part)], width)[0]
    span_rows = byte_tokens.shape[1] // PATCH
    total_patches = doc_ids.shape[1]
    offset = lax.axis_index("seq") * span_rows
    my_pos = offset + jnp.arange(span_rows)
    keep_first = (jnp.arange(PATCH) > 0).astype(single)

    def item_pass(my_bytes, my_groups, all_docs):
        group_hot = one_hot(my_groups, GROUPS, single)
        my_docs = lax.dynamic_slice_in_dim(all_docs, offset, span_rows)
        prior_docs = jnp.concatenate(
            [lax.dynamic_slice_in_dim(all_docs, jnp.maximum(offset - 1, 0), 1), my_docs[:-1]]
        )
        starts = (my_pos == 0) | (my_docs != prior_docs)

        allowed = (jnp.arange(total_patches)[None, :] <= my_pos[:, None]) & (
            all_docs[None, :] == my_docs[:, None]
        )
        bias = jnp.where(allowed, 0.0, NEGATIVE)
        narrow_spec = pl.BlockSpec((span_rows, LANES), lambda at: (0, at))

        def global_forward(qkv_half):
            both_all = gather_seq(qkv_half[:, width:])
            mixed = by_heads(
                patch_forward_kernel,
                jax.ShapeDtypeStruct((span_rows, width), half),
                narrow_spec,
                qkv_half,
                both_all,
                bias,
            )
            return (mixed, both_all)

        def global_backward(grad_half, qkv_half, both_all, mixed):
            seq = lax.axis_size("seq")
            query_grad, both_grad = by_heads(
                patch_backward_kernel,
                (
                    jax.ShapeDtypeStruct((span_rows, width), half),
                    jax.ShapeDtypeStruct((seq, 2, span_rows, width), half),
                ),
                (
                    narrow_spec,
                    pl.BlockSpec((seq, 2, span_rows, LANES), lambda at: (0, 0, 0, at)),
                ),
                qkv_half,
                both_all,
                bias,
                grad_half,
            )
            pairs = both_grad.reshape(seq // 2, 2, 2, span_rows, width)
            core = lax.axis_index("seq") % 2
            got = swap(pick(pairs, 1 - core, 1), "seq", 1)
            key_value_grad = to_half(along_depth(wide(pick(pairs, core, 1)) + wide(got)))
            return jnp.concatenate([query_grad, key_value_grad[0], key_value_grad[1]], axis=1)

        byte_grid = my_bytes.reshape(span_rows, PATCH)
        resid = jnp.where(starts[:, None], vectors[5][None, :], projected)
        top, saved_top = layer_forward(
            resid, vectors[0:2], qkv_w[0], out_w[0], in_w[0], down_w[0], global_forward
        )
        patch_sides = gather_rows(
            jnp.concatenate([saved_top[2], saved_top[5], saved_top[9]], axis=1)
        )
        top, active_columns = lax.optimization_barrier((top, deal_columns([saved_top[11]])[0]))
        before = jnp.concatenate([jnp.zeros((span_rows, 1), jnp.int32), byte_grid[:, :-1]], axis=1)
        before_hot = one_hot(before, VOCAB, half)
        local_embed = jnp.dot(before_hot, table_w[1], preferred_element_type=single).reshape(
            span_rows, PATCH, width
        )
        local_in = (
            local_embed * keep_first[None, :, None] + top[:, None, :] + vectors[6 : 6 + PATCH][None]
        )
        result, saved_low = layer_forward(
            local_in.reshape(span_rows * PATCH, width),
            vectors[2:4],
            qkv_w[1],
            out_w[1],
            in_w[1],
            down_w[1],
            local_forward,
        )
        final, (final_normed, final_scale) = norm_forward(result, vectors[4])
        final_half = final.astype(half)
        logits = jnp.einsum("rd,vd->rv", final_half, table_w[2], preferred_element_type=single)
        shifted = logits - jnp.max(logits, axis=-1, keepdims=True)
        totals = jnp.sum(jnp.exp(shifted), axis=-1, keepdims=True)
        probs = jnp.exp(shifted) / totals
        target_hot = one_hot(my_bytes, VOCAB, single)
        losses = jnp.log(totals[:, 0]) - jnp.sum(shifted * target_hot, axis=-1)
        loss_terms = jnp.sum(losses[:, None] * group_hot, axis=0)
        row_weight = jnp.sum(group_hot * (1.0 / (GROUPS * counts))[None, :], axis=-1)
        logit_half = (row_weight[:, None] * (probs - target_hot)).astype(half)
        head_grad = jnp.einsum("rv,rd->vd", logit_half, final_half, preferred_element_type=single)
        final_grad = jnp.einsum("rv,vd->rd", logit_half, table_w[2], preferred_element_type=single)
        result_grad, final_gain_grad = norm_backward(
            final_grad, final_normed, final_scale, vectors[4]
        )
        running, sides = {}, {}

        def after_low(where, value, *others):
            if where == "mlp":
                grads = [to_half(outer(pair)) for pair in others]
                running["early"] = Stepped(group_steps(grads + [to_half(head_grad)], width))
            elif where == "projections":
                attn_half, mixed_half, proj_half = others
                value, sides["all"] = lax.optimization_barrier((value, patch_sides))
                value, proj_half = advance([value, proj_half], running["early"])
                sides["qkv"], sides["out"] = (attn_half, value), (mixed_half, proj_half)
                return value
            (value,) = advance([value], running["early"])
            return value

        def after_top(where, value, *others):
            if where == "mlp":
                sides["mlp"] = others[0][1]
                (value,) = advance([value], running["low"])
            elif where == "attention":
                (value,) = advance([value], running["early"], running["low"])
            elif where == "projections":
                value, sides["top"] = lax.optimization_barrier((value, top_all))
                (value,) = tie([value], [running["low"]])
                sides["patch"] = [value, others[2], sides["mlp"]]
            return value

        local_grad, low_gains = layer_backward(
            result_grad,
            saved_low,
            vectors[2:4],
            qkv_w[1],
            out_w[1],
            in_w[1],
            down_w[1],
            local_backward,
            after_low,
        )
        grid_grad = local_grad.reshape(span_rows, PATCH, width)
        top_grad = jnp.sum(grid_grad, axis=1)
        position_grad = jnp.sum(grid_grad, axis=0)
        masked_grad = (grid_grad * keep_first[None, :, None]).reshape(span_rows * PATCH, width)
        local_table_grad = hot_sum(before_hot, masked_grad)
        top_all = gather_rows(to_half(top_grad))
        low_partials = [to_half(outer(sides["qkv"])), to_half(outer(sides["out"]))]
        running["low"] = Stepped(
            group_steps(low_partials + [to_half(local_table_grad)], width, deal=False)
        )
        (top_grad,) = advance([top_grad], running["low"])
        resid_grad, top_gains = layer_backward(
            top_grad,
            saved_top,
            vectors[0:2],
            qkv_w[0],
            out_w[0],
            in_w[0],
            down_w[0],
            global_backward,
            after_top,
        )
        start_grad = jnp.sum(jnp.where(starts[:, None], resid_grad, 0.0), axis=0)
        projected_half = jnp.where(starts[:, None], 0.0, resid_grad).astype(half)
        vector_grad = jnp.concatenate(
            [top_gains, low_gains, final_gain_grad[None], start_grad[None], position_grad],
            axis=0,
        )
        own = jnp.broadcast_to(
            projected_half[None], (lax.axis_size("seq") // 2,) + projected_half.shape
        )
        joint = deal_depth(jnp.concatenate([own, running["low"].held[0]], axis=1))
        joint, *patch = lax.optimization_barrier((joint, *sides["patch"]))
        running["low"].feed([joint[:, span_rows:]])
        running["gather"] = Stepped(gather_steps(joint[:, :span_rows]))
        advance([], running["gather"])
        columns = deal_columns(patch)
        patch_down = outer((active_columns, sides["top"]))
        (patch_down,) = advance([patch_down], running["gather"])
        columns = advance(columns, running["gather"])
        attn_all, mixed_all, mlp_all = (
            sides["all"][:, at * width : (at + 1) * width] for at in range(3)
        )
        blocks = [outer(pair) for pair in zip((attn_all, mixed_all, mlp_all), columns)]
        blocks = advance([to_half(part) for part in blocks], running["gather"])
        patch_qkv, patch_out, patch_in = deal_rows(blocks)
        projected_all = running["gather"].result
        proj_grad = jnp.einsum(
            "ri,rd->id", embed_part, projected_all, preferred_element_type=single
        )
        embed_grad = jnp.einsum(
            "rd,id->ri", projected_all, proj_half, preferred_element_type=single
        )
        slot_grad = hot_sum(slot_hot, embed_grad)
        slot_grad, patch_qkv, patch_out, patch_in = lax.optimization_barrier(
            (slot_grad, patch_qkv, patch_out, patch_in)
        )
        slot_size, vector_rows = slot_grad.size // count, spread(vector_grad.reshape(-1))
        dealt = lax.all_to_all(
            jnp.concatenate([slot_grad.reshape(count, slot_size), vector_rows], axis=1),
            ("items", "seq"),
            0,
            0,
            tiled=True,
        )
        vector_piece = jnp.sum(dealt[:, slot_size:], axis=0)
        slot_rows = dealt[:, :slot_size].reshape(count, -1, mine)
        slot_rows = jnp.sum(slot_rows.reshape(PATCH, splits, -1, mine), axis=0)
        global_table_grad = slot_rows.transpose(1, 0, 2).reshape(-1, width)
        assert all(group.result is not None for group in running.values())
        early, low = running["early"].result, running["low"].result
        owned = (
            proj_grad,
            jnp.stack([global_table_grad, low[2], early[2]]),
            jnp.stack([patch_qkv, low[0]]),
            jnp.stack([patch_out, low[1]]),
            jnp.stack([patch_in, early[0]]),
            jnp.stack([patch_down, early[1]]),
        )
        return (loss_terms, owned, vector_piece)

    loss_terms, owned, vector_piece = item_pass(byte_tokens[0], groups[0], doc_ids[0])
    shard_square = sum((jnp.sum(piece * piece) for piece in owned))
    shard_square = shard_square + jnp.sum(vector_piece * vector_piece)
    tail = share(jnp.concatenate([vector_piece, shard_square[None], loss_terms]))
    size = vector_piece.shape[0]
    vector_total = tail[:, :size].reshape(-1)[: vectors.size].reshape(vectors.shape)
    loss_total = jnp.sum(tail[:, size + 1 :], axis=0)
    loss = jnp.sum(loss_total / counts) / GROUPS
    grad_norm = jnp.sqrt(jnp.sum(tail[:, size]))
    factor = jnp.minimum(1.0, CLIP_AT / grad_norm)
    step = float(STEP_NUMBER)
    rates = (
        (PATCH * D) ** (-0.5),
        jnp.array([1.0, 1.0, 2.0 * D ** (-0.5)], single).reshape(3, 1, 1),
        D ** (-0.5),
        (D // 8) ** (-0.5),
        D ** (-0.5),
        FF ** (-0.5),
        0.5,
    )
    masters = (patch_proj, tables, attn_qkv, attn_out, mlp_in, mlp_out, vectors)
    grads = tuple(owned) + (vector_total,)
    firsts = (first_proj, first_tables, first_qkv, first_out, first_in, first_down, first_vectors)
    seconds = (
        second_proj,
        second_tables,
        second_qkv,
        second_out,
        second_in,
        second_down,
        second_vectors,
    )
    done = [
        adam_step(masters[n], grads[n] * factor, firsts[n], seconds[n], rates[n], step)
        for n in range(7)
    ]
    return (
        loss,
        grad_norm,
        done[0][0],
        done[1][0],
        done[2][0],
        done[3][0],
        done[4][0],
        done[5][0],
        done[6][0],
        done[0][1],
        done[1][1],
        done[2][1],
        done[3][1],
        done[4][1],
        done[5][1],
        done[6][1],
        done[0][2],
        done[1][2],
        done[2][2],
        done[3][2],
        done[4][2],
        done[5][2],
        done[6][2],
    )


def solution(mesh):
    return jax.shard_map(
        body,
        mesh=mesh,
        in_specs=(
            P("items", "seq"),
            P("items", "seq"),
            P("items", None),
            P(("items", "seq"), None),
            P(None, ("items", "seq"), None),
            P(None, ("items", "seq"), None),
            P(None, ("items", "seq"), None),
            P(None, ("items", "seq"), None),
            P(None, ("items", "seq"), None),
            P(),
            P(("items", "seq"), None),
            P(None, ("items", "seq"), None),
            P(None, ("items", "seq"), None),
            P(None, ("items", "seq"), None),
            P(None, ("items", "seq"), None),
            P(None, ("items", "seq"), None),
            P(),
            P(("items", "seq"), None),
            P(None, ("items", "seq"), None),
            P(None, ("items", "seq"), None),
            P(None, ("items", "seq"), None),
            P(None, ("items", "seq"), None),
            P(None, ("items", "seq"), None),
            P(),
        ),
        out_specs=(
            P(),
            P(),
            P(("items", "seq"), None),
            P(None, ("items", "seq"), None),
            P(None, ("items", "seq"), None),
            P(None, ("items", "seq"), None),
            P(None, ("items", "seq"), None),
            P(None, ("items", "seq"), None),
            P(),
            P(("items", "seq"), None),
            P(None, ("items", "seq"), None),
            P(None, ("items", "seq"), None),
            P(None, ("items", "seq"), None),
            P(None, ("items", "seq"), None),
            P(None, ("items", "seq"), None),
            P(),
            P(("items", "seq"), None),
            P(None, ("items", "seq"), None),
            P(None, ("items", "seq"), None),
            P(None, ("items", "seq"), None),
            P(None, ("items", "seq"), None),
            P(None, ("items", "seq"), None),
            P(),
        ),
        check_vma=False,
    )
```

time: 965 us -> 661 us (0.68)
  waiting for transfers between devices: 484 us -> 273 us
  Pallas kernels: 0 us -> 40.1 us
  local copies, waits for them, and re-layouts: 98.3 us -> 59 us
  matrix products: 126 us -> 97.9 us
  other arithmetic: 109 us -> 81.3 us
  blocking collectives: 34.5 us -> 12.2 us
  starting transfers between devices: 76.7 us -> 61.5 us
    all_gather x6 -> x4, waiting for transfers between devices: 305 us -> 86.2 us  [gather_rows(): return lax.all_gather(value, ('items', 'seq'), axis=0, tiled=True)]
    all_to_all x9 -> x10, waiting for transfers between devices: 54.5 us -> 143 us  [the longest x4 83.3 us: deal_depth(): lax.all_to_all(to_half(value), 'seq', 0, 0, axis_index_groups=same_core()...]
    ppermute x24 -> x22, waiting for transfers between devices: 118 us -> 34.9 us  [swap(): return lax.ppermute(value, axis, [(at, at ^ bit) for at in range(count)])]
    pallas_call x0 -> x4, Pallas kernels: none -> 40.1 us  [the longest x2 26.6 us: by_rows(): pl.pallas_call(kernel, grid=(rows // ROWS,), in_specs=[pl.BlockSpec((ROWS...]
    all_gather x2 -> x0, blocking collectives: 34.5 us -> none  [the longest x1 17.8 us: global_forward(): lax.all_gather(qkv_half[:, 2 * width:], 'seq', axis=0, tiled=True)]
    add x19 -> x1, other arithmetic: 32.1 us -> 0.37 us  [layer_backward(): resid_grad = after('end', resid_grad + middle_grad)]
    dot_general x26 -> x16, matrix products: 62.1 us -> 31.7 us  [the longest x8 21 us: outer(): return jnp.einsum('ri,rj->ij', *pair, preferred_element_type=jnp.float32)]
    squeeze x8 -> x4, local copies, waits for them, and re-layouts: 17.8 us -> 3.11 us  [pick(): return lax.dynamic_index_in_dim(value, index, axis, keepdims=False)]
  transfers between devices with their start and end apart: 44 -> 37, of which waited for: 24 -> 19; matrix products, arithmetic and copies ran while one was open for 26% -> 27% of each run, Pallas kernels for 0% -> 6%
where the time goes in v2:
time: 661 us; the launch traced here: 649 us
  waiting for transfers between devices  273 us (41%)
  matrix products  97.9 us (15%)
  other arithmetic  81.3 us (12%)
  starting transfers between devices  61.5 us (9%)
  local copies, waits for them, and re-layouts  59 us (9%)
  Pallas kernels  40.1 us (6%)
  between operations  24.5 us (4%)
  blocking collectives  12.2 us (2%)
    all_gather x4, waiting for transfers between devices, gather_rows(): return lax.all_gather(value, ('items', 'seq'), axis=0, tiled=True)  86.2 us
    all_to_all x4, waiting for transfers between devices, deal_depth(): lax.all_to_all(to_half(value), 'seq', 0, 0, axis_index_groups=same_core()...  83.3 us
    ppermute x22, waiting for transfers between devices, swap(): return lax.ppermute(value, axis, [(at, at ^ bit) for at in range(count)])  34.9 us
    convert_element_type x18, other arithmetic, to_half(): return value.astype(jnp.bfloat16)  29.1 us
    all_to_all x1, waiting for transfers between devices, gather_seq(): lax.all_to_all(jnp.broadcast_to(value[None], (seq // 2,) + value.shape),...  28.4 us
    pallas_call x2, Pallas kernels, by_rows(): pl.pallas_call(kernel, grid=(rows // ROWS,), in_specs=[pl.BlockSpec((ROWS...  26.6 us
    dot_general x8, matrix products, outer(): return jnp.einsum('ri,rj->ij', *pair, preferred_element_type=jnp.float32)  21 us
    ppermute x22, starting transfers between devices, swap(): return lax.ppermute(value, axis, [(at, at ^ bit) for at in range(count)])  18.5 us
  transfers between devices with their start and end apart: 37, of which 19 were waited for; matrix products, arithmetic and copies ran while one was open for 27% of the time, Pallas kernels for 6%

profile of v2, /device:TPU:0, one launch (start us, length us, event | category | flops | bytes accessed | tf_op | source)
XLA Modules:
  0.0 649.2 jit_solution(15854705835540595426)
XLA Ops:
  13.0 7.3 %all-to-all-start = ((s32[32,1,1024]{2,1,0:T(1,128)}), s32[32,1,1024]{2,1,0:T(1,128)S(1)}, u32[]{:S(2)}, u32[]{:S(2)}) async-start(s32[32,1,1024]{2,1,0:T(1,128)} %broadcast_in_dim.50), calls=%async_computation | async-start | bytes 262144 | tf_op jit(solution)/shard_map/all_to_all | solution.py:236
  20.5 8.1 %all-to-all-done = s32[32,1,1024]{2,1,0:T(1,128)S(1)} async-done(((s32[32,1,1024]{2,1,0:T(1,128)}), s32[32,1,1024]{2,1,0:T(1,128)S(1)}, u32[]{:S(2)}, u32[]{:S(2)}) %all-to-all-start) | async-done | bytes 131104 | tf_op jit(solution)/shard_map/all_to_all | solution.py:236
  34.3 7.4 %all-to-all-done.1 = bf16[32,8,192]{2,1,0:T(8,128)(2,1)S(1)} async-done(((bf16[32,8,192]{2,1,0:T(8,128)(2,1)}), bf16[32,8,192]{2,1,0:T(8,128)(2,1)S(1)}, u32[]{:S(2)}, u32[]{:S(2)}) %all-to-all-start.1) | async-done | bytes 98336 | tf_op jit(solution)/shard_map/all_to_all | solution.py:599
  54.0 14.3 %collective-permute-done.1 = bf16[2,1,4,32,768]{4,3,2,1,0:T(8,128)(2,1)} collective-permute-done((bf16[2,1,4,32,768]{4,3,2,1,0:T(8,128)(2,1)}, bf16[2,1,4,32,768]{4,3,2,1,0:T(8,128)(2,1)}, u32[]{:S(2)}, u32[]{:S(2)}) %collective-permute-start.1) | collective-permute-done | bytes 393248 | tf_op jit(solution)/shard_map/ppermute | solution.py:52
  79.8 4.7 all-to-all-start.2
  85.9 20.5 %all-to-all-done.2 = bf16[4,64,768]{2,1,0:T(8,128)(2,1)S(1)} async-done(((bf16[4,64,768]{2,1,0:T(8,128)(2,1)}), bf16[4,64,768]{2,1,0:T(8,128)(2,1)S(1)}, u32[]{:S(2)}, u32[]{:S(2)}) %all-to-all-start.2) | async-done | bytes 393248 | tf_op jit(solution)/shard_map/all_to_all | solution.py:61
  106.8 24.9 %all-gather.7.cloned.1.call-done = bf16[768,9216]{1,0:T(8,128)(2,1)} async-done(((bf16[24,9216]{1,0:T(8,128)(2,1)}), bf16[768,9216]{1,0:T(8,128)(2,1)}) %all-gather.7.cloned.1.call-update) | async-done | bytes 14155792 | tf_op jit(solution)/shard_map/all_gather | solution.py:248
  141.5 28.4 %all-to-all-done.3 = bf16[4,64,1536]{2,1,0:T(8,128)(2,1)S(1)} async-done(((bf16[4,64,1536]{2,1,0:T(8,128)(2,1)}), bf16[4,64,1536]{2,1,0:T(8,128)(2,1)S(1)}, u32[]{:S(2)}, u32[]{:S(2)}) %all-to-all-start.3) | async-done | bytes 786464 | tf_op jit(solution)/shard_map/all_to_all | solution.py:72
  176.7 6.0 shard_map.416
  198.4 61.2 %all-gather.5.cloned.1.call-done = bf16[768,9984]{1,0:T(8,128)(2,1)} async-done(((bf16[24,9984]{1,0:T(8,128)(2,1)}), bf16[768,9984]{1,0:T(8,128)(2,1)}) %all-gather.5.cloned.1.call-update) | async-done | bytes 15335440 | tf_op jit(solution)/shard_map/all_gather | solution.py:248
  266.9 5.4 convolution_convert_fusion.3.qkv_ref
  272.4 11.3 %shard_map.417 = bf16[512,768]{1,0:T(8,128)(2,1)} custom-call(bf16[512,2304]{1,0:T(8,128)(2,1)} %convolution_convert_fusion.3.qkv_ref), custom_call_target="tpu_custom_call" | custom-call | flops 402653184 | bytes 3145728 | tf_op jit(solution)/shard_map/pallas_call | solution.py:429
  297.7 6.2 fusion.6
  314.9 5.9 multiply_reduce_fusion.1
  334.7 15.3 %shard_map.418 = bf16[512,2304]{1,0:T(8,128)(2,1)} custom-call(bf16[512,2304]{1,0:T(8,128)(2,1)} %convolution_convert_fusion.3.qkv_ref, bf16[512,768]{1,0:T(8,128)(2,1)} %convolution_convert_fusion.8.grad_ref), custom_call_target="tpu_custom_call" | custom-call | flops 1207959552 | bytes 5505024 | tf_op jit(solution)/shard_map/pallas_call | solution.py:429
  350.1 7.8 %collective-permute-done.7 = bf16[2,1,4,96,768]{4,3,2,1,0:T(8,128)(2,1)} collective-permute-done((bf16[2,1,4,96,768]{4,3,2,1,0:T(8,128)(2,1)}, bf16[2,1,4,96,768]{4,3,2,1,0:T(8,128)(2,1)}, u32[]{:S(2)}, u32[]{:S(2)}) %collective-permute-start.7) | collective-permute-done | bytes 1179680 | tf_op jit(solution)/shard_map/ppermute | solution.py:52
  372.9 4.8 multiply_reduce_fusion.2
  408.5 15.4 %all-to-all-done.5 = bf16[4,200,768]{2,1,0:T(8,128)(2,1)S(1)} async-done(((bf16[4,200,768]{2,1,0:T(8,128)(2,1)}), bf16[4,200,768]{2,1,0:T(8,128)(2,1)S(1)}, u32[]{:S(2)}, u32[]{:S(2)}) %all-to-all-start.5) | async-done | bytes 1228832 | tf_op jit(solution)/shard_map/all_to_all | solution.py:61
  428.0 7.6 %shard_map.419 = (bf16[64,768]{1,0:T(8,128)(2,1)}, bf16[8,2,64,768]{3,2,1,0:T(8,128)(2,1)}) custom-call(bf16[64,2304]{1,0:T(8,128)(2,1)} %copy-done.17, bf16[512,1536]{1,0:T(8,128)(2,1)} %bitcast.312, bf16[512,1536]{1,0:T(8,128)(2,1)} %bitcast.313, f32[64,512]{1,0:T(8,128)} %fusion.102.bias_ref, bf16[64,768]{1,0:T(8,128)(2,1)} %convolution_convert_fusion.10.grad_ref), custom_call_target="tpu_custom_call" | custom-call | tf_op jit(solution)/shard_map/pallas_call | solution.py:494
  447.1 23.2 %all-to-all-done.6 = bf16[4,2,64,768]{3,2,1,0:T(8,128)(2,1)S(1)} async-done(((bf16[4,2,64,768]{3,2,1,0:T(8,128)(2,1)}), bf16[4,2,64,768]{3,2,1,0:T(8,128)(2,1)S(1)}, u32[]{:S(2)}, u32[]{:S(2)}) %all-to-all-start.6) | async-done | bytes 786464 | tf_op jit(solution)/shard_map/all_to_all | solution.py:61
  484.0 24.2 %all-to-all-done.7 = bf16[4,168,768]{2,1,0:T(8,128)(2,1)S(1)} async-done(((bf16[4,168,768]{2,1,0:T(8,128)(2,1)}), bf16[4,168,768]{2,1,0:T(8,128)(2,1)S(1)}, u32[]{:S(2)}, u32[]{:S(2)}) %all-to-all-start.7) | async-done | bytes 1032224 | tf_op jit(solution)/shard_map/all_to_all | solution.py:61
  531.0 15.6 %all-to-all-done.8 = bf16[32,64,192]{2,1,0:T(8,128)(2,1)S(1)} async-done(((bf16[32,64,192]{2,1,0:T(8,128)(2,1)}), bf16[32,64,192]{2,1,0:T(8,128)(2,1)S(1)}, u32[]{:S(2)}, u32[]{:S(2)}) %all-to-all-start.8) | async-done | bytes 786464 | tf_op jit(solution)/shard_map/all_to_all | solution.py:333
  569.4 7.7 %all-to-all-done.9 = bf16[32,24,192]{2,1,0:T(8,128)(2,1)} async-done(((bf16[32,24,192]{2,1,0:T(8,128)(2,1)}), bf16[32,24,192]{2,1,0:T(8,128)(2,1)}, u32[]{:S(2)}, u32[]{:S(2)}) %all-to-all-start.9) | async-done | bytes 294944 | tf_op jit(solution)/shard_map/all_to_all | solution.py:347
  613.9 12.2 %all_to_all.72 = f32[32,1,341]{2,1,0:T(1,128)S(1)} all-to-all(f32[32,1,341]{2,1,0:T(1,128)S(1)} %broadcast_in_dim.66), channel_id=1, replica_groups=mesh['items'=4,'seq'=8] {'items','seq'}, dimensions={0} | all-to-all | bytes 87296 | tf_op jit(solution)/shard_map/all_to_all | solution.py:236
  (509 shorter events, 279.3 us)
Async XLA Ops:
  7.2 124.5 %all-gather.7.cloned.1.call-start = ((), (), s32[]{:S(2)}) async-start(), calls=%async_computation.13 | async-start | bytes 14598144 | tf_op jit(solution)/shard_map/all_gather | solution.py:248
  11.4 248.3 %all-gather.5.cloned.1.call-start = ((), (), s32[]{:S(2)}) async-start(), calls=%async_computation.12 | async-start | bytes 15814656 | tf_op jit(solution)/shard_map/all_gather | solution.py:248
  13.0 15.6 %all-to-all-start = ((s32[32,1,1024]{2,1,0:T(1,128)}), s32[32,1,1024]{2,1,0:T(1,128)S(1)}, u32[]{:S(2)}, u32[]{:S(2)}) async-start(s32[32,1,1024]{2,1,0:T(1,128)} %broadcast_in_dim.50), calls=%async_computation | async-start | bytes 262144 | tf_op jit(solution)/shard_map/all_to_all | solution.py:236
  52.7 15.5 %collective-permute-start.1 = (bf16[2,1,4,32,768]{4,3,2,1,0:T(8,128)(2,1)}, bf16[2,1,4,32,768]{4,3,2,1,0:T(8,128)(2,1)}, u32[]{:S(2)}, u32[]{:S(2)}) collective-permute-start(bf16[2,1,4,32,768]{4,3,2,1,0:T(8,128)(2,1)} %fusion.57), channel_id=1, source_target_pairs={{0,8},{8,0},{16,24},{24,16},{1,9},{9,1},{17,25},{25,17},{2,10},{10... | collective-permute-start | bytes 1179656 | tf_op jit(solution)/shard_map/ppermute | solution.py:52
  79.8 26.7 %all-to-all-start.2 = ((bf16[4,64,768]{2,1,0:T(8,128)(2,1)}), bf16[4,64,768]{2,1,0:T(8,128)(2,1)S(1)}, u32[]{:S(2)}, u32[]{:S(2)}) async-start(bf16[4,64,768]{2,1,0:T(8,128)(2,1)} %pad_maximum_fusion.9), calls=%async_computation.2 | async-start | bytes 786432 | tf_op jit(solution)/shard_map/all_to_all | solution.py:61
  135.5 34.4 %all-to-all-start.3 = ((bf16[4,64,1536]{2,1,0:T(8,128)(2,1)}), bf16[4,64,1536]{2,1,0:T(8,128)(2,1)S(1)}, u32[]{:S(2)}, u32[]{:S(2)}) async-start(bf16[4,64,1536]{2,1,0:T(8,128)(2,1)} %broadcast_in_dim.54), calls=%async_computation.3 | async-start | bytes 1572864 | tf_op jit(solution)/shard_map/all_to_all | solution.py:72
  190.4 75.0 %all-to-all-start.4 = ((bf16[32,64,96]{2,1,0:T(8,128)(2,1)}), bf16[32,64,96]{2,1,0:T(8,128)(2,1)S(1)}, u32[]{:S(2)}, u32[]{:S(2)}) async-start(bf16[32,64,96]{2,1,0:T(8,128)(2,1)} %bitcast.305), calls=%async_computation.4 | async-start | bytes 1048576 | tf_op jit(solution)/shard_map/all_to_all | solution.py:333
  194.3 155.8 %all-gather.9.cloned.1.call-start = ((), (), s32[]{:S(2)}) async-start(), calls=%async_computation.14 | async-start | bytes 9732096 | tf_op jit(solution)/shard_map/all_gather | solution.py:248
  198.4 273.0 %all-gather.11.cloned.1.call-start = ((), (), s32[]{:S(2)}) async-start(), calls=%async_computation.15 | async-start | bytes 3244032 | tf_op jit(solution)/shard_map/all_gather | solution.py:248
  328.3 30.5 %collective-permute-start.8 = (bf16[1,2,4,104,768]{4,3,2,1,0:T(8,128)(2,1)}, bf16[1,2,4,104,768]{4,3,2,1,0:T(8,128)(2,1)}, u32[]{:S(2)}, u32[]{:S(2)}) collective-permute-start(bf16[1,2,4,104,768]{4,3,2,1,0:T(8,128)(2,1)} %add_convert_fusion), channel_id=1, source_target_pairs={{0,16},{8,24},{16,0},{24,8},{1,17},{9,25},{17,1},{25,9},{2,18},{10... | collective-permute-start | bytes 3833864 | tf_op jit(solution)/shard_map/ppermute | solution.py:52
  329.8 28.2 %collective-permute-start.7 = (bf16[2,1,4,96,768]{4,3,2,1,0:T(8,128)(2,1)}, bf16[2,1,4,96,768]{4,3,2,1,0:T(8,128)(2,1)}, u32[]{:S(2)}, u32[]{:S(2)}) collective-permute-start(bf16[2,1,4,96,768]{4,3,2,1,0:T(8,128)(2,1)} %add_convert_fusion.1), channel_id=1, source_target_pairs={{0,8},{8,0},{16,24},{24,16},{1,9},{9,1},{17,25},{25,17},{2,10},{10... | collective-permute-start | bytes 3538952 | tf_op jit(solution)/shard_map/ppermute | solution.py:52
  362.2 17.0 %collective-permute-start.10 = (bf16[1,1,4,104,768]{4,3,2,1,0:T(8,128)(2,1)S(1)}, bf16[1,1,4,104,768]{4,3,2,1,0:T(8,128)(2,1)S(1)}, u32[]{:S(2)}, u32[]{:S(2)}) collective-permute-start(bf16[1,1,4,104,768]{4,3,2,1,0:T(8,128)(2,1)S(1)} %add_convert_fusion.4), channel_id=1, source_target_pairs={{0,8},{8,0},{16,24},{24,16},{1,9},{9,1},{17,25},{25,17},{2,10},{10... | collective-permute-start | bytes 1916936 | tf_op jit(solution)/shard_map/ppermute | solution.py:52
  363.7 15.5 %collective-permute-start.9 = (bf16[1,1,4,96,768]{4,3,2,1,0:T(8,128)(2,1)S(1)}, bf16[1,1,4,96,768]{4,3,2,1,0:T(8,128)(2,1)S(1)}, u32[]{:S(2)}, u32[]{:S(2)}) collective-permute-start(bf16[1,1,4,96,768]{4,3,2,1,0:T(8,128)(2,1)S(1)} %add_convert_fusion.7), channel_id=1, source_target_pairs={{0,16},{8,24},{16,0},{24,8},{1,17},{9,25},{17,1},{25,9},{2,18},{10... | collective-permute-start | bytes 1769480 | tf_op jit(solution)/shard_map/ppermute | solution.py:52
  387.3 36.6 %all-to-all-start.5 = ((bf16[4,200,768]{2,1,0:T(8,128)(2,1)}), bf16[4,200,768]{2,1,0:T(8,128)(2,1)S(1)}, u32[]{:S(2)}, u32[]{:S(2)}) async-start(bf16[4,200,768]{2,1,0:T(8,128)(2,1)} %pad_maximum_fusion.4), calls=%async_computation.5 | async-start | bytes 2457600 | tf_op jit(solution)/shard_map/all_to_all | solution.py:61
  399.3 24.6 %collective-permute-start.13 = (bf16[1,2,4,56,768]{4,3,2,1,0:T(8,128)(2,1)S(1)}, bf16[1,2,4,56,768]{4,3,2,1,0:T(8,128)(2,1)S(1)}, u32[]{:S(2)}, u32[]{:S(2)}) collective-permute-start(bf16[1,2,4,56,768]{4,3,2,1,0:T(8,128)(2,1)S(1)} %add_convert_fusion.2), channel_id=1, source_target_pairs={{0,16},{8,24},{16,0},{24,8},{1,17},{9,25},{17,1},{25,9},{2,18},{10... | collective-permute-start | bytes 2064392 | tf_op jit(solution)/shard_map/ppermute | solution.py:52
  400.8 23.1 %collective-permute-start.12 = (bf16[2,1,4,48,768]{4,3,2,1,0:T(8,128)(2,1)}, bf16[2,1,4,48,768]{4,3,2,1,0:T(8,128)(2,1)}, u32[]{:S(2)}, u32[]{:S(2)}) collective-permute-start(bf16[2,1,4,48,768]{4,3,2,1,0:T(8,128)(2,1)} %add_convert_fusion.5), channel_id=1, source_target_pairs={{0,8},{8,0},{16,24},{24,16},{1,9},{9,1},{17,25},{25,17},{2,10},{10... | collective-permute-start | bytes 1769480 | tf_op jit(solution)/shard_map/ppermute | solution.py:52
  441.4 28.9 %all-to-all-start.6 = ((bf16[4,2,64,768]{3,2,1,0:T(8,128)(2,1)}), bf16[4,2,64,768]{3,2,1,0:T(8,128)(2,1)S(1)}, u32[]{:S(2)}, u32[]{:S(2)}) async-start(bf16[4,2,64,768]{3,2,1,0:T(8,128)(2,1)} %fusion.29), calls=%async_computation.6 | async-start | bytes 1572864 | tf_op jit(solution)/shard_map/all_to_all | solution.py:61
  445.0 26.4 %collective-permute-start.16 = (bf16[1,1,4,56,768]{4,3,2,1,0:T(8,128)(2,1)}, bf16[1,1,4,56,768]{4,3,2,1,0:T(8,128)(2,1)S(1)}, u32[]{:S(2)}, u32[]{:S(2)}) collective-permute-start(bf16[1,1,4,56,768]{4,3,2,1,0:T(8,128)(2,1)} %add_convert_fusion.9), channel_id=1, source_target_pairs={{0,8},{8,0},{16,24},{24,16},{1,9},{9,1},{17,25},{25,17},{2,10},{10... | collective-permute-start | bytes 1032200 | tf_op jit(solution)/shard_map/ppermute | solution.py:52
  446.6 24.8 %collective-permute-start.15 = (bf16[1,1,4,48,768]{4,3,2,1,0:T(8,128)(2,1)}, bf16[1,1,4,48,768]{4,3,2,1,0:T(8,128)(2,1)S(1)}, u32[]{:S(2)}, u32[]{:S(2)}) collective-permute-start(bf16[1,1,4,48,768]{4,3,2,1,0:T(8,128)(2,1)} %add_convert_fusion.11), channel_id=1, source_target_pairs={{0,16},{8,24},{16,0},{24,8},{1,17},{9,25},{17,1},{25,9},{2,18},{10... | collective-permute-start | bytes 884744 | tf_op jit(solution)/shard_map/ppermute | solution.py:52
  479.2 29.0 %all-to-all-start.7 = ((bf16[4,168,768]{2,1,0:T(8,128)(2,1)}), bf16[4,168,768]{2,1,0:T(8,128)(2,1)S(1)}, u32[]{:S(2)}, u32[]{:S(2)}) async-start(bf16[4,168,768]{2,1,0:T(8,128)(2,1)} %pad_maximum_fusion.5), calls=%async_computation.7 | async-start | bytes 2064384 | tf_op jit(solution)/shard_map/all_to_all | solution.py:61
  516.2 30.4 %all-to-all-start.8 = ((bf16[32,64,192]{2,1,0:T(8,128)(2,1)}), bf16[32,64,192]{2,1,0:T(8,128)(2,1)S(1)}, u32[]{:S(2)}, u32[]{:S(2)}) async-start(bf16[32,64,192]{2,1,0:T(8,128)(2,1)} %maximum_bitcast_fusion), calls=%async_computation.8 | async-start | bytes 2097152 | tf_op jit(solution)/shard_map/all_to_all | solution.py:333
  524.7 22.3 %collective-permute-start.19 = (bf16[2,4,64,384]{3,2,1,0:T(8,128)(2,1)S(1)}, bf16[2,4,64,384]{3,2,1,0:T(8,128)(2,1)}, u32[]{:S(2)}, u32[]{:S(2)}) collective-permute-start(bf16[2,4,64,384]{3,2,1,0:T(8,128)(2,1)S(1)} %pad_maximum_fusion.10), channel_id=1, source_target_pairs={{0,16},{8,24},{16,0},{24,8},{1,17},{9,25},{17,1},{25,9},{2,18},{10... | collective-permute-start | bytes 1179656 | tf_op jit(solution)/shard_map/ppermute | solution.py:52
  526.6 20.5 %collective-permute-start.20 = (bf16[2,4,64,384]{3,2,1,0:T(8,128)(2,1)S(1)}, bf16[2,4,64,384]{3,2,1,0:T(8,128)(2,1)}, u32[]{:S(2)}, u32[]{:S(2)}) collective-permute-start(bf16[2,4,64,384]{3,2,1,0:T(8,128)(2,1)S(1)} %pad_maximum_fusion.11), channel_id=1, source_target_pairs={{0,8},{8,0},{16,24},{24,16},{1,9},{9,1},{17,25},{25,17},{2,10},{10... | collective-permute-start | bytes 1179656 | tf_op jit(solution)/shard_map/ppermute | solution.py:52
  560.4 16.7 %all-to-all-start.9 = ((bf16[32,24,192]{2,1,0:T(8,128)(2,1)}), bf16[32,24,192]{2,1,0:T(8,128)(2,1)}, u32[]{:S(2)}, u32[]{:S(2)}) async-start(bf16[32,24,192]{2,1,0:T(8,128)(2,1)} %bitcast.101), calls=%async_computation.9 | async-start | bytes 786432 | tf_op jit(solution)/shard_map/all_to_all | solution.py:347
  (117 other events, 1619.0 us)
Sparse Core Ops, SparseCore 0:
  11.6 120.0 all-gather.6
  135.4 124.2 all-gather.4
  263.2 79.9 all-gather.8
  387.4 74.6 all-gather.10

commit v3 on v2

--- a/solution.py
+++ b/solution.py
@@ -226,6 +226,18 @@
 
 def reduce_group(partials, width):
     group = Stepped(group_steps(partials, width))
+    while group.result is None:
+        advance([], group)
+    return group.result
+
+
+def to_depth(value):
+    half_seq = lax.axis_size("seq") // 2
+    return deal_depth(jnp.broadcast_to(value[None], (half_seq,) + value.shape))
+
+
+def gather_swaps(mine):
+    group = Stepped(gather_steps(mine))
     while group.result is None:
         advance([], group)
     return group.result
@@ -326,13 +338,16 @@
     return jnp.einsum("ri,rj->ij", *pair, preferred_element_type=jnp.float32)
 
 
-def deal_columns(parts):
+def column_blocks(parts):
     count = lax.axis_size("items") * lax.axis_size("seq")
     rows = parts[0].shape[0]
     blocks = jnp.concatenate([part.reshape(rows, count, -1) for part in parts], axis=2)
-    dealt = lax.all_to_all(
-        blocks.transpose(1, 0, 2), ("items", "seq"), 0, 0, tiled=True
-    ).reshape(count * rows, -1)
+    return blocks.transpose(1, 0, 2)
+
+
+def deal_columns(blocks, parts):
+    count, rows = blocks.shape[:2]
+    dealt = lax.all_to_all(blocks, ("items", "seq"), 0, 0, tiled=True).reshape(count * rows, -1)
     out, at = [], 0
     for part in parts:
         size = part.shape[1] // count
@@ -344,9 +359,12 @@
 def deal_rows(parts):
     count = lax.axis_size("items") * lax.axis_size("seq")
     blocks = jnp.concatenate([to_half(part) for part in parts], axis=1)
-    dealt = lax.all_to_all(
+    return lax.all_to_all(
         blocks.reshape(count, -1, blocks.shape[1]), ("items", "seq"), 0, 0, tiled=True
     )
+
+
+def whole_rows(dealt, parts):
     out, at = [], 0
     for part in parts:
         size = part.shape[1]
@@ -550,8 +568,23 @@
     depth = attn_qkv.shape[1]
     count = lax.axis_size("items") * lax.axis_size("seq")
     rank = lax.axis_index("items") * lax.axis_size("seq") + lax.axis_index("seq")
-    told = share(jnp.concatenate([byte_tokens.reshape(-1), groups.reshape(-1)]))
-    told = told.reshape(count, 2, -1)
+    mine = patch_proj.shape[0]
+    splits = width // mine
+    slot, column = rank // splits, rank % splits
+    narrow = tables[0].astype(half).reshape(-1, splits, mine).transpose(1, 0, 2)
+    narrow = jnp.tile(narrow.reshape(splits, -1), (count // splits, 1))
+    own = jnp.concatenate([byte_tokens.reshape(-1), groups.reshape(-1)]).astype(half)
+    patch_mine = to_depth(jnp.concatenate([attn_qkv[0], attn_out[0]], axis=1).astype(half))
+    patch_mine, own = lax.optimization_barrier((patch_mine, own))
+    dealt = lax.all_to_all(
+        jnp.concatenate([narrow, jnp.broadcast_to(own[None], (count,) + own.shape)], axis=1),
+        ("items", "seq"),
+        0,
+        0,
+        tiled=True,
+    )
+    told = dealt[:, narrow.shape[1] :].astype(jnp.int32).reshape(count, 2, -1)
+    narrow = dealt[:, : narrow.shape[1]].reshape(-1, mine)
     counts = jnp.sum(one_hot(told[:, 1], GROUPS, single), axis=0)
 
     def flat(value):
@@ -572,33 +605,30 @@
             flat(mlp_out[n]),
         ]
 
-    ends = [3 * width, 4 * width, 4 * width + mlp_in.shape[2]]
-    ends.append(ends[2] + mlp_out.shape[1] // depth * width)
-
-    def layer_weights(joined):
-        return (
-            joined[:, : ends[0]],
-            joined[:, ends[0] : ends[1]],
-            joined[:, ends[1] : ends[2]],
-            tall(joined[:, ends[2] : ends[3]]).reshape(-1, width),
-        )
-
-    patch_all = gather_rows(jnp.concatenate(layer_parts(0), axis=1))
-    byte_all = gather_rows(
-        jnp.concatenate(layer_parts(1) + [flat(tables.reshape(-1, width))], axis=1)
-    )
-    weights = [layer_weights(patch_all), layer_weights(byte_all)]
+    sizes = [3 * width, width, mlp_in.shape[2], mlp_out.shape[1] // depth * width]
+
+    def cut(joined, begin, lengths):
+        pieces = []
+        for length in lengths:
+            pieces.append(joined[:, begin : begin + length])
+            begin += length
+        return pieces
+
+    patch_parts, byte_parts = layer_parts(0), layer_parts(1)
+    patch_all = gather_swaps(patch_mine)
+    rest_all = gather_rows(
+        jnp.concatenate(
+            patch_parts[2:] + byte_parts + [flat(tables.reshape(-1, width))], axis=1
+        )
+    )
+    rest = cut(rest_all, 0, sizes[2:] + sizes + [tables.shape[0] * tables.shape[1] // depth * width])
+    weights = [cut(patch_all, 0, sizes[:2]) + rest[:2], rest[2:6]]
+    for part in weights:
+        part[3] = tall(part[3]).reshape(-1, width)
     qkv_w, out_w, in_w, down_w = ([weights[n][at] for n in range(2)] for at in range(4))
-    table_rows = byte_all[:, ends[3] :].reshape(count, tables.shape[0], -1, width)
+    table_rows = rest[6].reshape(count, tables.shape[0], -1, width)
     table_w = [table_rows[:, n].reshape(-1, width) for n in range(3)]
 
-    mine = patch_proj.shape[0]
-    splits = width // mine
-    slot, column = rank // splits, rank % splits
-    narrow = tables[0].astype(half).reshape(-1, splits, mine).transpose(1, 0, 2)
-    narrow = lax.all_to_all(
-        jnp.tile(narrow, (count // splits, 1, 1)), ("items", "seq"), 0, 0, tiled=True
-    ).reshape(-1, mine)
     all_grid = told[:, 0].reshape(byte_tokens.shape[0] * lax.axis_size("items"), -1, PATCH)
     ahead = jnp.concatenate([jnp.zeros_like(all_grid[:, :1]), all_grid[:, :-1]], axis=1)
     slot_hot = one_hot(pick(ahead, slot, 2), VOCAB, half)
@@ -666,10 +696,11 @@
         top, saved_top = layer_forward(
             resid, vectors[0:2], qkv_w[0], out_w[0], in_w[0], down_w[0], global_forward
         )
+        top, active_blocks = lax.optimization_barrier((top, column_blocks(saved_top[11:])))
+        (active_columns,) = deal_columns(active_blocks, saved_top[11:])
         patch_sides = gather_rows(
             jnp.concatenate([saved_top[2], saved_top[5], saved_top[9]], axis=1)
         )
-        top, active_columns = lax.optimization_barrier((top, deal_columns([saved_top[11]])[0]))
         before = jnp.concatenate([jnp.zeros((span_rows, 1), jnp.int32), byte_grid[:, :-1]], axis=1)
         before_hot = one_hot(before, VOCAB, half)
         local_embed = jnp.dot(before_hot, table_w[1], preferred_element_type=single).reshape(
@@ -709,6 +740,8 @@
             if where == "mlp":
                 grads = [to_half(outer(pair)) for pair in others]
                 running["early"] = Stepped(group_steps(grads + [to_half(head_grad)], width))
+            elif where == "attention":
+                value, sides["active"] = lax.optimization_barrier((value, active_columns))
             elif where == "projections":
                 attn_half, mixed_half, proj_half = others
                 value, sides["all"] = lax.optimization_barrier((value, patch_sides))
@@ -773,20 +806,21 @@
             projected_half[None], (lax.axis_size("seq") // 2,) + projected_half.shape
         )
         joint = deal_depth(jnp.concatenate([own, running["low"].held[0]], axis=1))
-        joint, *patch = lax.optimization_barrier((joint, *sides["patch"]))
+        joint, patch, patch_down = lax.optimization_barrier(
+            (joint, column_blocks(sides["patch"]), outer((sides["active"], sides["top"])))
+        )
         running["low"].feed([joint[:, span_rows:]])
         running["gather"] = Stepped(gather_steps(joint[:, :span_rows]))
         advance([], running["gather"])
-        columns = deal_columns(patch)
-        patch_down = outer((active_columns, sides["top"]))
-        (patch_down,) = advance([patch_down], running["gather"])
-        columns = advance(columns, running["gather"])
+        columns = deal_columns(patch, sides["patch"])
+        advance([], running["gather"])
+        advance([], running["gather"])
         attn_all, mixed_all, mlp_all = (
             sides["all"][:, at * width : (at + 1) * width] for at in range(3)
         )
         blocks = [outer(pair) for pair in zip((attn_all, mixed_all, mlp_all), columns)]
-        blocks = advance([to_half(part) for part in blocks], running["gather"])
-        patch_qkv, patch_out, patch_in = deal_rows(blocks)
+        dealt_rows = deal_rows(blocks)
+        advance([], running["gather"])
         projected_all = running["gather"].result
         proj_grad = jnp.einsum(
             "ri,rd->id", embed_part, projected_all, preferred_element_type=single
@@ -795,9 +829,8 @@
             "rd,id->ri", projected_all, proj_half, preferred_element_type=single
         )
         slot_grad = hot_sum(slot_hot, embed_grad)
-        slot_grad, patch_qkv, patch_out, patch_in = lax.optimization_barrier(
-            (slot_grad, patch_qkv, patch_out, patch_in)
-        )
+        slot_grad, dealt_rows = lax.optimization_barrier((slot_grad, dealt_rows))
+        patch_qkv, patch_out, patch_in = whole_rows(dealt_rows, blocks)
         slot_size, vector_rows = slot_grad.size // count, spread(vector_grad.reshape(-1))
         dealt = lax.all_to_all(
             jnp.concatenate([slot_grad.reshape(count, slot_size), vector_rows], axis=1),
@@ -820,11 +853,13 @@
             jnp.stack([patch_in, early[0]]),
             jnp.stack([patch_down, early[1]]),
         )
-        return (loss_terms, owned, vector_piece)
-
-    loss_terms, owned, vector_piece = item_pass(byte_tokens[0], groups[0], doc_ids[0])
-    shard_square = sum((jnp.sum(piece * piece) for piece in owned))
-    shard_square = shard_square + jnp.sum(vector_piece * vector_piece)
+        pieces = [proj_grad, global_table_grad, *low, *early, patch_down, vector_piece]
+        shard_square = sum(jnp.sum(piece * piece) for piece in pieces + [wide(dealt_rows)])
+        return (loss_terms, owned, vector_piece, shard_square)
+
+    loss_terms, owned, vector_piece, shard_square = item_pass(
+        byte_tokens[0], groups[0], doc_ids[0]
+    )
     tail = share(jnp.concatenate([vector_piece, shard_square[None], loss_terms]))
     size = vector_piece.shape[0]
     vector_total = tail[:, :size].reshape(-1)[: vectors.size].reshape(vectors.shape)

time: 661 us -> 633 us (0.958)
  waiting for transfers between devices: 273 us -> 235 us
  blocking collectives: 12.2 us -> 0 us
  other arithmetic: 81.3 us -> 91.9 us
  starting transfers between devices: 61.5 us -> 70.5 us
    all_gather x4 -> x3, waiting for transfers between devices: 86.2 us -> 3.25 us  [gather_rows(): return lax.all_gather(value, ('items', 'seq'), axis=0, tiled=True)]
    all_to_all x4 -> x5, waiting for transfers between devices: 83.3 us -> 97.1 us  [deal_depth(): lax.all_to_all(to_half(value), 'seq', 0, 0, axis_index_groups=same_core()...]
    ppermute x22 -> x27, waiting for transfers between devices: 34.9 us -> 47.3 us  [swap(): return lax.ppermute(value, axis, [(at, at ^ bit) for at in range(count)])]
    all_to_all x1 -> x0, blocking collectives: 12.2 us -> none  [share(): lax.all_to_all(jnp.broadcast_to(row[None], (count,) + row.shape), ('items...]
    all_to_all x1, waiting for transfers between devices: 28.4 us -> 39 us  [gather_seq(): lax.all_to_all(jnp.broadcast_to(value[None], (seq // 2,) + value.shape),...]
    unnamed x233 -> x252, local copies, waits for them, and re-layouts: 15.4 us -> 25.5 us
    convert_element_type x6, local copies, waits for them, and re-layouts: 8.14 us -> 0.92 us  [wide(): return value.astype(jnp.float32)]
    all_to_all x4 -> x5, starting transfers between devices: 16 us -> 21.7 us  [deal_depth(): lax.all_to_all(to_half(value), 'seq', 0, 0, axis_index_groups=same_core()...]
  transfers between devices with their start and end apart: 37 -> 42, of which waited for: 19 -> 27; matrix products, arithmetic and copies ran while one was open for 27% -> 32% of each run, Pallas kernels for 6% -> 6%
where the time goes in v3:
time: 633 us; the launch traced here: 624 us
  waiting for transfers between devices  235 us (37%)
  matrix products  96.8 us (15%)
  other arithmetic  91.9 us (15%)
  starting transfers between devices  70.5 us (11%)
  local copies, waits for them, and re-layouts  63.2 us (10%)
  Pallas kernels  40.1 us (6%)
  between operations  26.9 us (4%)
    all_to_all x5, waiting for transfers between devices, deal_depth(): lax.all_to_all(to_half(value), 'seq', 0, 0, axis_index_groups=same_core()...  97.1 us
    ppermute x27, waiting for transfers between devices, swap(): return lax.ppermute(value, axis, [(at, at ^ bit) for at in range(count)])  47.3 us
    all_to_all x1, waiting for transfers between devices, gather_seq(): lax.all_to_all(jnp.broadcast_to(value[None], (seq // 2,) + value.shape),...  39 us
    convert_element_type x18, other arithmetic, to_half(): return value.astype(jnp.bfloat16)  32.3 us
    pallas_call x2, Pallas kernels, by_rows(): pl.pallas_call(kernel, grid=(rows // ROWS,), in_specs=[pl.BlockSpec((ROWS...  26.4 us
    unnamed x252, local copies, waits for them, and re-layouts  25.5 us
    all_to_all x2, waiting for transfers between devices, deal_columns(): lax.all_to_all(blocks, ('items', 'seq'), 0, 0, tiled=True)  25.1 us
    ppermute x27, starting transfers between devices, swap(): return lax.ppermute(value, axis, [(at, at ^ bit) for at in range(count)])  24 us
  transfers between devices with their start and end apart: 42, of which 27 were waited for; matrix products, arithmetic and copies ran while one was open for 32% of the time, Pallas kernels for 6%

profile of v3, /device:TPU:0, one launch (start us, length us, event | category | flops | bytes accessed | tf_op | source)
XLA Modules:
  0.0 624.2 jit_solution(12133428079270543785)
XLA Ops:
  13.5 6.3 %all-to-all-start = ((bf16[4,24,3072]{2,1,0:T(8,128)(2,1)}), bf16[4,24,3072]{2,1,0:T(8,128)(2,1)S(1)}, u32[]{:S(2)}, u32[]{:S(2)}) async-start(bf16[4,24,3072]{2,1,0:T(8,128)(2,1)} %broadcast_in_dim.52), calls=%async_computation | async-start | bytes 1179648 | tf_op jit(solution)/shard_map/all_to_all | solution.py:61
  20.2 26.8 %all-to-all-done = bf16[4,24,3072]{2,1,0:T(8,128)(2,1)S(1)} async-done(((bf16[4,24,3072]{2,1,0:T(8,128)(2,1)}), bf16[4,24,3072]{2,1,0:T(8,128)(2,1)S(1)}, u32[]{:S(2)}, u32[]{:S(2)}) %all-to-all-start) | async-done | bytes 589856 | tf_op jit(solution)/shard_map/all_to_all | solution.py:61
  72.7 11.5 %collective-permute-done.7 = bf16[2,4,24,1536]{3,2,1,0:T(8,128)(2,1)} collective-permute-done((bf16[2,4,24,1536]{3,2,1,0:T(8,128)(2,1)}, bf16[2,4,24,1536]{3,2,1,0:T(8,128)(2,1)}, u32[]{:S(2)}, u32[]{:S(2)}) %collective-permute-start.7) | collective-permute-done | bytes 589856 | tf_op jit(solution)/shard_map/ppermute | solution.py:52
  96.7 6.9 %collective-permute-done.1 = bf16[2,1,4,32,768]{4,3,2,1,0:T(8,128)(2,1)} collective-permute-done((bf16[2,1,4,32,768]{4,3,2,1,0:T(8,128)(2,1)}, bf16[2,1,4,32,768]{4,3,2,1,0:T(8,128)(2,1)}, u32[]{:S(2)}, u32[]{:S(2)}) %collective-permute-start.1) | collective-permute-done | bytes 393248 | tf_op jit(solution)/shard_map/ppermute | solution.py:52
  120.8 19.3 %all-to-all-done.2 = bf16[4,64,768]{2,1,0:T(8,128)(2,1)S(1)} async-done(((bf16[4,64,768]{2,1,0:T(8,128)(2,1)}), bf16[4,64,768]{2,1,0:T(8,128)(2,1)S(1)}, u32[]{:S(2)}, u32[]{:S(2)}) %all-to-all-start.2) | async-done | bytes 393248 | tf_op jit(solution)/shard_map/all_to_all | solution.py:61
  147.6 5.6 all-to-all-start.3
  156.0 39.0 %all-to-all-done.3 = bf16[4,64,1536]{2,1,0:T(8,128)(2,1)S(1)} async-done(((bf16[4,64,1536]{2,1,0:T(8,128)(2,1)}), bf16[4,64,1536]{2,1,0:T(8,128)(2,1)S(1)}, u32[]{:S(2)}, u32[]{:S(2)}) %all-to-all-start.3) | async-done | bytes 786464 | tf_op jit(solution)/shard_map/all_to_all | solution.py:72
  198.9 6.1 shard_map.416
  211.8 6.5 %fusion.123 = (bf16[768,768]{1,0:T(8,128)(2,1)}, bf16[768,768]{1,0:T(8,128)(2,1)}, bf16[768,768]{1,0:T(8,128)(2,1)}, bf16[768,768]{1,0:T(8,128)(2,1)}, bf16[768,...) fusion(bf16[768,16128]{1,0:T(8,128)(2,1)} %all-gather.4.cloned., ...), kind=kLoop, calls=%fused_computation.380 | loop fusion | bytes 21233664 | tf_op jit(solution)/shard_map/slice | solution.py:596
  219.0 6.1 multiply_convert_fusion.6
  229.9 5.4 convolution_convert_fusion.3.qkv_ref
  235.3 11.2 %shard_map.417 = bf16[512,768]{1,0:T(8,128)(2,1)} custom-call(bf16[512,2304]{1,0:T(8,128)(2,1)} %convolution_convert_fusion.3.qkv_ref), custom_call_target="tpu_custom_call" | custom-call | flops 402653184 | bytes 3145728 | tf_op jit(solution)/shard_map/pallas_call | solution.py:447
  262.0 6.2 fusion.6
  291.0 7.0 %multiply_reduce_fusion.1 = (f32[768]{0:T(1024)}, f32[512]{0:T(512)S(1)}, f32[512,768]{1,0:T(8,128)S(1)}) fusion(f32[512,768]{1,0:T(8,128)S(1)} %get-tuple-element.311, f32[512]{0:T(512)} %copy-done.87, f32[768]{0:T(1024)} %get-tuple-element.194, bf16[512,3072]{1,0:T(8,128)(2,1)} %copy-done.107, bf16[768,16128]{1,0:T(8,128)(2,1)} %all-gather.4.cloned.1.call-done), kind=kOutput, calls=%fused_computation.65 | convolution fusion | flops 2418277120 | bytes 11021312 | tf_op jit(solution)/shard_map/rf,df->rd/dot_general | solution.py:323
  315.4 15.1 %shard_map.418 = bf16[512,2304]{1,0:T(8,128)(2,1)} custom-call(bf16[512,2304]{1,0:T(8,128)(2,1)} %convolution_convert_fusion.3.qkv_ref, bf16[512,768]{1,0:T(8,128)(2,1)} %convolution_convert_fusion.8.grad_ref), custom_call_target="tpu_custom_call" | custom-call | flops 1207959552 | bytes 5505024 | tf_op jit(solution)/shard_map/pallas_call | solution.py:447
  330.6 11.3 %collective-permute-done.12 = bf16[2,1,4,96,768]{4,3,2,1,0:T(8,128)(2,1)} collective-permute-done((bf16[2,1,4,96,768]{4,3,2,1,0:T(8,128)(2,1)}, bf16[2,1,4,96,768]{4,3,2,1,0:T(8,128)(2,1)}, u32[]{:S(2)}, u32[]{:S(2)}) %collective-permute-start.12) | collective-permute-done | bytes 1179680 | tf_op jit(solution)/shard_map/ppermute | solution.py:52
  393.1 15.5 %all-to-all-done.5 = bf16[4,200,768]{2,1,0:T(8,128)(2,1)S(1)} async-done(((bf16[4,200,768]{2,1,0:T(8,128)(2,1)}), bf16[4,200,768]{2,1,0:T(8,128)(2,1)S(1)}, u32[]{:S(2)}, u32[]{:S(2)}) %all-to-all-start.5) | async-done | bytes 1228832 | tf_op jit(solution)/shard_map/all_to_all | solution.py:61
  412.8 7.6 %shard_map.419 = (bf16[64,768]{1,0:T(8,128)(2,1)}, bf16[8,2,64,768]{3,2,1,0:T(8,128)(2,1)}) custom-call(bf16[64,2304]{1,0:T(8,128)(2,1)} %copy-done.20, bf16[512,1536]{1,0:T(8,128)(2,1)} %bitcast.334, bf16[512,1536]{1,0:T(8,128)(2,1)} %bitcast.335, f32[64,512]{1,0:T(8,128)} %fusion.106.bias_ref, bf16[64,768]{1,0:T(8,128)(2,1)} %convolution_convert_fusion.10.grad_ref), custom_call_target="tpu_custom_call" | custom-call | tf_op jit(solution)/shard_map/pallas_call | solution.py:512
  432.0 23.2 %all-to-all-done.6 = bf16[4,2,64,768]{3,2,1,0:T(8,128)(2,1)S(1)} async-done(((bf16[4,2,64,768]{3,2,1,0:T(8,128)(2,1)}), bf16[4,2,64,768]{3,2,1,0:T(8,128)(2,1)S(1)}, u32[]{:S(2)}, u32[]{:S(2)}) %all-to-all-start.6) | async-done | bytes 786464 | tf_op jit(solution)/shard_map/all_to_all | solution.py:61
  480.4 12.3 %all-to-all-done.7 = bf16[4,168,768]{2,1,0:T(8,128)(2,1)S(1)} async-done(((bf16[4,168,768]{2,1,0:T(8,128)(2,1)}), bf16[4,168,768]{2,1,0:T(8,128)(2,1)S(1)}, u32[]{:S(2)}, u32[]{:S(2)}) %all-to-all-start.7) | async-done | bytes 1032224 | tf_op jit(solution)/shard_map/all_to_all | solution.py:61
  513.7 21.7 %all-to-all-done.8 = bf16[32,64,192]{2,1,0:T(8,128)(2,1)} async-done(((bf16[32,64,192]{2,1,0:T(8,128)(2,1)}), bf16[32,64,192]{2,1,0:T(8,128)(2,1)}, u32[]{:S(2)}, u32[]{:S(2)}) %all-to-all-start.8) | async-done | bytes 786464 | tf_op jit(solution)/shard_map/all_to_all | solution.py:350
  553.2 7.7 %all-to-all-done.9 = bf16[32,24,192]{2,1,0:T(8,128)(2,1)S(1)} async-done(((bf16[32,24,192]{2,1,0:T(8,128)(2,1)}), bf16[32,24,192]{2,1,0:T(8,128)(2,1)S(1)}, u32[]{:S(2)}, u32[]{:S(2)}) %all-to-all-start.9) | async-done | bytes 294944 | tf_op jit(solution)/shard_map/all_to_all | solution.py:362
  575.5 5.5 all-to-all-done.10
  595.2 6.1 all-to-all-done.11
  (550 shorter events, 307.3 us)
Async XLA Ops:
  7.2 204.6 %all-gather.4.cloned.1.call-start = ((), (), s32[]{:S(2)}) async-start(), calls=%async_computation.12 | async-start | bytes 25546752 | tf_op jit(solution)/shard_map/all_gather | solution.py:260
  13.5 33.5 %all-to-all-start = ((bf16[4,24,3072]{2,1,0:T(8,128)(2,1)}), bf16[4,24,3072]{2,1,0:T(8,128)(2,1)S(1)}, u32[]{:S(2)}, u32[]{:S(2)}) async-start(bf16[4,24,3072]{2,1,0:T(8,128)(2,1)} %broadcast_in_dim.52), calls=%async_computation | async-start | bytes 1179648 | tf_op jit(solution)/shard_map/all_to_all | solution.py:61
  57.1 27.1 %collective-permute-start.7 = (bf16[2,4,24,1536]{3,2,1,0:T(8,128)(2,1)}, bf16[2,4,24,1536]{3,2,1,0:T(8,128)(2,1)}, u32[]{:S(2)}, u32[]{:S(2)}) collective-permute-start(bf16[2,4,24,1536]{3,2,1,0:T(8,128)(2,1)} %pad_maximum_fusion.7), channel_id=1, source_target_pairs={{0,16},{8,24},{16,0},{24,8},{1,17},{9,25},{17,1},{25,9},{2,18},{10... | collective-permute-start | bytes 1769480 | tf_op jit(solution)/shard_map/ppermute | solution.py:52
  58.7 28.9 %collective-permute-start.8 = (bf16[2,4,24,1536]{3,2,1,0:T(8,128)(2,1)}, bf16[2,4,24,1536]{3,2,1,0:T(8,128)(2,1)}, u32[]{:S(2)}, u32[]{:S(2)}) collective-permute-start(bf16[2,4,24,1536]{3,2,1,0:T(8,128)(2,1)} %pad_maximum_fusion.8), channel_id=1, source_target_pairs={{0,8},{8,0},{16,24},{24,16},{1,9},{9,1},{17,25},{25,17},{2,10},{10... | collective-permute-start | bytes 1769480 | tf_op jit(solution)/shard_map/ppermute | solution.py:52
  70.7 19.6 %collective-permute-start = (bf16[2,2,4,64,768]{4,3,2,1,0:T(8,128)(2,1)}, bf16[2,2,4,64,768]{4,3,2,1,0:T(8,128)(2,1)}, u32[]{:S(2)}, u32[]{:S(2)}) collective-permute-start(bf16[2,2,4,64,768]{4,3,2,1,0:T(8,128)(2,1)} %dynamic-slice_bitcast_fusion.4), channel_id=1, source_target_pairs={{0,1},{1,0},{2,3},{3,2},{4,5},{5,4},{6,7},{7,6},{8,9},{9,8},{10,11... | collective-permute-start | bytes 4718600 | tf_op jit(solution)/shard_map/ppermute | solution.py:52
  96.7 43.8 %collective-permute-start.9 = (bf16[2,2,4,24,3072]{4,3,2,1,0:T(8,128)(2,1)}, bf16[2,2,4,24,3072]{4,3,2,1,0:T(8,128)(2,1)}, u32[]{:S(2)}, u32[]{:S(2)}) collective-permute-start(bf16[2,2,4,24,3072]{4,3,2,1,0:T(8,128)(2,1)} %maximum_maximum_fusion), channel_id=1, source_target_pairs={{0,1},{1,0},{2,3},{3,2},{4,5},{5,4},{6,7},{7,6},{8,9},{9,8},{10,11... | collective-permute-start | bytes 7077896 | tf_op jit(solution)/shard_map/ppermute | solution.py:52
  114.4 25.8 %all-to-all-start.2 = ((bf16[4,64,768]{2,1,0:T(8,128)(2,1)}), bf16[4,64,768]{2,1,0:T(8,128)(2,1)S(1)}, u32[]{:S(2)}, u32[]{:S(2)}) async-start(bf16[4,64,768]{2,1,0:T(8,128)(2,1)} %pad_maximum_fusion.9), calls=%async_computation.2 | async-start | bytes 786432 | tf_op jit(solution)/shard_map/all_to_all | solution.py:61
  147.6 47.4 %all-to-all-start.3 = ((bf16[4,64,1536]{2,1,0:T(8,128)(2,1)}), bf16[4,64,1536]{2,1,0:T(8,128)(2,1)S(1)}, u32[]{:S(2)}, u32[]{:S(2)}) async-start(bf16[4,64,1536]{2,1,0:T(8,128)(2,1)} %broadcast_in_dim.58), calls=%async_computation.3 | async-start | bytes 1572864 | tf_op jit(solution)/shard_map/all_to_all | solution.py:72
  153.2 177.4 %all-gather.6.cloned.1.call-start = ((), (), s32[]{:S(2)}) async-start(), calls=%async_computation.13 | async-start | bytes 9732096 | tf_op jit(solution)/shard_map/all_gather | solution.py:260
  286.6 20.2 %collective-permute-start.11 = (bf16[2,2,4,200,768]{4,3,2,1,0:T(8,128)(2,1)}, bf16[2,2,4,200,768]{4,3,2,1,0:T(8,128)(2,1)}, u32[]{:S(2)}, u32[]{:S(2)}) collective-permute-start(bf16[2,2,4,200,768]{4,3,2,1,0:T(8,128)(2,1)} %get-tuple-element.123), channel_id=1, source_target_pairs={{0,1},{1,0},{2,3},{3,2},{4,5},{5,4},{6,7},{7,6},{8,9},{9,8},{10,11... | collective-permute-start | bytes 14745608 | tf_op jit(solution)/shard_map/ppermute | solution.py:52
  286.8 20.0 %all-to-all-start.4 = ((bf16[32,64,96]{2,1,0:T(8,128)(2,1)}), bf16[32,64,96]{2,1,0:T(8,128)(2,1)}, u32[]{:S(2)}, u32[]{:S(2)}) async-start(bf16[32,64,96]{2,1,0:T(8,128)(2,1)} %bitcast.364), calls=%async_computation.4 | async-start | bytes 1048576 | tf_op jit(solution)/shard_map/all_to_all | solution.py:350
  290.5 164.9 %all-gather.8.cloned.1.call-start = ((), (), s32[]{:S(2)}) async-start(), calls=%async_computation.14 | async-start | bytes 3244032 | tf_op jit(solution)/shard_map/all_gather | solution.py:260
  312.8 30.2 %collective-permute-start.13 = (bf16[1,2,4,104,768]{4,3,2,1,0:T(8,128)(2,1)}, bf16[1,2,4,104,768]{4,3,2,1,0:T(8,128)(2,1)S(1)}, u32[]{:S(2)}, u32[]{:S(2)}) collective-permute-start(bf16[1,2,4,104,768]{4,3,2,1,0:T(8,128)(2,1)} %add_convert_fusion), channel_id=1, source_target_pairs={{0,16},{8,24},{16,0},{24,8},{1,17},{9,25},{17,1},{25,9},{2,18},{10... | collective-permute-start | bytes 3833864 | tf_op jit(solution)/shard_map/ppermute | solution.py:52
  314.1 27.8 %collective-permute-start.12 = (bf16[2,1,4,96,768]{4,3,2,1,0:T(8,128)(2,1)}, bf16[2,1,4,96,768]{4,3,2,1,0:T(8,128)(2,1)}, u32[]{:S(2)}, u32[]{:S(2)}) collective-permute-start(bf16[2,1,4,96,768]{4,3,2,1,0:T(8,128)(2,1)} %add_convert_fusion.1), channel_id=1, source_target_pairs={{0,8},{8,0},{16,24},{24,16},{1,9},{9,1},{17,25},{25,17},{2,10},{10... | collective-permute-start | bytes 3538952 | tf_op jit(solution)/shard_map/ppermute | solution.py:52
  346.6 17.7 %collective-permute-start.15 = (bf16[1,1,4,104,768]{4,3,2,1,0:T(8,128)(2,1)S(1)}, bf16[1,1,4,104,768]{4,3,2,1,0:T(8,128)(2,1)S(1)}, u32[]{:S(2)}, u32[]{:S(2)}) collective-permute-start(bf16[1,1,4,104,768]{4,3,2,1,0:T(8,128)(2,1)S(1)} %add_convert_fusion.4), channel_id=1, source_target_pairs={{0,8},{8,0},{16,24},{24,16},{1,9},{9,1},{17,25},{25,17},{2,10},{10... | collective-permute-start | bytes 1916936 | tf_op jit(solution)/shard_map/ppermute | solution.py:52
  372.3 36.3 %all-to-all-start.5 = ((bf16[4,200,768]{2,1,0:T(8,128)(2,1)}), bf16[4,200,768]{2,1,0:T(8,128)(2,1)S(1)}, u32[]{:S(2)}, u32[]{:S(2)}) async-start(bf16[4,200,768]{2,1,0:T(8,128)(2,1)} %pad_maximum_fusion.5), calls=%async_computation.5 | async-start | bytes 2457600 | tf_op jit(solution)/shard_map/all_to_all | solution.py:61
  383.9 24.8 %collective-permute-start.18 = (bf16[1,2,4,56,768]{4,3,2,1,0:T(8,128)(2,1)S(1)}, bf16[1,2,4,56,768]{4,3,2,1,0:T(8,128)(2,1)S(1)}, u32[]{:S(2)}, u32[]{:S(2)}) collective-permute-start(bf16[1,2,4,56,768]{4,3,2,1,0:T(8,128)(2,1)S(1)} %add_convert_fusion.2), channel_id=1, source_target_pairs={{0,16},{8,24},{16,0},{24,8},{1,17},{9,25},{17,1},{25,9},{2,18},{10... | collective-permute-start | bytes 2064392 | tf_op jit(solution)/shard_map/ppermute | solution.py:52
  385.3 23.3 %collective-permute-start.17 = (bf16[2,1,4,48,768]{4,3,2,1,0:T(8,128)(2,1)}, bf16[2,1,4,48,768]{4,3,2,1,0:T(8,128)(2,1)}, u32[]{:S(2)}, u32[]{:S(2)}) collective-permute-start(bf16[2,1,4,48,768]{4,3,2,1,0:T(8,128)(2,1)} %add_convert_fusion.5), channel_id=1, source_target_pairs={{0,8},{8,0},{16,24},{24,16},{1,9},{9,1},{17,25},{25,17},{2,10},{10... | collective-permute-start | bytes 1769480 | tf_op jit(solution)/shard_map/ppermute | solution.py:52
  426.1 29.0 %all-to-all-start.6 = ((bf16[4,2,64,768]{3,2,1,0:T(8,128)(2,1)}), bf16[4,2,64,768]{3,2,1,0:T(8,128)(2,1)S(1)}, u32[]{:S(2)}, u32[]{:S(2)}) async-start(bf16[4,2,64,768]{3,2,1,0:T(8,128)(2,1)} %fusion.29), calls=%async_computation.6 | async-start | bytes 1572864 | tf_op jit(solution)/shard_map/all_to_all | solution.py:61
  429.8 25.6 %collective-permute-start.21 = (bf16[1,1,4,56,768]{4,3,2,1,0:T(8,128)(2,1)}, bf16[1,1,4,56,768]{4,3,2,1,0:T(8,128)(2,1)S(1)}, u32[]{:S(2)}, u32[]{:S(2)}) collective-permute-start(bf16[1,1,4,56,768]{4,3,2,1,0:T(8,128)(2,1)} %add_convert_fusion.9), channel_id=1, source_target_pairs={{0,8},{8,0},{16,24},{24,16},{1,9},{9,1},{17,25},{25,17},{2,10},{10... | collective-permute-start | bytes 1032200 | tf_op jit(solution)/shard_map/ppermute | solution.py:52
  431.1 24.3 %collective-permute-start.20 = (bf16[1,1,4,48,768]{4,3,2,1,0:T(8,128)(2,1)}, bf16[1,1,4,48,768]{4,3,2,1,0:T(8,128)(2,1)}, u32[]{:S(2)}, u32[]{:S(2)}) collective-permute-start(bf16[1,1,4,48,768]{4,3,2,1,0:T(8,128)(2,1)} %add_convert_fusion.11), channel_id=1, source_target_pairs={{0,16},{8,24},{16,0},{24,8},{1,17},{9,25},{17,1},{25,9},{2,18},{10... | collective-permute-start | bytes 884744 | tf_op jit(solution)/shard_map/ppermute | solution.py:52
  463.4 29.3 %all-to-all-start.7 = ((bf16[4,168,768]{2,1,0:T(8,128)(2,1)}), bf16[4,168,768]{2,1,0:T(8,128)(2,1)S(1)}, u32[]{:S(2)}, u32[]{:S(2)}) async-start(bf16[4,168,768]{2,1,0:T(8,128)(2,1)} %pad_maximum_fusion.6), calls=%async_computation.7 | async-start | bytes 2064384 | tf_op jit(solution)/shard_map/all_to_all | solution.py:61
  504.4 31.0 %all-to-all-start.8 = ((bf16[32,64,192]{2,1,0:T(8,128)(2,1)}), bf16[32,64,192]{2,1,0:T(8,128)(2,1)}, u32[]{:S(2)}, u32[]{:S(2)}) async-start(bf16[32,64,192]{2,1,0:T(8,128)(2,1)} %maximum_bitcast_fusion), calls=%async_computation.8 | async-start | bytes 2097152 | tf_op jit(solution)/shard_map/all_to_all | solution.py:350
  510.4 37.0 %collective-permute-start.26 = (bf16[2,2,4,64,768]{4,3,2,1,0:T(8,128)(2,1)S(1)}, bf16[2,2,4,64,768]{4,3,2,1,0:T(8,128)(2,1)}, u32[]{:S(2)}, u32[]{:S(2)}) collective-permute-start(bf16[2,2,4,64,768]{4,3,2,1,0:T(8,128)(2,1)S(1)} %maximum_maximum_fusion.1), channel_id=1, source_target_pairs={{0,1},{1,0},{2,3},{3,2},{4,5},{5,4},{6,7},{7,6},{8,9},{9,8},{10,11... | collective-permute-start | bytes 4718600 | tf_op jit(solution)/shard_map/ppermute | solution.py:52
  (126 other events, 1182.7 us)
Sparse Core Ops, SparseCore 0:
  12.7 199.0 all-gather.3
  215.4 81.9 all-gather.5
  372.4 74.3 all-gather.7

commit v4 on v3

--- a/solution.py
+++ b/solution.py
@@ -254,6 +254,11 @@
     count = lax.axis_size("items") * lax.axis_size("seq")
     size = -(-value.shape[0] // count)
     return jnp.pad(value, (0, size * count - value.shape[0])).reshape(count, size)
+
+
+def square_row(piece, width):
+    sums = jnp.sum(piece * piece, axis=0, keepdims=True)
+    return sum(sums[:, at : at + width] for at in range(0, piece.shape[1], width))
 
 
 def gather_rows(value):
@@ -829,22 +834,28 @@
             "rd,id->ri", projected_all, proj_half, preferred_element_type=single
         )
         slot_grad = hot_sum(slot_hot, embed_grad)
-        slot_grad, dealt_rows = lax.optimization_barrier((slot_grad, dealt_rows))
-        patch_qkv, patch_out, patch_in = whole_rows(dealt_rows, blocks)
         slot_size, vector_rows = slot_grad.size // count, spread(vector_grad.reshape(-1))
-        dealt = lax.all_to_all(
-            jnp.concatenate([slot_grad.reshape(count, slot_size), vector_rows], axis=1),
-            ("items", "seq"),
-            0,
-            0,
-            tiled=True,
-        )
-        vector_piece = jnp.sum(dealt[:, slot_size:], axis=0)
+        own = [
+            slot_grad.reshape(count, slot_size),
+            vector_rows,
+            jnp.broadcast_to(loss_terms[None], (count, GROUPS)),
+        ]
+        own, dealt_rows = lax.optimization_barrier((jnp.concatenate(own, axis=1), dealt_rows))
+        dealt = lax.all_to_all(own, ("items", "seq"), 0, 0, tiled=True)
+        vector_piece = jnp.sum(dealt[:, slot_size:-GROUPS], axis=0)
+        loss_total = jnp.sum(dealt[:, -GROUPS:], axis=0)
         slot_rows = dealt[:, :slot_size].reshape(count, -1, mine)
         slot_rows = jnp.sum(slot_rows.reshape(PATCH, splits, -1, mine), axis=0)
         global_table_grad = slot_rows.transpose(1, 0, 2).reshape(-1, width)
         assert all(group.result is not None for group in running.values())
         early, low = running["early"].result, running["low"].result
+        pieces = [*low, *early, patch_down, proj_grad, global_table_grad]
+        squares = sum(square_row(piece, width) for piece in pieces)
+        dealt_squares = jnp.sum(wide(dealt_rows) * wide(dealt_rows), axis=(0, 1))
+        row = jnp.concatenate([vector_piece, squares[0], dealt_squares])
+        row, dealt_rows = lax.optimization_barrier((row, dealt_rows))
+        tail = share(row)
+        patch_qkv, patch_out, patch_in = whole_rows(dealt_rows, blocks)
         owned = (
             proj_grad,
             jnp.stack([global_table_grad, low[2], early[2]]),
@@ -853,19 +864,12 @@
             jnp.stack([patch_in, early[0]]),
             jnp.stack([patch_down, early[1]]),
         )
-        pieces = [proj_grad, global_table_grad, *low, *early, patch_down, vector_piece]
-        shard_square = sum(jnp.sum(piece * piece) for piece in pieces + [wide(dealt_rows)])
-        return (loss_terms, owned, vector_piece, shard_square)
-
-    loss_terms, owned, vector_piece, shard_square = item_pass(
-        byte_tokens[0], groups[0], doc_ids[0]
-    )
-    tail = share(jnp.concatenate([vector_piece, shard_square[None], loss_terms]))
-    size = vector_piece.shape[0]
+        return (loss_total, owned, tail, vector_piece.shape[0])
+
+    loss_total, owned, tail, size = item_pass(byte_tokens[0], groups[0], doc_ids[0])
     vector_total = tail[:, :size].reshape(-1)[: vectors.size].reshape(vectors.shape)
-    loss_total = jnp.sum(tail[:, size + 1 :], axis=0)
     loss = jnp.sum(loss_total / counts) / GROUPS
-    grad_norm = jnp.sqrt(jnp.sum(tail[:, size]))
+    grad_norm = jnp.sqrt(jnp.sum(tail[:, :size] * tail[:, :size]) + jnp.sum(tail[:, size:]))
     factor = jnp.minimum(1.0, CLIP_AT / grad_norm)
     step = float(STEP_NUMBER)
     rates = (

time: 633 us -> 626 us (0.989)
  local copies, waits for them, and re-layouts: 63.2 us -> 69.7 us
  between operations: 26.9 us -> 20.4 us
  transfers between devices with their start and end apart: 42 -> 42, of which waited for: 27 -> 27; matrix products, arithmetic and copies ran while one was open for 32% -> 33% of each run, Pallas kernels for 6% -> 7%
where the time goes in v4:
time: 626 us; the launch traced here: 616 us
  waiting for transfers between devices  229 us (37%)
  matrix products  96.9 us (15%)
  other arithmetic  88.5 us (14%)
  starting transfers between devices  71.9 us (11%)
  local copies, waits for them, and re-layouts  69.7 us (11%)
  Pallas kernels  40.1 us (6%)
  between operations  20.4 us (3%)
    all_to_all x5, waiting for transfers between devices, deal_depth(): lax.all_to_all(to_half(value), 'seq', 0, 0, axis_index_groups=same_core()...  97 us
    ppermute x27, waiting for transfers between devices, swap(): return lax.ppermute(value, axis, [(at, at ^ bit) for at in range(count)])  47.4 us
    all_to_all x1, waiting for transfers between devices, gather_seq(): lax.all_to_all(jnp.broadcast_to(value[None], (seq // 2,) + value.shape),...  39 us
    convert_element_type x18, other arithmetic, to_half(): return value.astype(jnp.bfloat16)  32.3 us
    unnamed x252, local copies, waits for them, and re-layouts  27 us
    pallas_call x2, Pallas kernels, by_rows(): pl.pallas_call(kernel, grid=(rows // ROWS,), in_specs=[pl.BlockSpec((ROWS...  26.4 us
    all_to_all x2, waiting for transfers between devices, deal_columns(): lax.all_to_all(blocks, ('items', 'seq'), 0, 0, tiled=True)  24.9 us
    ppermute x27, starting transfers between devices, swap(): return lax.ppermute(value, axis, [(at, at ^ bit) for at in range(count)])  24.1 us
  transfers between devices with their start and end apart: 42, of which 27 were waited for; matrix products, arithmetic and copies ran while one was open for 33% of the time, Pallas kernels for 7%

profile of v4, /device:TPU:0, one launch (start us, length us, event | category | flops | bytes accessed | tf_op | source)
XLA Modules:
  0.0 616.4 jit_solution(7187960751395701410)
XLA Ops:
  13.5 6.3 %all-to-all-start = ((bf16[4,24,3072]{2,1,0:T(8,128)(2,1)}), bf16[4,24,3072]{2,1,0:T(8,128)(2,1)S(1)}, u32[]{:S(2)}, u32[]{:S(2)}) async-start(bf16[4,24,3072]{2,1,0:T(8,128)(2,1)} %broadcast_in_dim.78), calls=%async_computation | async-start | bytes 1179648 | tf_op jit(solution)/shard_map/all_to_all | solution.py:61
  20.1 26.8 %all-to-all-done = bf16[4,24,3072]{2,1,0:T(8,128)(2,1)S(1)} async-done(((bf16[4,24,3072]{2,1,0:T(8,128)(2,1)}), bf16[4,24,3072]{2,1,0:T(8,128)(2,1)S(1)}, u32[]{:S(2)}, u32[]{:S(2)}) %all-to-all-start) | async-done | bytes 589856 | tf_op jit(solution)/shard_map/all_to_all | solution.py:61
  72.7 11.5 %collective-permute-done.7 = bf16[2,4,24,1536]{3,2,1,0:T(8,128)(2,1)} collective-permute-done((bf16[2,4,24,1536]{3,2,1,0:T(8,128)(2,1)}, bf16[2,4,24,1536]{3,2,1,0:T(8,128)(2,1)}, u32[]{:S(2)}, u32[]{:S(2)}) %collective-permute-start.7) | collective-permute-done | bytes 589856 | tf_op jit(solution)/shard_map/ppermute | solution.py:52
  96.7 6.9 %collective-permute-done.1 = bf16[2,1,4,32,768]{4,3,2,1,0:T(8,128)(2,1)} collective-permute-done((bf16[2,1,4,32,768]{4,3,2,1,0:T(8,128)(2,1)}, bf16[2,1,4,32,768]{4,3,2,1,0:T(8,128)(2,1)}, u32[]{:S(2)}, u32[]{:S(2)}) %collective-permute-start.1) | collective-permute-done | bytes 393248 | tf_op jit(solution)/shard_map/ppermute | solution.py:52
  120.8 19.3 %all-to-all-done.2 = bf16[4,64,768]{2,1,0:T(8,128)(2,1)S(1)} async-done(((bf16[4,64,768]{2,1,0:T(8,128)(2,1)}), bf16[4,64,768]{2,1,0:T(8,128)(2,1)S(1)}, u32[]{:S(2)}, u32[]{:S(2)}) %all-to-all-start.2) | async-done | bytes 393248 | tf_op jit(solution)/shard_map/all_to_all | solution.py:61
  147.6 5.6 all-to-all-start.3
  156.0 39.0 %all-to-all-done.3 = bf16[4,64,1536]{2,1,0:T(8,128)(2,1)S(1)} async-done(((bf16[4,64,1536]{2,1,0:T(8,128)(2,1)}), bf16[4,64,1536]{2,1,0:T(8,128)(2,1)S(1)}, u32[]{:S(2)}, u32[]{:S(2)}) %all-to-all-start.3) | async-done | bytes 786464 | tf_op jit(solution)/shard_map/all_to_all | solution.py:72
  198.8 6.1 shard_map.416
  211.8 6.5 %fusion.127 = (bf16[768,768]{1,0:T(8,128)(2,1)}, bf16[768,768]{1,0:T(8,128)(2,1)}, bf16[768,768]{1,0:T(8,128)(2,1)}, bf16[768,768]{1,0:T(8,128)(2,1)}, bf16[768,...) fusion(bf16[768,16128]{1,0:T(8,128)(2,1)} %all-gather.4.cloned., ...), kind=kLoop, calls=%fused_computation.388 | loop fusion | bytes 21233664 | tf_op jit(solution)/shard_map/slice | solution.py:601
  219.0 6.1 multiply_convert_fusion.6
  229.9 5.4 convolution_convert_fusion.3.qkv_ref
  235.4 11.3 %shard_map.417 = bf16[512,768]{1,0:T(8,128)(2,1)} custom-call(bf16[512,2304]{1,0:T(8,128)(2,1)} %convolution_convert_fusion.3.qkv_ref), custom_call_target="tpu_custom_call" | custom-call | flops 402653184 | bytes 3145728 | tf_op jit(solution)/shard_map/pallas_call | solution.py:452
  250.3 4.8 fusion.9
  262.1 6.2 %fusion.6 = bf16[512,3072]{1,0:T(8,128)(2,1)S(1)} fusion(f32[512,3072]{1,0:T(8,128)S(1)} %fusion.9, bf16[3072,768]{1,0:T(8,128)(2,1)S(1)} %bitcast.349, f32[512,768]{1,0:T(8,128)S(1)} %subtract_multiply_fusion), kind=kOutput, calls=%fused_computation.8 | convolution fusion | flops 2447769600 | bytes 15728640 | tf_op jit(solution)/shard_map/rd,fd->rf/dot_general | solution.py:324
  291.1 7.0 %multiply_reduce_fusion.1 = (f32[768]{0:T(1024)}, f32[512]{0:T(512)S(1)}, f32[512,768]{1,0:T(8,128)S(1)}) fusion(f32[512,768]{1,0:T(8,128)S(1)} %get-tuple-element.315, f32[512]{0:T(512)} %copy-done.88, f32[768]{0:T(1024)} %get-tuple-element.198, bf16[512,3072]{1,0:T(8,128)(2,1)} %copy-done.107, bf16[768,16128]{1,0:T(8,128)(2,1)} %all-gather.4.cloned.1.call-done), kind=kOutput, calls=%fused_computation.65 | convolution fusion | flops 2418277120 | bytes 11021312 | tf_op jit(solution)/shard_map/rf,df->rd/dot_general | solution.py:328
  315.6 15.1 %shard_map.418 = bf16[512,2304]{1,0:T(8,128)(2,1)} custom-call(bf16[512,2304]{1,0:T(8,128)(2,1)} %convolution_convert_fusion.3.qkv_ref, bf16[512,768]{1,0:T(8,128)(2,1)} %convolution_convert_fusion.8.grad_ref), custom_call_target="tpu_custom_call" | custom-call | flops 1207959552 | bytes 5505024 | tf_op jit(solution)/shard_map/pallas_call | solution.py:452
  330.8 11.3 %collective-permute-done.12 = bf16[2,1,4,96,768]{4,3,2,1,0:T(8,128)(2,1)} collective-permute-done((bf16[2,1,4,96,768]{4,3,2,1,0:T(8,128)(2,1)}, bf16[2,1,4,96,768]{4,3,2,1,0:T(8,128)(2,1)}, u32[]{:S(2)}, u32[]{:S(2)}) %collective-permute-start.12) | collective-permute-done | bytes 1179680 | tf_op jit(solution)/shard_map/ppermute | solution.py:52
  393.3 15.5 %all-to-all-done.5 = bf16[4,200,768]{2,1,0:T(8,128)(2,1)S(1)} async-done(((bf16[4,200,768]{2,1,0:T(8,128)(2,1)}), bf16[4,200,768]{2,1,0:T(8,128)(2,1)S(1)}, u32[]{:S(2)}, u32[]{:S(2)}) %all-to-all-start.5) | async-done | bytes 1228832 | tf_op jit(solution)/shard_map/all_to_all | solution.py:61
  412.9 7.6 %shard_map.419 = (bf16[64,768]{1,0:T(8,128)(2,1)}, bf16[8,2,64,768]{3,2,1,0:T(8,128)(2,1)}) custom-call(bf16[64,2304]{1,0:T(8,128)(2,1)} %copy-done.20, bf16[512,1536]{1,0:T(8,128)(2,1)} %bitcast.333, bf16[512,1536]{1,0:T(8,128)(2,1)} %bitcast.334, f32[64,512]{1,0:T(8,128)} %fusion.106.bias_ref, bf16[64,768]{1,0:T(8,128)(2,1)} %convolution_convert_fusion.10.grad_ref), custom_call_target="tpu_custom_call" | custom-call | tf_op jit(solution)/shard_map/pallas_call | solution.py:517
  432.2 23.1 %all-to-all-done.6 = bf16[4,2,64,768]{3,2,1,0:T(8,128)(2,1)S(1)} async-done(((bf16[4,2,64,768]{3,2,1,0:T(8,128)(2,1)}), bf16[4,2,64,768]{3,2,1,0:T(8,128)(2,1)S(1)}, u32[]{:S(2)}, u32[]{:S(2)}) %all-to-all-start.6) | async-done | bytes 786464 | tf_op jit(solution)/shard_map/all_to_all | solution.py:61
  480.6 12.2 %all-to-all-done.7 = bf16[4,168,768]{2,1,0:T(8,128)(2,1)S(1)} async-done(((bf16[4,168,768]{2,1,0:T(8,128)(2,1)}), bf16[4,168,768]{2,1,0:T(8,128)(2,1)S(1)}, u32[]{:S(2)}, u32[]{:S(2)}) %all-to-all-start.7) | async-done | bytes 1032224 | tf_op jit(solution)/shard_map/all_to_all | solution.py:61
  513.9 21.7 %all-to-all-done.8 = bf16[32,64,192]{2,1,0:T(8,128)(2,1)} async-done(((bf16[32,64,192]{2,1,0:T(8,128)(2,1)}), bf16[32,64,192]{2,1,0:T(8,128)(2,1)}, u32[]{:S(2)}, u32[]{:S(2)}) %all-to-all-start.8) | async-done | bytes 786464 | tf_op jit(solution)/shard_map/all_to_all | solution.py:355
  571.1 5.6 all-to-all-done.10
  586.4 6.2 %all-to-all-done.11 = f32[32,1,1296]{2,1,0:T(1,128)} async-done(((f32[32,1,1296]{2,1,0:T(1,128)}), f32[32,1,1296]{2,1,0:T(1,128)}, u32[]{:S(2)}, u32[]{:S(2)}) %all-to-all-start.11) | async-done | bytes 165920 | tf_op jit(solution)/shard_map/all_to_all | solution.py:248
  (554 shorter events, 308.7 us)
Async XLA Ops:
  7.2 204.6 %all-gather.4.cloned.1.call-start = ((), (), s32[]{:S(2)}) async-start(), calls=%async_computation.12 | async-start | bytes 25546752 | tf_op jit(solution)/shard_map/all_gather | solution.py:265
  13.5 33.5 %all-to-all-start = ((bf16[4,24,3072]{2,1,0:T(8,128)(2,1)}), bf16[4,24,3072]{2,1,0:T(8,128)(2,1)S(1)}, u32[]{:S(2)}, u32[]{:S(2)}) async-start(bf16[4,24,3072]{2,1,0:T(8,128)(2,1)} %broadcast_in_dim.78), calls=%async_computation | async-start | bytes 1179648 | tf_op jit(solution)/shard_map/all_to_all | solution.py:61
  57.1 27.1 %collective-permute-start.7 = (bf16[2,4,24,1536]{3,2,1,0:T(8,128)(2,1)}, bf16[2,4,24,1536]{3,2,1,0:T(8,128)(2,1)}, u32[]{:S(2)}, u32[]{:S(2)}) collective-permute-start(bf16[2,4,24,1536]{3,2,1,0:T(8,128)(2,1)} %pad_maximum_fusion.7), channel_id=1, source_target_pairs={{0,16},{8,24},{16,0},{24,8},{1,17},{9,25},{17,1},{25,9},{2,18},{10... | collective-permute-start | bytes 1769480 | tf_op jit(solution)/shard_map/ppermute | solution.py:52
  58.7 28.9 %collective-permute-start.8 = (bf16[2,4,24,1536]{3,2,1,0:T(8,128)(2,1)}, bf16[2,4,24,1536]{3,2,1,0:T(8,128)(2,1)}, u32[]{:S(2)}, u32[]{:S(2)}) collective-permute-start(bf16[2,4,24,1536]{3,2,1,0:T(8,128)(2,1)} %pad_maximum_fusion.8), channel_id=1, source_target_pairs={{0,8},{8,0},{16,24},{24,16},{1,9},{9,1},{17,25},{25,17},{2,10},{10... | collective-permute-start | bytes 1769480 | tf_op jit(solution)/shard_map/ppermute | solution.py:52
  70.7 19.6 %collective-permute-start = (bf16[2,2,4,64,768]{4,3,2,1,0:T(8,128)(2,1)}, bf16[2,2,4,64,768]{4,3,2,1,0:T(8,128)(2,1)}, u32[]{:S(2)}, u32[]{:S(2)}) collective-permute-start(bf16[2,2,4,64,768]{4,3,2,1,0:T(8,128)(2,1)} %dynamic-slice_bitcast_fusion.4), channel_id=1, source_target_pairs={{0,1},{1,0},{2,3},{3,2},{4,5},{5,4},{6,7},{7,6},{8,9},{9,8},{10,11... | collective-permute-start | bytes 4718600 | tf_op jit(solution)/shard_map/ppermute | solution.py:52
  96.7 43.8 %collective-permute-start.9 = (bf16[2,2,4,24,3072]{4,3,2,1,0:T(8,128)(2,1)}, bf16[2,2,4,24,3072]{4,3,2,1,0:T(8,128)(2,1)}, u32[]{:S(2)}, u32[]{:S(2)}) collective-permute-start(bf16[2,2,4,24,3072]{4,3,2,1,0:T(8,128)(2,1)} %maximum_maximum_fusion), channel_id=1, source_target_pairs={{0,1},{1,0},{2,3},{3,2},{4,5},{5,4},{6,7},{7,6},{8,9},{9,8},{10,11... | collective-permute-start | bytes 7077896 | tf_op jit(solution)/shard_map/ppermute | solution.py:52
  114.4 25.8 %all-to-all-start.2 = ((bf16[4,64,768]{2,1,0:T(8,128)(2,1)}), bf16[4,64,768]{2,1,0:T(8,128)(2,1)S(1)}, u32[]{:S(2)}, u32[]{:S(2)}) async-start(bf16[4,64,768]{2,1,0:T(8,128)(2,1)} %pad_maximum_fusion.9), calls=%async_computation.2 | async-start | bytes 786432 | tf_op jit(solution)/shard_map/all_to_all | solution.py:61
  147.6 47.4 %all-to-all-start.3 = ((bf16[4,64,1536]{2,1,0:T(8,128)(2,1)}), bf16[4,64,1536]{2,1,0:T(8,128)(2,1)S(1)}, u32[]{:S(2)}, u32[]{:S(2)}) async-start(bf16[4,64,1536]{2,1,0:T(8,128)(2,1)} %broadcast_in_dim.84), calls=%async_computation.3 | async-start | bytes 1572864 | tf_op jit(solution)/shard_map/all_to_all | solution.py:72
  153.2 177.6 %all-gather.6.cloned.1.call-start = ((), (), s32[]{:S(2)}) async-start(), calls=%async_computation.13 | async-start | bytes 9732096 | tf_op jit(solution)/shard_map/all_gather | solution.py:265
  286.7 20.1 %collective-permute-start.11 = (bf16[2,2,4,200,768]{4,3,2,1,0:T(8,128)(2,1)}, bf16[2,2,4,200,768]{4,3,2,1,0:T(8,128)(2,1)}, u32[]{:S(2)}, u32[]{:S(2)}) collective-permute-start(bf16[2,2,4,200,768]{4,3,2,1,0:T(8,128)(2,1)} %get-tuple-element.125), channel_id=1, source_target_pairs={{0,1},{1,0},{2,3},{3,2},{4,5},{5,4},{6,7},{7,6},{8,9},{9,8},{10,11... | collective-permute-start | bytes 14745608 | tf_op jit(solution)/shard_map/ppermute | solution.py:52
  287.0 19.9 %all-to-all-start.4 = ((bf16[32,64,96]{2,1,0:T(8,128)(2,1)}), bf16[32,64,96]{2,1,0:T(8,128)(2,1)}, u32[]{:S(2)}, u32[]{:S(2)}) async-start(bf16[32,64,96]{2,1,0:T(8,128)(2,1)} %bitcast.363), calls=%async_computation.4 | async-start | bytes 1048576 | tf_op jit(solution)/shard_map/all_to_all | solution.py:355
  290.6 164.9 %all-gather.8.cloned.1.call-start = ((), (), s32[]{:S(2)}) async-start(), calls=%async_computation.14 | async-start | bytes 3244032 | tf_op jit(solution)/shard_map/all_gather | solution.py:265
  313.0 30.2 %collective-permute-start.13 = (bf16[1,2,4,104,768]{4,3,2,1,0:T(8,128)(2,1)}, bf16[1,2,4,104,768]{4,3,2,1,0:T(8,128)(2,1)S(1)}, u32[]{:S(2)}, u32[]{:S(2)}) collective-permute-start(bf16[1,2,4,104,768]{4,3,2,1,0:T(8,128)(2,1)} %add_convert_fusion), channel_id=1, source_target_pairs={{0,16},{8,24},{16,0},{24,8},{1,17},{9,25},{17,1},{25,9},{2,18},{10... | collective-permute-start | bytes 3833864 | tf_op jit(solution)/shard_map/ppermute | solution.py:52
  314.2 27.8 %collective-permute-start.12 = (bf16[2,1,4,96,768]{4,3,2,1,0:T(8,128)(2,1)}, bf16[2,1,4,96,768]{4,3,2,1,0:T(8,128)(2,1)}, u32[]{:S(2)}, u32[]{:S(2)}) collective-permute-start(bf16[2,1,4,96,768]{4,3,2,1,0:T(8,128)(2,1)} %add_convert_fusion.1), channel_id=1, source_target_pairs={{0,8},{8,0},{16,24},{24,16},{1,9},{9,1},{17,25},{25,17},{2,10},{10... | collective-permute-start | bytes 3538952 | tf_op jit(solution)/shard_map/ppermute | solution.py:52
  346.8 17.6 %collective-permute-start.15 = (bf16[1,1,4,104,768]{4,3,2,1,0:T(8,128)(2,1)S(1)}, bf16[1,1,4,104,768]{4,3,2,1,0:T(8,128)(2,1)S(1)}, u32[]{:S(2)}, u32[]{:S(2)}) collective-permute-start(bf16[1,1,4,104,768]{4,3,2,1,0:T(8,128)(2,1)S(1)} %add_convert_fusion.4), channel_id=1, source_target_pairs={{0,8},{8,0},{16,24},{24,16},{1,9},{9,1},{17,25},{25,17},{2,10},{10... | collective-permute-start | bytes 1916936 | tf_op jit(solution)/shard_map/ppermute | solution.py:52
  372.4 36.3 %all-to-all-start.5 = ((bf16[4,200,768]{2,1,0:T(8,128)(2,1)}), bf16[4,200,768]{2,1,0:T(8,128)(2,1)S(1)}, u32[]{:S(2)}, u32[]{:S(2)}) async-start(bf16[4,200,768]{2,1,0:T(8,128)(2,1)} %pad_maximum_fusion.5), calls=%async_computation.5 | async-start | bytes 2457600 | tf_op jit(solution)/shard_map/all_to_all | solution.py:61
  384.0 24.8 %collective-permute-start.18 = (bf16[1,2,4,56,768]{4,3,2,1,0:T(8,128)(2,1)S(1)}, bf16[1,2,4,56,768]{4,3,2,1,0:T(8,128)(2,1)S(1)}, u32[]{:S(2)}, u32[]{:S(2)}) collective-permute-start(bf16[1,2,4,56,768]{4,3,2,1,0:T(8,128)(2,1)S(1)} %add_convert_fusion.2), channel_id=1, source_target_pairs={{0,16},{8,24},{16,0},{24,8},{1,17},{9,25},{17,1},{25,9},{2,18},{10... | collective-permute-start | bytes 2064392 | tf_op jit(solution)/shard_map/ppermute | solution.py:52
  385.4 23.3 %collective-permute-start.17 = (bf16[2,1,4,48,768]{4,3,2,1,0:T(8,128)(2,1)}, bf16[2,1,4,48,768]{4,3,2,1,0:T(8,128)(2,1)}, u32[]{:S(2)}, u32[]{:S(2)}) collective-permute-start(bf16[2,1,4,48,768]{4,3,2,1,0:T(8,128)(2,1)} %add_convert_fusion.5), channel_id=1, source_target_pairs={{0,8},{8,0},{16,24},{24,16},{1,9},{9,1},{17,25},{25,17},{2,10},{10... | collective-permute-start | bytes 1769480 | tf_op jit(solution)/shard_map/ppermute | solution.py:52
  426.3 29.0 %all-to-all-start.6 = ((bf16[4,2,64,768]{3,2,1,0:T(8,128)(2,1)}), bf16[4,2,64,768]{3,2,1,0:T(8,128)(2,1)S(1)}, u32[]{:S(2)}, u32[]{:S(2)}) async-start(bf16[4,2,64,768]{3,2,1,0:T(8,128)(2,1)} %fusion.29), calls=%async_computation.6 | async-start | bytes 1572864 | tf_op jit(solution)/shard_map/all_to_all | solution.py:61
  429.9 25.6 %collective-permute-start.21 = (bf16[1,1,4,56,768]{4,3,2,1,0:T(8,128)(2,1)}, bf16[1,1,4,56,768]{4,3,2,1,0:T(8,128)(2,1)S(1)}, u32[]{:S(2)}, u32[]{:S(2)}) collective-permute-start(bf16[1,1,4,56,768]{4,3,2,1,0:T(8,128)(2,1)} %add_convert_fusion.9), channel_id=1, source_target_pairs={{0,8},{8,0},{16,24},{24,16},{1,9},{9,1},{17,25},{25,17},{2,10},{10... | collective-permute-start | bytes 1032200 | tf_op jit(solution)/shard_map/ppermute | solution.py:52
  431.3 24.3 %collective-permute-start.20 = (bf16[1,1,4,48,768]{4,3,2,1,0:T(8,128)(2,1)}, bf16[1,1,4,48,768]{4,3,2,1,0:T(8,128)(2,1)}, u32[]{:S(2)}, u32[]{:S(2)}) collective-permute-start(bf16[1,1,4,48,768]{4,3,2,1,0:T(8,128)(2,1)} %add_convert_fusion.11), channel_id=1, source_target_pairs={{0,16},{8,24},{16,0},{24,8},{1,17},{9,25},{17,1},{25,9},{2,18},{10... | collective-permute-start | bytes 884744 | tf_op jit(solution)/shard_map/ppermute | solution.py:52
  463.5 29.3 %all-to-all-start.7 = ((bf16[4,168,768]{2,1,0:T(8,128)(2,1)}), bf16[4,168,768]{2,1,0:T(8,128)(2,1)S(1)}, u32[]{:S(2)}, u32[]{:S(2)}) async-start(bf16[4,168,768]{2,1,0:T(8,128)(2,1)} %pad_maximum_fusion.6), calls=%async_computation.7 | async-start | bytes 2064384 | tf_op jit(solution)/shard_map/all_to_all | solution.py:61
  504.5 31.0 %all-to-all-start.8 = ((bf16[32,64,192]{2,1,0:T(8,128)(2,1)}), bf16[32,64,192]{2,1,0:T(8,128)(2,1)}, u32[]{:S(2)}, u32[]{:S(2)}) async-start(bf16[32,64,192]{2,1,0:T(8,128)(2,1)} %maximum_bitcast_fusion), calls=%async_computation.8 | async-start | bytes 2097152 | tf_op jit(solution)/shard_map/all_to_all | solution.py:355
  510.6 37.0 %collective-permute-start.26 = (bf16[2,2,4,64,768]{4,3,2,1,0:T(8,128)(2,1)S(1)}, bf16[2,2,4,64,768]{4,3,2,1,0:T(8,128)(2,1)}, u32[]{:S(2)}, u32[]{:S(2)}) collective-permute-start(bf16[2,2,4,64,768]{4,3,2,1,0:T(8,128)(2,1)S(1)} %maximum_maximum_fusion.1), channel_id=1, source_target_pairs={{0,1},{1,0},{2,3},{3,2},{4,5},{5,4},{6,7},{7,6},{8,9},{9,8},{10,11... | collective-permute-start | bytes 4718600 | tf_op jit(solution)/shard_map/ppermute | solution.py:52
  (126 other events, 1147.5 us)
Sparse Core Ops, SparseCore 0:
  12.7 199.0 all-gather.3
  215.4 82.0 all-gather.5
  372.6 74.4 all-gather.7
